TPU v7x, 32 devices: a whole 2x2x4 slice. The times are simulated.
32 devices in a mesh: fsdp: 16 (over z, y, x), dp: 2 (over core).
Axes of the slice: x: 2, y: 2, z: 4, core: 2. Of those that a mesh axis runs over, the one named last changes fastest.
Arguments:
- normed: bfloat16 [2, 4096, 4096], P(None, ('fsdp', 'dp')), may hold values from -6 to 6
- kv_cotangent: bfloat16 [2, 4096, 512], P(None, ('fsdp', 'dp')), may hold values from -6 to 6
- kv_weight: bfloat16 [4096, 512], P('fsdp'), may hold values from -0.09375 to 0.09375
- main_grad: float32 [4096, 512], P('fsdp'), may hold values from -6 to 6
- owner_order: int32 [16], replicated, may hold values from 0 to 15, each once
Outputs:
- key_rows: bfloat16 [2, 4096, 512], P(None, ('fsdp', 'dp'))
- input_grad: bfloat16 [2, 4096, 4096], P(None, ('fsdp', 'dp'))
- grad_buffer: float32 [4096, 512], P('fsdp')
Inputs may be any that keep to these rules, and one draw needn't show every extreme that they name: `owner_order`: a permutation: each value appears once.
All inputs are finite; a program needn't handle non-finite values.
Results may differ from a plain program's by a relative error of at most 0.0075.
Values may be sent and summed in bfloat16 or wider, within the bound.
No kernel may reach another device: no remote copies, remote signals or barrier semaphores. Data moves between devices by JAX's collectives and lax.ppermute only.
A program may use at most 64 MiB of HBM per device.

v0:
```python
import functools
import math

import jax
import jax.numpy as jnp
from jax import lax
from jax.experimental import pallas as pl
from jax.experimental.pallas import tpu as pltpu
from jax.sharding import PartitionSpec as P


LANES = 128


def plain_body(normed, kv_cotangent, kv_weight, main_grad, owner_order):
    micro_count, tok_dev, width = normed.shape
    shard_rows, key_width = kv_weight.shape
    owners = lax.axis_size("fsdp")
    everyone = owners * lax.axis_size("dp")
    all_rows = micro_count * tok_dev
    permuted = jnp.take(normed.reshape(all_rows, owners, shard_rows), owner_order, axis=1).reshape(
        all_rows, width
    )
    flat_cot = kv_cotangent.reshape(all_rows, key_width)
    gathered = lax.all_gather(kv_weight, "fsdp", axis=0, tiled=True)
    key_sum = jnp.dot(permuted, gathered, preferred_element_type=jnp.float32)
    grad_permuted = lax.dot_general(
        flat_cot, gathered, (((1,), (1,)), ((), ())), preferred_element_type=jnp.float32
    ).astype(jnp.bfloat16)
    inverse_owner = jnp.argsort(owner_order)
    input_grad = jnp.take(
        grad_permuted.reshape(all_rows, owners, shard_rows), inverse_owner, axis=1
    ).reshape(micro_count, tok_dev, width)
    partial = lax.dot_general(
        permuted, flat_cot, (((0,), (0,)), ((), ())), preferred_element_type=jnp.float32
    )
    shard_sum = lax.psum_scatter(partial, "fsdp", scatter_dimension=0, tiled=True)
    replica_total = lax.psum(shard_sum, "dp")
    grad_scale = 1.0 / math.sqrt(micro_count * tok_dev * everyone)
    grad_buffer = main_grad + replica_total * grad_scale
    key_rows = key_sum.astype(jnp.bfloat16).reshape(micro_count, tok_dev, key_width)
    return (key_rows, input_grad, grad_buffer)


def grid_of(mesh):
    count = mesh.shape["fsdp"]
    spots = [getattr(d, "coords", None) for d in mesh.devices.reshape(count, -1)[:, 0]]
    if any(s is None for s in spots):
        return None
    sizes, step = [], 1
    while step < count:
        axis = [i for i in range(3) if spots[step][i] != spots[0][i]]
        if len(axis) != 1:
            return None
        seen = 1
        while seen * step < count and all(
            spots[seen * step][i] == spots[0][i] for i in range(3) if i != axis[0]
        ):
            seen += 1
        sizes.insert(0, seen)
        step *= seen
    return tuple(sizes)


def owner_at(grid, spot):
    nz, ny, nx = grid
    me = lax.axis_index("fsdp")
    z, y, x = me // (ny * nx), me // nx % ny, me % nx
    dz, dy, dx = spot
    return (((z + dz) % nz) * ny + (y + dy) % ny) * nx + (x + dx) % nx


def wgrad_kernel(grid, lists, order_ref, x_ref, cot_ref, xgot_ref, cgot_ref, *outs):
    half = lax.axis_index("dp") % 2
    cot = jnp.concatenate([cot_ref[...], cgot_ref[...]], axis=0)
    for out, spots in zip(outs, lists):
        columns = []
        for spot in spots:
            col = order_ref[owner_at(grid, spot)]
            at = pl.ds(pl.multiple_of((2 * col + half) * LANES, LANES), LANES)
            columns.append(jnp.concatenate([x_ref[:, at], xgot_ref[:, at]], axis=0))
        out[...] = lax.dot_general(
            jnp.concatenate(columns, axis=1),
            cot,
            (((0,), (0,)), ((), ())),
            preferred_element_type=jnp.float32,
        ).astype(out.dtype)


def apply_kernel(grid, pieces, first, order_ref, x_ref, cot_ref, *refs):
    half = lax.axis_index("dp") % 2
    refs = list(refs)
    scratch, sems = refs[-2:]
    key_ref, grad_ref = refs[-4:-2]
    weights = refs[: len(pieces)]
    cot = cot_ref[...]
    total = None if first else refs[len(pieces)][...]
    copies = []
    for place, (weight_ref, (spots, partner)) in enumerate(zip(weights, pieces)):
        side = 1 - half if partner else half
        starts = []
        for spot in spots:
            col = order_ref[owner_at(grid, spot)]
            starts.append(pl.multiple_of((2 * col + side) * LANES, LANES))
        weight = weight_ref[...]
        back = lax.dot_general(
            cot, weight, (((1,), (1,)), ((), ())), preferred_element_type=jnp.float32
        )
        scratch[place] = back.astype(scratch.dtype)
        for k, s in enumerate(starts):
            copy = pltpu.make_async_copy(
                scratch.at[place, :, k * LANES : (k + 1) * LANES],
                grad_ref.at[:, pl.ds(s, LANES)],
                sems.at[len(copies)],
            )
            copy.start()
            copies.append(copy)
        columns = jnp.concatenate([x_ref[:, pl.ds(s, LANES)] for s in starts], axis=1)
        term = jnp.dot(columns, weight, preferred_element_type=jnp.float32)
        total = term if total is None else total + term
    key_ref[...] = total.astype(key_ref.dtype)
    for copy in copies:
        copy.wait()


def staged_body(grid, normed, kv_cotangent, kv_weight, main_grad, owner_order):
    nz, ny, nx = grid
    micro_count, tok_dev, width = normed.shape
    shard_rows, key_width = kv_weight.shape
    owners, replicas = lax.axis_size("fsdp"), lax.axis_size("dp")
    rows = micro_count * tok_dev
    part = shard_rows // 2
    half = lax.axis_index("dp") % 2
    f32, bf16 = jnp.float32, jnp.bfloat16
    vmem = pl.BlockSpec(memory_space=pltpu.VMEM)
    smem = pl.BlockSpec(memory_space=pltpu.SMEM)
    anywhere = pl.BlockSpec(memory_space=pl.ANY)

    def send(value, move):
        pairs = []
        for z in range(nz):
            for y in range(ny):
                for x in range(nx):
                    for r in range(replicas):
                        tz, ty, tx, tr = move(z, y, x, r)
                        to = ((tz % nz) * ny + ty % ny) * nx + tx % nx
                        pairs.append((((z * ny + y) * nx + x) * replicas + r, to * replicas + tr))
        return lax.ppermute(value, ("fsdp", "dp"), pairs)

    def over_x(value):
        return send(value, lambda z, y, x, r: (z, y, x + 1, r))

    def over_y(value):
        return send(value, lambda z, y, x, r: (z, y + 1, x, r))

    def over_z(value, far):
        return send(value, lambda z, y, x, r: (z + far, y, x, r))

    def to_core(value):
        return send(value, lambda z, y, x, r: (z, y, x, r ^ 1))

    flat = normed.reshape(rows, width)
    cot = kv_cotangent.reshape(rows, key_width)
    cut = nz // 2
    near, far = range(cut), range(cut, nz)
    red_rows, blue_rows = part * len(near), part * len(far)

    xgot = to_core(flat)
    cgot = to_core(cot)

    def wgrad(lists, dtype):
        return pl.pallas_call(
            functools.partial(wgrad_kernel, grid, lists),
            in_specs=[smem] + [vmem] * 4,
            out_specs=[vmem] * len(lists),
            out_shape=[
                jax.ShapeDtypeStruct((part * len(s), key_width), dtype) for s in lists
            ],
            cost_estimate=pl.CostEstimate(
                flops=rows * width * key_width,
                bytes_accessed=4 * rows * width,
                transcendentals=0,
            ),
            compiler_params=pltpu.CompilerParams(vmem_limit_bytes=24 << 20),
        )(owner_order, flat, cot, xgot, cgot)

    red_out, blue_out = wgrad(
        [
            [(k, 1, dx) for dx in (0, 1) for k in near],
            [(k, dy, 1) for dy in (0, 1) for k in far],
        ],
        bf16,
    )
    red_on, blue_on, red_keep, blue_keep = wgrad(
        [
            [(k, 0, 1) for k in near],
            [(k, 1, 0) for k in far],
            [(k, 0, 0) for k in near],
            [(k, 0, 0) for k in far],
        ],
        f32,
    )

    own = lax.dynamic_slice_in_dim(kv_weight, half * part, part, axis=0)
    line = [own] + [over_z(own, d) for d in range(1, nz)]
    red = jnp.concatenate(line[:cut], axis=0)
    blue = jnp.concatenate(line[cut:], axis=0)
    red = jnp.concatenate([red, over_x(red)], axis=0)
    blue = jnp.concatenate([blue, over_y(blue)], axis=0)
    red_y = over_y(red)
    blue_x = over_x(blue)
    red_spots = [(-k, 0, dx) for dx in (0, 1) for k in near]
    blue_spots = [(-k, dy, 0) for dy in (0, 1) for k in far]
    red_y_spots = [(-k, 1, dx) for dx in (0, 1) for k in near]
    blue_x_spots = [(-k, dy, 1) for dy in (0, 1) for k in far]

    red_in = over_y(red_out)
    blue_in = over_x(blue_out)
    red_far = (red_on + red_in[red_rows:]).astype(bf16)
    blue_far = (blue_on + blue_in[blue_rows:]).astype(bf16)
    red_sum = red_keep + red_in[:red_rows] + over_x(red_far)
    blue_sum = blue_keep + blue_in[:blue_rows] + over_y(blue_far)
    along = [red_sum[k * part : (k + 1) * part] for k in range(len(near))]
    along += [blue_sum[k * part : (k + 1) * part] for k in range(len(far))]
    total = along[0]
    for d in range(1, nz):
        total = total + over_z(along[d].astype(bf16), d)
    if replicas > 2:
        groups = [[r for r in range(replicas) if r % 2 == h] for h in (0, 1)]
        total = lax.psum(total, "dp", axis_index_groups=groups)
    grad_scale = 1.0 / math.sqrt(rows * owners * replicas)
    kept = lax.dynamic_slice_in_dim(main_grad, half * part, part, axis=0) + total * grad_scale
    there = to_core(kept)
    grad_buffer = jnp.where(
        half == 0,
        jnp.concatenate([kept, there], axis=0),
        jnp.concatenate([there, kept], axis=0),
    )

    def apply(pieces, before, last):
        weights = [w for w, _, _ in pieces]
        inputs = [owner_order, flat, cot, *weights, *before]
        specs = [smem, vmem, vmem] + [vmem] * len(pieces) + [vmem, anywhere][: len(before)]
        return pl.pallas_call(
            functools.partial(apply_kernel, grid, [p[1:] for p in pieces], not before),
            in_specs=specs,
            out_specs=[vmem, anywhere],
            out_shape=[
                jax.ShapeDtypeStruct((rows, key_width), bf16 if last else f32),
                jax.ShapeDtypeStruct((rows, width), bf16),
            ],
            scratch_shapes=[
                pltpu.VMEM((len(pieces), rows, max(w.shape[0] for w in weights)), bf16),
                pltpu.SemaphoreType.DMA((sum(len(p[1]) for p in pieces),)),
            ],
            input_output_aliases={len(inputs) - 1: 1} if before else {},
            cost_estimate=pl.CostEstimate(
                flops=4 * rows * key_width * sum(w.shape[0] for w in weights),
                bytes_accessed=2 * rows * width,
                transcendentals=0,
            ),
            compiler_params=pltpu.CompilerParams(vmem_limit_bytes=24 << 20),
        )(*inputs)

    done = apply(
        [
            (red, red_spots, False),
            (blue, blue_spots, False),
            (to_core(red), red_spots, True),
            (to_core(blue), blue_spots, True),
        ],
        (),
        False,
    )
    done = apply([(red_y, red_y_spots, False), (blue_x, blue_x_spots, False)], done, False)
    key, input_grad = apply(
        [(to_core(red_y), red_y_spots, True), (to_core(blue_x), blue_x_spots, True)], done, True
    )
    return (
        key.reshape(micro_count, tok_dev, key_width),
        input_grad.reshape(micro_count, tok_dev, width),
        grad_buffer,
    )


def solution(mesh):
    in_specs = (
        P(None, ("fsdp", "dp"), None),
        P(None, ("fsdp", "dp"), None),
        P("fsdp", None),
        P("fsdp", None),
        P(),
    )
    out_specs = (P(None, ("fsdp", "dp"), None), P(None, ("fsdp", "dp"), None), P("fsdp", None))
    grid = grid_of(mesh)
    staged = grid is not None and len(grid) == 3 and grid[1:] == (2, 2)
    staged = staged and mesh.shape["dp"] % 2 == 0

    def body(normed, kv_cotangent, kv_weight, main_grad, owner_order):
        args = (normed, kv_cotangent, kv_weight, main_grad, owner_order)
        if staged and kv_weight.shape[0] == 2 * LANES:
            return staged_body(grid, *args)
        return plain_body(*args)

    return jax.shard_map(body, mesh=mesh, in_specs=in_specs, out_specs=out_specs, check_vma=False)
```

profile of v0, /device:TPU:0, one launch (start us, length us, event | category | flops | bytes accessed | tf_op | source)
XLA Modules:
  0.0 84.5 jit_solution(16615401152178215267)
XLA Ops:
  0.6 0.0 copy-start
  0.6 0.6 collective-permute-start.11
  1.2 0.1 collective-permute-start.12
  1.3 0.3 copy-done
  1.6 4.1 %collective-permute-start.4 = (bf16[128,512]{1,0:T(8,128)(2,1)S(1)}, bf16[128,512]{1,0:T(8,128)(2,1)S(1)}, u32[]{:S(2)}, u32[]{:S(2)}) collective-permute-start(bf16[128,512]{1,0:T(8,128)(2,1)S(1)} %constant_dynamic-slice_fusion), channel_id=1, source_target_pairs={{0,16},{1,17},{2,18},{3,19},{4,20},{5,21},{6,22},{7,23},{8,24},{9,... | collective-permute-start | bytes 393224 | tf_op jit(solution)/shard_map/ppermute | solution.py:148
  5.7 1.3 %collective-permute-start.5 = (bf16[128,512]{1,0:T(8,128)(2,1)S(1)}, bf16[128,512]{1,0:T(8,128)(2,1)S(1)}, u32[]{:S(2)}, u32[]{:S(2)}) collective-permute-start(bf16[128,512]{1,0:T(8,128)(2,1)S(1)} %constant_dynamic-slice_fusion), channel_id=1, source_target_pairs={{0,24},{1,25},{2,26},{3,27},{4,28},{5,29},{6,30},{7,31},{8,0},{9,1... | collective-permute-start | bytes 393224 | tf_op jit(solution)/shard_map/ppermute | solution.py:148
  7.1 0.7 collective-permute-start
  7.8 0.0 collective-permute-done.12.cgot_ref
  7.8 0.0 collective-permute-done.11.xgot_ref
  7.8 1.6 %copy-done.1 = bf16[2,128,4096]{2,1,0:T(8,128)(2,1)S(1)} copy-done((bf16[2,128,4096]{2,1,0:T(8,128)(2,1)S(1)}, bf16[2,128,4096]{2,1,0:T(8,128)(2,1)}, u32[]{:S(2)}) %copy-start.1) | copy-done | bytes 2097176
  9.4 0.9 %copy-done.3 = bf16[2,128,512]{2,1,0:T(8,128)(2,1)S(1)} copy-done((bf16[2,128,512]{2,1,0:T(8,128)(2,1)S(1)}, bf16[2,128,512]{2,1,0:T(8,128)(2,1)}, u32[]{:S(2)}) %copy-start.3) | copy-done | bytes 262168
  10.3 0.7 copy-done.5
  11.0 1.3 %shard_map.80 = (bf16[512,512]{1,0:T(8,128)(2,1)S(1)}, bf16[512,512]{1,0:T(8,128)(2,1)S(1)}) custom-call(s32[16]{0:T(128)S(1)} %copy-done.5, bf16[256,4096]{1,0:T(8,128)(2,1)S(1)} %bitcast.5, bf16[256,512]{1,0:T(8,128)(2,1)S(1)} %bitcast.11, bf16[256,4096]{1,0:T(8,128)(2,1)S(1)} %collective-permute-done.11.xgot_ref, ...), custom_call_target="tpu_custom_call" | custom-call | flops 536870912 | bytes 4194304 | tf_op jit(solution)/shard_map/pallas_call | solution.py:172
  12.3 1.6 %collective-permute-start.13 = (bf16[512,512]{1,0:T(8,128)(2,1)S(1)}, bf16[512,512]{1,0:T(8,128)(2,1)S(1)}, u32[]{:S(2)}, u32[]{:S(2)}) collective-permute-start(bf16[512,512]{1,0:T(8,128)(2,1)S(1)} %get-tuple-element.22), channel_id=1, source_target_pairs={{0,4},{1,5},{2,6},{3,7},{4,0},{5,1},{6,2},{7,3},{8,12},{9,13},{10,... | collective-permute-start | bytes 1572872 | tf_op jit(solution)/shard_map/ppermute | solution.py:148
  13.9 0.0 collective-permute-done.4
  13.9 0.0 collective-permute-done.5
  13.9 2.0 %collective-permute-start.6 = (bf16[256,512]{1,0:T(8,128)(2,1)S(1)}, bf16[256,512]{1,0:T(8,128)(2,1)S(1)}, u32[]{:S(2)}, u32[]{:S(2)}) collective-permute-start(bf16[256,512]{1,0:T(8,128)(2,1)S(1)} %pad_maximum_fusion.2), channel_id=1, source_target_pairs={{0,4},{1,5},{2,6},{3,7},{4,0},{5,1},{6,2},{7,3},{8,12},{9,13},{10,... | collective-permute-start | bytes 786440 | tf_op jit(solution)/shard_map/ppermute | solution.py:148
  15.9 0.1 collective-permute-done
  16.1 1.6 %collective-permute-start.1 = (bf16[256,512]{1,0:T(8,128)(2,1)S(1)}, bf16[256,512]{1,0:T(8,128)(2,1)S(1)}, u32[]{:S(2)}, u32[]{:S(2)}) collective-permute-start(bf16[256,512]{1,0:T(8,128)(2,1)S(1)} %pad_maximum_fusion.1), channel_id=1, source_target_pairs={{0,2},{1,3},{2,0},{3,1},{4,6},{5,7},{6,4},{7,5},{8,10},{9,11},{10,... | collective-permute-start | bytes 786440 | tf_op jit(solution)/shard_map/ppermute | solution.py:148
  17.6 0.7 constant_dynamic-update-slice_fusion.2
  18.3 0.7 constant_dynamic-update-slice_fusion.1
  19.0 0.5 collective-permute-start.16
  19.5 11.4 %collective-permute-done.6 = bf16[256,512]{1,0:T(8,128)(2,1)S(1)} collective-permute-done((bf16[256,512]{1,0:T(8,128)(2,1)S(1)}, bf16[256,512]{1,0:T(8,128)(2,1)S(1)}, u32[]{:S(2)}, u32[]{:S(2)}) %collective-permute-start.6) | collective-permute-done | bytes 262176 | tf_op jit(solution)/shard_map/ppermute | solution.py:148
  30.9 0.7 constant_dynamic-update-slice_fusion.refs_1_
  31.6 0.0 collective-permute-start.10
  31.6 1.7 %collective-permute-start.7 = (bf16[512,512]{1,0:T(8,128)(2,1)}, bf16[512,512]{1,0:T(8,128)(2,1)}, u32[]{:S(2)}, u32[]{:S(2)}) collective-permute-start(bf16[512,512]{1,0:T(8,128)(2,1)} %constant_dynamic-update-slice_fusion.refs_1_), channel_id=1, source_target_pairs={{0,2},{1,3},{2,0},{3,1},{4,6},{5,7},{6,4},{7,5},{8,10},{9,11},{10,... | collective-permute-start | bytes 1572872 | tf_op jit(solution)/shard_map/ppermute | solution.py:148
  33.3 1.3 %shard_map.79 = (f32[256,512]{1,0:T(8,128)S(1)}, f32[256,512]{1,0:T(8,128)S(1)}, f32[256,512]{1,0:T(8,128)S(1)}, f32[256,512]{1,0:T(8,128)S(1)}) custom-call(s32[16]{0:T(128)S(1)} %copy-done.5, bf16[256,4096]{1,0:T(8,128)(2,1)S(1)} %bitcast.6, bf16[256,512]{1,0:T(8,128)(2,1)S(1)} %bitcast.12, bf16[256,4096]{1,0:T(8,128)(2,1)S(1)} %collective-permute-done.11.xgot_ref, ...), custom_call_target="tpu_custom_call" | custom-call | flops 536870912 | bytes 4194304 | tf_op jit(solution)/shard_map/pallas_call | solution.py:172
  34.7 0.0 collective-permute-done.13
  34.7 0.1 add_convert_fusion.2
  34.8 0.4 collective-permute-start.14
  35.1 0.0 collective-permute-done.1
  35.2 0.1 collective-permute-start.9
  35.3 0.0 collective-permute-done.16
  35.3 1.8 %collective-permute-start.2 = (bf16[512,512]{1,0:T(8,128)(2,1)S(1)}, bf16[512,512]{1,0:T(8,128)(2,1)}, u32[]{:S(2)}, u32[]{:S(2)}) collective-permute-start(bf16[512,512]{1,0:T(8,128)(2,1)S(1)} %pad_maximum_fusion.refs_0_), channel_id=1, source_target_pairs={{0,4},{1,5},{2,6},{3,7},{4,0},{5,1},{6,2},{7,3},{8,12},{9,13},{10,... | collective-permute-start | bytes 1572872 | tf_op jit(solution)/shard_map/ppermute | solution.py:148
  37.1 0.1 add_convert_fusion.1
  37.2 0.0 copy-start.7
  37.2 14.6 %collective-permute-done.14 = bf16[256,512]{1,0:T(8,128)(2,1)S(1)} collective-permute-done((bf16[256,512]{1,0:T(8,128)(2,1)S(1)}, bf16[256,512]{1,0:T(8,128)(2,1)S(1)}, u32[]{:S(2)}, u32[]{:S(2)}) %collective-permute-start.14) | collective-permute-done | bytes 262176 | tf_op jit(solution)/shard_map/ppermute | solution.py:148
  51.8 1.7 %collective-permute-start.17 = (bf16[256,512]{1,0:T(8,128)(2,1)S(1)}, bf16[256,512]{1,0:T(8,128)(2,1)S(1)}, u32[]{:S(2)}, u32[]{:S(2)}) collective-permute-start(bf16[256,512]{1,0:T(8,128)(2,1)S(1)} %add_convert_fusion.1), channel_id=1, source_target_pairs={{0,4},{1,5},{2,6},{3,7},{4,0},{5,1},{6,2},{7,3},{8,12},{9,13},{10,... | collective-permute-start | bytes 786440 | tf_op jit(solution)/shard_map/ppermute | solution.py:148
  53.5 0.1 convert_add_fusion
  53.7 6.0 %collective-permute-done.17 = bf16[256,512]{1,0:T(8,128)(2,1)S(1)} collective-permute-done((bf16[256,512]{1,0:T(8,128)(2,1)S(1)}, bf16[256,512]{1,0:T(8,128)(2,1)S(1)}, u32[]{:S(2)}, u32[]{:S(2)}) %collective-permute-start.17) | collective-permute-done | bytes 262176 | tf_op jit(solution)/shard_map/ppermute | solution.py:148
  59.7 2.3 %collective-permute-start.15 = (bf16[128,512]{1,0:T(8,128)(2,1)S(1)}, bf16[128,512]{1,0:T(8,128)(2,1)S(1)}, u32[]{:S(2)}, u32[]{:S(2)}) collective-permute-start(bf16[128,512]{1,0:T(8,128)(2,1)S(1)} %slice.57), channel_id=1, source_target_pairs={{0,8},{1,9},{2,10},{3,11},{4,12},{5,13},{6,14},{7,15},{8,16},{9,17... | collective-permute-start | bytes 393224 | tf_op jit(solution)/shard_map/ppermute | solution.py:148
  61.9 0.1 add_convert_fusion
  62.1 0.0 collective-permute-done.7.refs_1_
  62.1 2.7 %collective-permute-start.18 = (bf16[128,512]{1,0:T(8,128)(2,1)S(1)}, bf16[128,512]{1,0:T(8,128)(2,1)S(1)}, u32[]{:S(2)}, u32[]{:S(2)}) collective-permute-start(bf16[128,512]{1,0:T(8,128)(2,1)S(1)} %get-tuple-element.27), channel_id=1, source_target_pairs={{0,16},{1,17},{2,18},{3,19},{4,20},{5,21},{6,22},{7,23},{8,24},{9,... | collective-permute-start | bytes 393224 | tf_op jit(solution)/shard_map/ppermute | solution.py:148
  64.7 0.0 collective-permute-done.2.refs_0_
  64.7 2.5 %collective-permute-start.19 = (bf16[128,512]{1,0:T(8,128)(2,1)S(1)}, bf16[128,512]{1,0:T(8,128)(2,1)S(1)}, u32[]{:S(2)}, u32[]{:S(2)}) collective-permute-start(bf16[128,512]{1,0:T(8,128)(2,1)S(1)} %get-tuple-element.28), channel_id=1, source_target_pairs={{0,24},{1,25},{2,26},{3,27},{4,28},{5,29},{6,30},{7,31},{8,0},{9,1... | collective-permute-start | bytes 393224 | tf_op jit(solution)/shard_map/ppermute | solution.py:148
  67.3 0.8 collective-permute-done.15
  68.0 0.0 collective-permute-start.8
  68.0 4.6 %collective-permute-done.18 = bf16[128,512]{1,0:T(8,128)(2,1)S(1)} collective-permute-done((bf16[128,512]{1,0:T(8,128)(2,1)S(1)}, bf16[128,512]{1,0:T(8,128)(2,1)S(1)}, u32[]{:S(2)}, u32[]{:S(2)}) %collective-permute-start.18) | collective-permute-done | bytes 131104 | tf_op jit(solution)/shard_map/ppermute | solution.py:148
  72.6 0.0 collective-permute-start.3
  72.6 0.0 collective-permute-done.19
  72.6 0.0 copy-done.7
  72.6 0.1 fusion.3
  72.7 0.6 collective-permute-start.20
  73.3 0.0 collective-permute-done.10.refs_3_
  73.3 0.0 collective-permute-done.9.refs_2_
  73.3 0.0 copy-done.2
  73.3 3.4 %shard_map.76 = (f32[256,512]{1,0:T(8,128)S(1)}, bf16[256,4096]{1,0:T(8,128)(2,1)}) custom-call(s32[16]{0:T(128)S(1)} %copy-done.6, bf16[256,4096]{1,0:T(8,128)(2,1)S(1)} %bitcast.7, bf16[256,512]{1,0:T(8,128)(2,1)S(1)} %bitcast.13, bf16[512,512]{1,0:T(8,128)(2,1)S(1)} %pad_maximum_fusion.refs_0_, ...), custom_call_target="tpu_custom_call" | custom-call | flops 1073741824 | bytes 2097152 | tf_op jit(solution)/shard_map/pallas_call | solution.py:244
  76.7 2.6 %shard_map.77 = (f32[256,512]{1,0:T(8,128)S(1)}, bf16[256,4096]{1,0:T(8,128)(2,1)}) custom-call(s32[16]{0:T(128)S(1)} %copy-done.6, bf16[256,4096]{1,0:T(8,128)(2,1)S(1)} %bitcast.8, bf16[256,512]{1,0:T(8,128)(2,1)S(1)} %bitcast.14, bf16[512,512]{1,0:T(8,128)(2,1)} %collective-permute-done.2.refs_0_, ...), custom_call_target="tpu_custom_call", output_to_operand_aliasing={{1}: (6, {})} | custom-call | flops 536870912 | bytes 2097152 | tf_op jit(solution)/shard_map/pallas_call | solution.py:244
  79.3 0.0 collective-permute-done.8.refs_1_
  79.3 0.0 collective-permute-done.3.refs_0_
  79.3 3.3 %shard_map.78 = (bf16[256,512]{1,0:T(8,128)(2,1)}, bf16[256,4096]{1,0:T(8,128)(2,1)}) custom-call(s32[16]{0:T(128)S(1)} %copy-done.6, bf16[256,4096]{1,0:T(8,128)(2,1)S(1)} %bitcast.9, bf16[256,512]{1,0:T(8,128)(2,1)S(1)} %bitcast.15, bf16[512,512]{1,0:T(8,128)(2,1)} %collective-permute-done.3.refs_0_, ...), custom_call_target="tpu_custom_call", output_to_operand_aliasing={{1}: (6, {})} | custom-call | flops 536870912 | bytes 2097152 | tf_op jit(solution)/shard_map/pallas_call | solution.py:244
  82.6 0.0 collective-permute-done.20
  82.6 1.9 %maximum_select_fusion = f32[256,512]{1,0:T(8,128)} fusion(f32[128,512]{1,0:T(8,128)} %collective-permute-done.20, f32[128,512]{1,0:T(8,128)S(1)} %fusion.3, pred[]{:T(512)S(6)} %eq.5), kind=kLoop, calls=%fused_computation.1 | loop fusion | flops 393216 | bytes 1048577 | tf_op jit(solution)/shard_map/jit(_where)/select_n | solution.py:234
  (14 shorter events, 0.1 us)
Async XLA Ops:
  0.6 1.0 %copy-start = (bf16[256,512]{1,0:T(8,128)(2,1)S(1)}, bf16[256,512]{1,0:T(8,128)(2,1)}, u32[]{:S(2)}) copy-start(bf16[256,512]{1,0:T(8,128)(2,1)} %param.7) | copy-start | bytes 786436
  0.6 7.1 %collective-permute-start.11 = (bf16[256,4096]{1,0:T(8,128)(2,1)}, bf16[256,4096]{1,0:T(8,128)(2,1)S(1)}, u32[]{:S(2)}, u32[]{:S(2)}) collective-permute-start(bf16[256,4096]{1,0:T(8,128)(2,1)} %bitcast.4), channel_id=1, source_target_pairs={{0,1},{1,0},{2,3},{3,2},{4,5},{5,4},{6,7},{7,6},{8,9},{9,8},{10,11... | collective-permute-start | bytes 6291464 | tf_op jit(solution)/shard_map/ppermute | solution.py:148
  1.2 6.6 %collective-permute-start.12 = (bf16[256,512]{1,0:T(8,128)(2,1)}, bf16[256,512]{1,0:T(8,128)(2,1)S(1)}, u32[]{:S(2)}, u32[]{:S(2)}) collective-permute-start(bf16[256,512]{1,0:T(8,128)(2,1)} %bitcast.10), channel_id=1, source_target_pairs={{0,1},{1,0},{2,3},{3,2},{4,5},{5,4},{6,7},{7,6},{8,9},{9,8},{10,11... | collective-permute-start | bytes 786440 | tf_op jit(solution)/shard_map/ppermute | solution.py:148
  1.6 12.3 %collective-permute-start.4 = (bf16[128,512]{1,0:T(8,128)(2,1)S(1)}, bf16[128,512]{1,0:T(8,128)(2,1)S(1)}, u32[]{:S(2)}, u32[]{:S(2)}) collective-permute-start(bf16[128,512]{1,0:T(8,128)(2,1)S(1)} %constant_dynamic-slice_fusion), channel_id=1, source_target_pairs={{0,16},{1,17},{2,18},{3,19},{4,20},{5,21},{6,22},{7,23},{8,24},{9,... | collective-permute-start | bytes 393224 | tf_op jit(solution)/shard_map/ppermute | solution.py:148
  5.7 8.2 %collective-permute-start.5 = (bf16[128,512]{1,0:T(8,128)(2,1)S(1)}, bf16[128,512]{1,0:T(8,128)(2,1)S(1)}, u32[]{:S(2)}, u32[]{:S(2)}) collective-permute-start(bf16[128,512]{1,0:T(8,128)(2,1)S(1)} %constant_dynamic-slice_fusion), channel_id=1, source_target_pairs={{0,24},{1,25},{2,26},{3,27},{4,28},{5,29},{6,30},{7,31},{8,0},{9,1... | collective-permute-start | bytes 393224 | tf_op jit(solution)/shard_map/ppermute | solution.py:148
  7.1 9.0 %collective-permute-start = (bf16[128,512]{1,0:T(8,128)(2,1)S(1)}, bf16[128,512]{1,0:T(8,128)(2,1)S(1)}, u32[]{:S(2)}, u32[]{:S(2)}) collective-permute-start(bf16[128,512]{1,0:T(8,128)(2,1)S(1)} %constant_dynamic-slice_fusion), channel_id=1, source_target_pairs={{0,8},{1,9},{2,10},{3,11},{4,12},{5,13},{6,14},{7,15},{8,16},{9,17... | collective-permute-start | bytes 393224 | tf_op jit(solution)/shard_map/ppermute | solution.py:148
  7.8 1.6 %copy-start.1 = (bf16[2,128,4096]{2,1,0:T(8,128)(2,1)S(1)}, bf16[2,128,4096]{2,1,0:T(8,128)(2,1)}, u32[]{:S(2)}) copy-start(bf16[2,128,4096]{2,1,0:T(8,128)(2,1)} %param.5) | copy-start | bytes 6291460
  9.4 0.9 %copy-start.3 = (bf16[2,128,512]{2,1,0:T(8,128)(2,1)S(1)}, bf16[2,128,512]{2,1,0:T(8,128)(2,1)}, u32[]{:S(2)}) copy-start(bf16[2,128,512]{2,1,0:T(8,128)(2,1)} %param.6) | copy-start | bytes 786436
  10.3 0.7 copy-start.5
  12.3 22.4 %collective-permute-start.13 = (bf16[512,512]{1,0:T(8,128)(2,1)S(1)}, bf16[512,512]{1,0:T(8,128)(2,1)S(1)}, u32[]{:S(2)}, u32[]{:S(2)}) collective-permute-start(bf16[512,512]{1,0:T(8,128)(2,1)S(1)} %get-tuple-element.22), channel_id=1, source_target_pairs={{0,4},{1,5},{2,6},{3,7},{4,0},{5,1},{6,2},{7,3},{8,12},{9,13},{10,... | collective-permute-start | bytes 1572872 | tf_op jit(solution)/shard_map/ppermute | solution.py:148
  13.9 17.0 %collective-permute-start.6 = (bf16[256,512]{1,0:T(8,128)(2,1)S(1)}, bf16[256,512]{1,0:T(8,128)(2,1)S(1)}, u32[]{:S(2)}, u32[]{:S(2)}) collective-permute-start(bf16[256,512]{1,0:T(8,128)(2,1)S(1)} %pad_maximum_fusion.2), channel_id=1, source_target_pairs={{0,4},{1,5},{2,6},{3,7},{4,0},{5,1},{6,2},{7,3},{8,12},{9,13},{10,... | collective-permute-start | bytes 786440 | tf_op jit(solution)/shard_map/ppermute | solution.py:148
  16.1 19.1 %collective-permute-start.1 = (bf16[256,512]{1,0:T(8,128)(2,1)S(1)}, bf16[256,512]{1,0:T(8,128)(2,1)S(1)}, u32[]{:S(2)}, u32[]{:S(2)}) collective-permute-start(bf16[256,512]{1,0:T(8,128)(2,1)S(1)} %pad_maximum_fusion.1), channel_id=1, source_target_pairs={{0,2},{1,3},{2,0},{3,1},{4,6},{5,7},{6,4},{7,5},{8,10},{9,11},{10,... | collective-permute-start | bytes 786440 | tf_op jit(solution)/shard_map/ppermute | solution.py:148
  19.0 16.3 %collective-permute-start.16 = (bf16[512,512]{1,0:T(8,128)(2,1)S(1)}, bf16[512,512]{1,0:T(8,128)(2,1)S(1)}, u32[]{:S(2)}, u32[]{:S(2)}) collective-permute-start(bf16[512,512]{1,0:T(8,128)(2,1)S(1)} %get-tuple-element.25), channel_id=1, source_target_pairs={{0,2},{1,3},{2,0},{3,1},{4,6},{5,7},{6,4},{7,5},{8,10},{9,11},{10,... | collective-permute-start | bytes 1572872 | tf_op jit(solution)/shard_map/ppermute | solution.py:148
  31.6 41.6 %collective-permute-start.10 = (bf16[512,512]{1,0:T(8,128)(2,1)}, bf16[512,512]{1,0:T(8,128)(2,1)}, u32[]{:S(2)}, u32[]{:S(2)}) collective-permute-start(bf16[512,512]{1,0:T(8,128)(2,1)} %constant_dynamic-update-slice_fusion.refs_1_), channel_id=1, source_target_pairs={{0,1},{1,0},{2,3},{3,2},{4,5},{5,4},{6,7},{7,6},{8,9},{9,8},{10,11... | collective-permute-start | bytes 1572872 | tf_op jit(solution)/shard_map/ppermute | solution.py:148
  31.6 30.4 %collective-permute-start.7 = (bf16[512,512]{1,0:T(8,128)(2,1)}, bf16[512,512]{1,0:T(8,128)(2,1)}, u32[]{:S(2)}, u32[]{:S(2)}) collective-permute-start(bf16[512,512]{1,0:T(8,128)(2,1)} %constant_dynamic-update-slice_fusion.refs_1_), channel_id=1, source_target_pairs={{0,2},{1,3},{2,0},{3,1},{4,6},{5,7},{6,4},{7,5},{8,10},{9,11},{10,... | collective-permute-start | bytes 1572872 | tf_op jit(solution)/shard_map/ppermute | solution.py:148
  34.8 17.0 %collective-permute-start.14 = (bf16[256,512]{1,0:T(8,128)(2,1)S(1)}, bf16[256,512]{1,0:T(8,128)(2,1)S(1)}, u32[]{:S(2)}, u32[]{:S(2)}) collective-permute-start(bf16[256,512]{1,0:T(8,128)(2,1)S(1)} %add_convert_fusion.2), channel_id=1, source_target_pairs={{0,2},{1,3},{2,0},{3,1},{4,6},{5,7},{6,4},{7,5},{8,10},{9,11},{10,... | collective-permute-start | bytes 786440 | tf_op jit(solution)/shard_map/ppermute | solution.py:148
  35.2 38.1 %collective-permute-start.9 = (bf16[512,512]{1,0:T(8,128)(2,1)S(1)}, bf16[512,512]{1,0:T(8,128)(2,1)}, u32[]{:S(2)}, u32[]{:S(2)}) collective-permute-start(bf16[512,512]{1,0:T(8,128)(2,1)S(1)} %pad_maximum_fusion.refs_0_), channel_id=1, source_target_pairs={{0,1},{1,0},{2,3},{3,2},{4,5},{5,4},{6,7},{7,6},{8,9},{9,8},{10,11... | collective-permute-start | bytes 1572872 | tf_op jit(solution)/shard_map/ppermute | solution.py:148
  35.3 29.4 %collective-permute-start.2 = (bf16[512,512]{1,0:T(8,128)(2,1)S(1)}, bf16[512,512]{1,0:T(8,128)(2,1)}, u32[]{:S(2)}, u32[]{:S(2)}) collective-permute-start(bf16[512,512]{1,0:T(8,128)(2,1)S(1)} %pad_maximum_fusion.refs_0_), channel_id=1, source_target_pairs={{0,4},{1,5},{2,6},{3,7},{4,0},{5,1},{6,2},{7,3},{8,12},{9,13},{10,... | collective-permute-start | bytes 1572872 | tf_op jit(solution)/shard_map/ppermute | solution.py:148
  37.2 35.4 %copy-start.7 = (f32[256,512]{1,0:T(8,128)S(1)}, f32[256,512]{1,0:T(8,128)}, u32[]{:S(2)}) copy-start(f32[256,512]{1,0:T(8,128)} %param.8) | copy-start | bytes 1572868
  51.8 7.9 %collective-permute-start.17 = (bf16[256,512]{1,0:T(8,128)(2,1)S(1)}, bf16[256,512]{1,0:T(8,128)(2,1)S(1)}, u32[]{:S(2)}, u32[]{:S(2)}) collective-permute-start(bf16[256,512]{1,0:T(8,128)(2,1)S(1)} %add_convert_fusion.1), channel_id=1, source_target_pairs={{0,4},{1,5},{2,6},{3,7},{4,0},{5,1},{6,2},{7,3},{8,12},{9,13},{10,... | collective-permute-start | bytes 786440 | tf_op jit(solution)/shard_map/ppermute | solution.py:148
  53.5 19.7 %copy-start.2 = (bf16[2,128,4096]{2,1,0:T(8,128)(2,1)S(1)}, bf16[2,128,4096]{2,1,0:T(8,128)(2,1)}, u32[]{:S(2)}) copy-start(bf16[2,128,4096]{2,1,0:T(8,128)(2,1)} %param.5) | copy-start | bytes 6291460
  53.5 19.7 %copy-start.4 = (bf16[2,128,512]{2,1,0:T(8,128)(2,1)S(1)}, bf16[2,128,512]{2,1,0:T(8,128)(2,1)}, u32[]{:S(2)}) copy-start(bf16[2,128,512]{2,1,0:T(8,128)(2,1)} %param.6) | copy-start | bytes 786436
  53.5 19.7 %copy-start.6 = (s32[16]{0:T(128)S(1)}, s32[16]{0:T(128)}, u32[]{:S(2)}) copy-start(s32[16]{0:T(128)} %order_ref.9) | copy-start | bytes 196
  59.7 8.4 %collective-permute-start.15 = (bf16[128,512]{1,0:T(8,128)(2,1)S(1)}, bf16[128,512]{1,0:T(8,128)(2,1)S(1)}, u32[]{:S(2)}, u32[]{:S(2)}) collective-permute-start(bf16[128,512]{1,0:T(8,128)(2,1)S(1)} %slice.57), channel_id=1, source_target_pairs={{0,8},{1,9},{2,10},{3,11},{4,12},{5,13},{6,14},{7,15},{8,16},{9,17... | collective-permute-start | bytes 393224 | tf_op jit(solution)/shard_map/ppermute | solution.py:148
  62.1 10.5 %collective-permute-start.18 = (bf16[128,512]{1,0:T(8,128)(2,1)S(1)}, bf16[128,512]{1,0:T(8,128)(2,1)S(1)}, u32[]{:S(2)}, u32[]{:S(2)}) collective-permute-start(bf16[128,512]{1,0:T(8,128)(2,1)S(1)} %get-tuple-element.27), channel_id=1, source_target_pairs={{0,16},{1,17},{2,18},{3,19},{4,20},{5,21},{6,22},{7,23},{8,24},{9,... | collective-permute-start | bytes 393224 | tf_op jit(solution)/shard_map/ppermute | solution.py:148
  64.7 7.9 %collective-permute-start.19 = (bf16[128,512]{1,0:T(8,128)(2,1)S(1)}, bf16[128,512]{1,0:T(8,128)(2,1)S(1)}, u32[]{:S(2)}, u32[]{:S(2)}) collective-permute-start(bf16[128,512]{1,0:T(8,128)(2,1)S(1)} %get-tuple-element.28), channel_id=1, source_target_pairs={{0,24},{1,25},{2,26},{3,27},{4,28},{5,29},{6,30},{7,31},{8,0},{9,1... | collective-permute-start | bytes 393224 | tf_op jit(solution)/shard_map/ppermute | solution.py:148
  68.0 11.3 %collective-permute-start.8 = (bf16[512,512]{1,0:T(8,128)(2,1)}, bf16[512,512]{1,0:T(8,128)(2,1)}, u32[]{:S(2)}, u32[]{:S(2)}) collective-permute-start(bf16[512,512]{1,0:T(8,128)(2,1)} %collective-permute-done.7.refs_1_), channel_id=1, source_target_pairs={{0,1},{1,0},{2,3},{3,2},{4,5},{5,4},{6,7},{7,6},{8,9},{9,8},{10,11... | collective-permute-start | bytes 1572872 | tf_op jit(solution)/shard_map/ppermute | solution.py:148
  72.6 6.7 %collective-permute-start.3 = (bf16[512,512]{1,0:T(8,128)(2,1)}, bf16[512,512]{1,0:T(8,128)(2,1)}, u32[]{:S(2)}, u32[]{:S(2)}) collective-permute-start(bf16[512,512]{1,0:T(8,128)(2,1)} %collective-permute-done.2.refs_0_), channel_id=1, source_target_pairs={{0,1},{1,0},{2,3},{3,2},{4,5},{5,4},{6,7},{7,6},{8,9},{9,8},{10,11... | collective-permute-start | bytes 1572872 | tf_op jit(solution)/shard_map/ppermute | solution.py:148
  72.7 9.9 %collective-permute-start.20 = (f32[128,512]{1,0:T(8,128)S(1)}, f32[128,512]{1,0:T(8,128)}, u32[]{:S(2)}, u32[]{:S(2)}) collective-permute-start(f32[128,512]{1,0:T(8,128)S(1)} %fusion.3), channel_id=1, source_target_pairs={{0,1},{1,0},{2,3},{3,2},{4,5},{5,4},{6,7},{7,6},{8,9},{9,8},{10,11... | collective-permute-start | bytes 786440 | tf_op jit(solution)/shard_map/ppermute | solution.py:148
where the time goes:
time: 84.8 us; the launch traced here: 84.5 us
  waiting for transfers between devices  37.5 us (44%)
  starting transfers between devices  26.2 us (31%)
  Pallas kernels  11.9 us (14%)
  local copies, waits for them, and re-layouts  5.62 us (7%)
  other arithmetic  2.4 us (3%)
  between operations  0.85 us (1%)
    ppermute x21, waiting for transfers between devices, send(): return lax.ppermute(value, ('fsdp', 'dp'), pairs)  37.5 us
    ppermute x21, starting transfers between devices, send(): return lax.ppermute(value, ('fsdp', 'dp'), pairs)  26.2 us
    pallas_call x3, Pallas kernels, apply(): pl.pallas_call(functools.partial(apply_kernel, grid, [p[1:] for p in piec...  9.25 us
    unnamed x18, local copies, waits for them, and re-layouts  4.85 us
    pallas_call x2, Pallas kernels, wgrad(): pl.pallas_call(functools.partial(wgrad_kernel, grid, lists), in_specs=[sm...  2.65 us
    select_n x1, other arithmetic, staged_body(): jnp.where(half == 0, jnp.concatenate([kept, there], axis=0), jnp.concaten...  1.89 us
  transfers between devices with their start and end apart: 21, of which 6 were waited for; matrix products, arithmetic and copies ran while one was open for 3% of the time, Pallas kernels for 14%

commit v1 on v0

--- a/solution.py
+++ b/solution.py
@@ -10,6 +10,7 @@
 
 
 LANES = 128
+TIGHT_BYTES = 62 << 20
 
 
 def plain_body(normed, kv_cotangent, kv_weight, main_grad, owner_order):
@@ -70,57 +71,120 @@
     return (((z + dz) % nz) * ny + (y + dy) % ny) * nx + (x + dx) % nx
 
 
-def wgrad_kernel(grid, lists, order_ref, x_ref, cot_ref, xgot_ref, cgot_ref, *outs):
+def stage_kernel(grid, lists, order_ref, x_ref, cot_ref, *refs):
+    outs, (buf, x_sems, cot_sems) = refs[: 2 * len(lists)], refs[2 * len(lists) :]
+    chunks, step, _ = buf.shape
     half = lax.axis_index("dp") % 2
-    cot = jnp.concatenate([cot_ref[...], cgot_ref[...]], axis=0)
-    for out, spots in zip(outs, lists):
-        columns = []
-        for spot in spots:
-            col = order_ref[owner_at(grid, spot)]
-            at = pl.ds(pl.multiple_of((2 * col + half) * LANES, LANES), LANES)
-            columns.append(jnp.concatenate([x_ref[:, at], xgot_ref[:, at]], axis=0))
+    loads = []
+    for c in range(chunks):
+        rows = pl.ds(c * step, step)
+        loads.append(pltpu.make_async_copy(x_ref.at[rows], buf.at[c], x_sems.at[c]))
+        loads[-1].start()
+    stores = []
+    for side in range(2):
+        to_ref = outs[side * len(lists)]
+        to = to_ref.at[:, len(lists[0]) * LANES :]
+        stores.append(pltpu.make_async_copy(cot_ref, to, cot_sems.at[side]))
+        stores[-1].start()
+    starts = []
+    for spots in lists:
+        cols = [order_ref[owner_at(grid, spot)] for spot in spots]
+        starts.append(cols)
+    for c in range(chunks):
+        loads[c].wait()
+        rows = slice(c * step, (c + 1) * step)
+        for side in range(2):
+            which = half if side == 0 else 1 - half
+            for cols, to_ref in zip(starts, outs[side * len(lists) :]):
+                for k, col in enumerate(cols):
+                    at = pl.ds(pl.multiple_of((2 * col + which) * LANES, LANES), LANES)
+                    to_ref[rows, k * LANES : (k + 1) * LANES] = buf[c, :, at]
+    for store in stores:
+        store.wait()
+
+
+def wgrad_kernel(cot_at, keep, *refs):
+    first, refs = refs[:2], refs[2:]
+    cot = jnp.concatenate([r[:, cot_at:] for r in first], axis=0)
+    sources = first
+    if keep:
+        sources, refs = refs[:2], refs[2:]
+    begin = 0
+    for out in refs:
+        at = slice(begin, begin + out.shape[0])
         out[...] = lax.dot_general(
-            jnp.concatenate(columns, axis=1),
+            jnp.concatenate([r[:, at] for r in sources], axis=0),
             cot,
             (((0,), (0,)), ((), ())),
             preferred_element_type=jnp.float32,
         ).astype(out.dtype)
-
-
-def apply_kernel(grid, pieces, first, order_ref, x_ref, cot_ref, *refs):
+        begin += out.shape[0]
+
+
+def apply_kernel(grid, pieces, first, last, order_ref, cot_ref, *refs):
     half = lax.axis_index("dp") % 2
     refs = list(refs)
-    scratch, sems = refs[-2:]
-    key_ref, grad_ref = refs[-4:-2]
-    weights = refs[: len(pieces)]
+    weights = [refs.pop(0) for _ in pieces]
+    columns = {}
+    for _, partner in pieces:
+        if partner not in columns:
+            columns[partner] = [refs.pop(0), 0]
+    before_ref = None if first else refs.pop(0)
+    if not first:
+        refs.pop(0)
+    halves = [refs.pop(0) for _ in range(2)] if last else []
+    key_ref, grad_ref = refs.pop(0), refs.pop(0)
+    buffer_ref = refs.pop(0) if last else None
+    scratch, total_buf, key_buf, out_sems, sems = refs
+    if not first:
+        fetch = pltpu.make_async_copy(before_ref, total_buf, sems.at[0])
+        fetch.start()
+    stores = []
+    for k, ref in enumerate(halves):
+        part = ref.shape[0]
+        side = half if k == 0 else 1 - half
+        stores.append(
+            pltpu.make_async_copy(
+                ref, buffer_ref.at[pl.ds(pl.multiple_of(side * part, part), part)], sems.at[2 + k]
+            )
+        )
+        stores[-1].start()
     cot = cot_ref[...]
-    total = None if first else refs[len(pieces)][...]
-    copies = []
-    for place, (weight_ref, (spots, partner)) in enumerate(zip(weights, pieces)):
+    count = 0
+    for place, (spots, partner) in enumerate(pieces):
         side = 1 - half if partner else half
-        starts = []
-        for spot in spots:
-            col = order_ref[owner_at(grid, spot)]
-            starts.append(pl.multiple_of((2 * col + side) * LANES, LANES))
-        weight = weight_ref[...]
         back = lax.dot_general(
-            cot, weight, (((1,), (1,)), ((), ())), preferred_element_type=jnp.float32
+            cot, weights[place][...], (((1,), (1,)), ((), ())), preferred_element_type=jnp.float32
         )
         scratch[place] = back.astype(scratch.dtype)
-        for k, s in enumerate(starts):
-            copy = pltpu.make_async_copy(
-                scratch.at[place, :, k * LANES : (k + 1) * LANES],
-                grad_ref.at[:, pl.ds(s, LANES)],
-                sems.at[len(copies)],
+        for k, spot in enumerate(spots):
+            col = order_ref[owner_at(grid, spot)]
+            start = pl.multiple_of((2 * col + side) * LANES, LANES)
+            stores.append(
+                pltpu.make_async_copy(
+                    scratch.at[place, :, k * LANES : (k + 1) * LANES],
+                    grad_ref.at[:, pl.ds(start, LANES)],
+                    out_sems.at[count],
+                )
             )
-            copy.start()
-            copies.append(copy)
-        columns = jnp.concatenate([x_ref[:, pl.ds(s, LANES)] for s in starts], axis=1)
-        term = jnp.dot(columns, weight, preferred_element_type=jnp.float32)
+            stores[-1].start()
+            count += 1
+    total = None
+    for place, (spots, partner) in enumerate(pieces):
+        source, begin = columns[partner]
+        columns[partner][1] = end = begin + len(spots) * LANES
+        term = jnp.dot(
+            source[:, begin:end], weights[place][...], preferred_element_type=jnp.float32
+        )
         total = term if total is None else total + term
-    key_ref[...] = total.astype(key_ref.dtype)
-    for copy in copies:
-        copy.wait()
+    if not first:
+        fetch.wait()
+        total = total + total_buf[...]
+    key_buf[...] = total.astype(key_buf.dtype)
+    stores.append(pltpu.make_async_copy(key_buf, key_ref, sems.at[1]))
+    stores[-1].start()
+    for store in stores:
+        store.wait()
 
 
 def staged_body(grid, normed, kv_cotangent, kv_weight, main_grad, owner_order):
@@ -134,7 +198,7 @@
     f32, bf16 = jnp.float32, jnp.bfloat16
     vmem = pl.BlockSpec(memory_space=pltpu.VMEM)
     smem = pl.BlockSpec(memory_space=pltpu.SMEM)
-    anywhere = pl.BlockSpec(memory_space=pl.ANY)
+    hbm = pl.BlockSpec(memory_space=pltpu.HBM)
 
     def send(value, move):
         pairs = []
@@ -165,54 +229,61 @@
     near, far = range(cut), range(cut, nz)
     red_rows, blue_rows = part * len(near), part * len(far)
 
-    xgot = to_core(flat)
-    cgot = to_core(cot)
-
-    def wgrad(lists, dtype):
+    far_spots = [(k, 1, dx) for dx in (0, 1) for k in near]
+    far_spots += [(k, dy, 1) for dy in (0, 1) for k in far]
+    near_spots = [(k, 0, dx) for dx in (0, 1) for k in near]
+    near_spots += [(k, dy, 0) for dy in (0, 1) for k in far]
+    far_wide, near_wide = part * len(far_spots), part * len(near_spots)
+    shapes = [
+        jax.ShapeDtypeStruct((rows, far_wide + key_width), bf16),
+        jax.ShapeDtypeStruct((rows, near_wide), bf16),
+    ]
+    chunks = 4
+    far_own, near_own, far_partner, near_partner = pl.pallas_call(
+        functools.partial(stage_kernel, grid, [far_spots, near_spots]),
+        in_specs=[smem, hbm, hbm],
+        out_specs=[vmem] * 4,
+        out_shape=shapes * 2,
+        scratch_shapes=[
+            pltpu.VMEM((chunks, rows // chunks, width), bf16),
+            pltpu.SemaphoreType.DMA((chunks,)),
+            pltpu.SemaphoreType.DMA((2,)),
+        ],
+        compiler_params=pltpu.CompilerParams(vmem_limit_bytes=TIGHT_BYTES),
+        name="stage",
+    )(owner_order, flat, cot)
+    far_got = to_core(far_partner)
+    near_got = to_core(near_partner)
+
+    def wgrad(sources, sizes, dtype):
         return pl.pallas_call(
-            functools.partial(wgrad_kernel, grid, lists),
-            in_specs=[smem] + [vmem] * 4,
-            out_specs=[vmem] * len(lists),
-            out_shape=[
-                jax.ShapeDtypeStruct((part * len(s), key_width), dtype) for s in lists
-            ],
+            functools.partial(wgrad_kernel, far_wide, len(sources) > 2),
+            in_specs=[vmem] * len(sources),
+            out_specs=[vmem] * len(sizes),
+            out_shape=[jax.ShapeDtypeStruct((size, key_width), dtype) for size in sizes],
             cost_estimate=pl.CostEstimate(
                 flops=rows * width * key_width,
                 bytes_accessed=4 * rows * width,
                 transcendentals=0,
             ),
             compiler_params=pltpu.CompilerParams(vmem_limit_bytes=24 << 20),
-        )(owner_order, flat, cot, xgot, cgot)
-
-    red_out, blue_out = wgrad(
-        [
-            [(k, 1, dx) for dx in (0, 1) for k in near],
-            [(k, dy, 1) for dy in (0, 1) for k in far],
-        ],
-        bf16,
-    )
-    red_on, blue_on, red_keep, blue_keep = wgrad(
-        [
-            [(k, 0, 1) for k in near],
-            [(k, 1, 0) for k in far],
-            [(k, 0, 0) for k in near],
-            [(k, 0, 0) for k in far],
-        ],
-        f32,
+        )(*sources)
+
+    red_out, blue_out = wgrad([far_own, far_got], [2 * red_rows, 2 * blue_rows], bf16)
+    red_keep, red_on, blue_keep, blue_on = wgrad(
+        [far_own, far_got, near_own, near_got], [red_rows, red_rows, blue_rows, blue_rows], f32
     )
 
     own = lax.dynamic_slice_in_dim(kv_weight, half * part, part, axis=0)
-    line = [own] + [over_z(own, d) for d in range(1, nz)]
+    line = [own] + [over_z(own, -d) for d in range(1, nz)]
     red = jnp.concatenate(line[:cut], axis=0)
     blue = jnp.concatenate(line[cut:], axis=0)
     red = jnp.concatenate([red, over_x(red)], axis=0)
     blue = jnp.concatenate([blue, over_y(blue)], axis=0)
     red_y = over_y(red)
     blue_x = over_x(blue)
-    red_spots = [(-k, 0, dx) for dx in (0, 1) for k in near]
-    blue_spots = [(-k, dy, 0) for dy in (0, 1) for k in far]
-    red_y_spots = [(-k, 1, dx) for dx in (0, 1) for k in near]
-    blue_x_spots = [(-k, dy, 1) for dy in (0, 1) for k in far]
+    red_spots, blue_spots = near_spots[: 2 * len(near)], near_spots[2 * len(near) :]
+    red_y_spots, blue_x_spots = far_spots[: 2 * len(near)], far_spots[2 * len(near) :]
 
     red_in = over_y(red_out)
     blue_in = over_x(blue_out)
@@ -231,29 +302,36 @@
     grad_scale = 1.0 / math.sqrt(rows * owners * replicas)
     kept = lax.dynamic_slice_in_dim(main_grad, half * part, part, axis=0) + total * grad_scale
     there = to_core(kept)
-    grad_buffer = jnp.where(
-        half == 0,
-        jnp.concatenate([kept, there], axis=0),
-        jnp.concatenate([there, kept], axis=0),
-    )
-
-    def apply(pieces, before, last):
+
+    def apply(pieces, columns, before, halves):
         weights = [w for w, _, _ in pieces]
-        inputs = [owner_order, flat, cot, *weights, *before]
-        specs = [smem, vmem, vmem] + [vmem] * len(pieces) + [vmem, anywhere][: len(before)]
+        inputs = [owner_order, cot, *weights, *columns, *before, *halves]
+        specs = [smem] + [vmem] * (1 + len(pieces) + len(columns)) + [hbm, hbm][: len(before)]
+        specs += [vmem] * len(halves)
+        count = sum(len(spots) for _, spots, _ in pieces)
+        wide = max(w.shape[0] for w in weights)
+        key_type = bf16 if halves else f32
+        shapes = [
+            jax.ShapeDtypeStruct((rows, key_width), key_type),
+            jax.ShapeDtypeStruct((rows, width), bf16),
+        ]
+        if halves:
+            shapes.append(jax.ShapeDtypeStruct((shard_rows, key_width), f32))
         return pl.pallas_call(
-            functools.partial(apply_kernel, grid, [p[1:] for p in pieces], not before),
+            functools.partial(
+                apply_kernel, grid, [p[1:] for p in pieces], not before, bool(halves)
+            ),
             in_specs=specs,
-            out_specs=[vmem, anywhere],
-            out_shape=[
-                jax.ShapeDtypeStruct((rows, key_width), bf16 if last else f32),
-                jax.ShapeDtypeStruct((rows, width), bf16),
+            out_specs=[hbm] * len(shapes),
+            out_shape=shapes,
+            scratch_shapes=[
+                pltpu.VMEM((len(pieces), rows, wide), bf16),
+                pltpu.VMEM((rows, key_width), f32),
+                pltpu.VMEM((rows, key_width), key_type),
+                pltpu.SemaphoreType.DMA((count,)),
+                pltpu.SemaphoreType.DMA((4,)),
             ],
-            scratch_shapes=[
-                pltpu.VMEM((len(pieces), rows, max(w.shape[0] for w in weights)), bf16),
-                pltpu.SemaphoreType.DMA((sum(len(p[1]) for p in pieces),)),
-            ],
-            input_output_aliases={len(inputs) - 1: 1} if before else {},
+            input_output_aliases={len(inputs) - 1 - len(halves): 1} if before else {},
             cost_estimate=pl.CostEstimate(
                 flops=4 * rows * key_width * sum(w.shape[0] for w in weights),
                 bytes_accessed=2 * rows * width,
@@ -269,12 +347,16 @@
             (to_core(red), red_spots, True),
             (to_core(blue), blue_spots, True),
         ],
+        [near_own, near_partner],
         (),
-        False,
-    )
-    done = apply([(red_y, red_y_spots, False), (blue_x, blue_x_spots, False)], done, False)
-    key, input_grad = apply(
-        [(to_core(red_y), red_y_spots, True), (to_core(blue_x), blue_x_spots, True)], done, True
+        (),
+    )
+    done = apply([(red_y, red_y_spots, False), (blue_x, blue_x_spots, False)], [far_own], done, ())
+    key, input_grad, grad_buffer = apply(
+        [(to_core(red_y), red_y_spots, True), (to_core(blue_x), blue_x_spots, True)],
+        [far_partner],
+        done,
+        (kept, there),
     )
     return (
         key.reshape(micro_count, tok_dev, key_width),

time: 84.8 us -> 69.7 us (0.82)
  waiting for transfers between devices: 37.5 us -> 24.2 us
  local copies, waits for them, and re-layouts: 5.62 us -> 1.27 us
  starting transfers between devices: 26.2 us -> 30.5 us
  other arithmetic: 2.4 us -> 0.53 us
    ppermute x21, waiting for transfers between devices: 37.5 us -> 24.2 us  [send(): return lax.ppermute(value, ('fsdp', 'dp'), pairs)]
    ppermute x21, starting transfers between devices: 26.2 us -> 30.5 us  [send(): return lax.ppermute(value, ('fsdp', 'dp'), pairs)]
    unnamed x18 -> x20, local copies, waits for them, and re-layouts: 4.85 us -> 1.2 us
    pallas_call x2 -> x3, Pallas kernels: 2.65 us -> 5.55 us  [the longest x1 4.07 us: staged_body(): pl.pallas_call(functools.partial(stage_kernel, grid, [far_spots, near_spo...]
    pallas_call x3, Pallas kernels: 9.25 us -> 6.55 us  [apply(): pl.pallas_call(functools.partial(apply_kernel, grid, [p[1:] for p in piec...]
    select_n x1 -> x0, other arithmetic: 1.89 us -> none  [staged_body(): jnp.where(half == 0, jnp.concatenate([kept, there], axis=0), jnp.concaten...]
  transfers between devices with their start and end apart: 21 -> 21, of which waited for: 6 -> 8; matrix products, arithmetic and copies ran while one was open for 3% -> 1% of each run, Pallas kernels for 14% -> 8%
where the time goes in v1:
time: 69.7 us; the launch traced here: 69.5 us
  starting transfers between devices  30.5 us (44%)
  waiting for transfers between devices  24.2 us (35%)
  Pallas kernels  12.1 us (17%)
  local copies, waits for them, and re-layouts  1.27 us (2%)
  between operations  0.94 us (1%)
    ppermute x21, starting transfers between devices, send(): return lax.ppermute(value, ('fsdp', 'dp'), pairs)  30.5 us
    ppermute x21, waiting for transfers between devices, send(): return lax.ppermute(value, ('fsdp', 'dp'), pairs)  24.2 us
    pallas_call x3, Pallas kernels, apply(): pl.pallas_call(functools.partial(apply_kernel, grid, [p[1:] for p in piec...  6.55 us
    pallas_call x1, Pallas kernels, staged_body(): pl.pallas_call(functools.partial(stage_kernel, grid, [far_spots, near_spo...  4.07 us
    pallas_call x2, Pallas kernels, wgrad(): pl.pallas_call(functools.partial(wgrad_kernel, far_wide, len(sources) > 2...  1.48 us
  transfers between devices with their start and end apart: 21, of which 8 were waited for; matrix products, arithmetic and copies ran while one was open for 1% of the time, Pallas kernels for 8%

profile of v1, /device:TPU:0, one launch (start us, length us, event | category | flops | bytes accessed | tf_op | source)
XLA Modules:
  0.0 69.5 jit_solution(5239727104742300343)
XLA Ops:
  0.6 0.0 copy-start
  0.6 4.1 %stage.1 = (bf16[256,1536]{1,0:T(8,128)(2,1)}, bf16[256,1024]{1,0:T(8,128)(2,1)}, bf16[256,1536]{1,0:T(8,128)(2,1)}, bf16[256,1024]{1,0:T(8,128)(2,1)}) custom-call(s32[16]{0:T(128)} %order_ref.7, bf16[256,4096]{1,0:T(8,128)(2,1)} %bitcast.9, bf16[256,512]{1,0:T(8,128)(2,1)} %bitcast.4), custom_call_target="tpu_custom_call" | custom-call | tf_op jit(solution)/shard_map/stage/pallas_call | solution.py:242
  4.7 0.6 collective-permute-start.11
  5.3 0.0 copy-done
  5.3 3.7 %collective-permute-start.4 = (bf16[128,512]{1,0:T(8,128)(2,1)S(1)}, bf16[128,512]{1,0:T(8,128)(2,1)S(1)}, u32[]{:S(2)}, u32[]{:S(2)}) collective-permute-start(bf16[128,512]{1,0:T(8,128)(2,1)S(1)} %constant_dynamic-slice_fusion), channel_id=1, source_target_pairs={{0,16},{1,17},{2,18},{3,19},{4,20},{5,21},{6,22},{7,23},{8,24},{9,... | collective-permute-start | bytes 393224 | tf_op jit(solution)/shard_map/ppermute | solution.py:212
  9.0 1.6 %collective-permute-start.5 = (bf16[128,512]{1,0:T(8,128)(2,1)S(1)}, bf16[128,512]{1,0:T(8,128)(2,1)S(1)}, u32[]{:S(2)}, u32[]{:S(2)}) collective-permute-start(bf16[128,512]{1,0:T(8,128)(2,1)S(1)} %constant_dynamic-slice_fusion), channel_id=1, source_target_pairs={{0,8},{1,9},{2,10},{3,11},{4,12},{5,13},{6,14},{7,15},{8,16},{9,17... | collective-permute-start | bytes 393224 | tf_op jit(solution)/shard_map/ppermute | solution.py:212
  10.6 2.2 %collective-permute-start = (bf16[128,512]{1,0:T(8,128)(2,1)S(1)}, bf16[128,512]{1,0:T(8,128)(2,1)S(1)}, u32[]{:S(2)}, u32[]{:S(2)}) collective-permute-start(bf16[128,512]{1,0:T(8,128)(2,1)S(1)} %constant_dynamic-slice_fusion), channel_id=1, source_target_pairs={{0,24},{1,25},{2,26},{3,27},{4,28},{5,29},{6,30},{7,31},{8,0},{9,1... | collective-permute-start | bytes 393224 | tf_op jit(solution)/shard_map/ppermute | solution.py:212
  12.8 0.0 collective-permute-start.12
  12.8 0.0 collective-permute-done.11.refs_1_
  12.8 1.1 %copy-done.1 = bf16[256,1536]{1,0:T(8,128)(2,1)S(1)} copy-done((bf16[256,1536]{1,0:T(8,128)(2,1)S(1)}, bf16[256,1536]{1,0:T(8,128)(2,1)}, u32[]{:S(2)}) %copy-start.1) | copy-done | bytes 786456
  13.9 0.7 %shard_map.79 = (bf16[512,512]{1,0:T(8,128)(2,1)S(1)}, bf16[512,512]{1,0:T(8,128)(2,1)S(1)}) custom-call(bf16[256,1536]{1,0:T(8,128)(2,1)S(1)} %copy-done.1, bf16[256,1536]{1,0:T(8,128)(2,1)S(1)} %collective-permute-done.11.refs_1_), custom_call_target="tpu_custom_call" | custom-call | flops 536870912 | bytes 4194304 | tf_op jit(solution)/shard_map/pallas_call | solution.py:259
  14.7 1.6 %collective-permute-start.16 = (bf16[512,512]{1,0:T(8,128)(2,1)S(1)}, bf16[512,512]{1,0:T(8,128)(2,1)S(1)}, u32[]{:S(2)}, u32[]{:S(2)}) collective-permute-start(bf16[512,512]{1,0:T(8,128)(2,1)S(1)} %get-tuple-element.32), channel_id=1, source_target_pairs={{0,2},{1,3},{2,0},{3,1},{4,6},{5,7},{6,4},{7,5},{8,10},{9,11},{10,... | collective-permute-start | bytes 1572872 | tf_op jit(solution)/shard_map/ppermute | solution.py:212
  16.2 2.7 %collective-permute-done.4 = bf16[128,512]{1,0:T(8,128)(2,1)S(1)} collective-permute-done((bf16[128,512]{1,0:T(8,128)(2,1)S(1)}, bf16[128,512]{1,0:T(8,128)(2,1)S(1)}, u32[]{:S(2)}, u32[]{:S(2)}) %collective-permute-start.4) | collective-permute-done | bytes 131104 | tf_op jit(solution)/shard_map/ppermute | solution.py:212
  19.0 0.0 collective-permute-done.5
  19.0 1.9 %collective-permute-start.6 = (bf16[256,512]{1,0:T(8,128)(2,1)S(1)}, bf16[256,512]{1,0:T(8,128)(2,1)S(1)}, u32[]{:S(2)}, u32[]{:S(2)}) collective-permute-start(bf16[256,512]{1,0:T(8,128)(2,1)S(1)} %pad_maximum_fusion.2), channel_id=1, source_target_pairs={{0,4},{1,5},{2,6},{3,7},{4,0},{5,1},{6,2},{7,3},{8,12},{9,13},{10,... | collective-permute-start | bytes 786440 | tf_op jit(solution)/shard_map/ppermute | solution.py:212
  20.9 0.0 collective-permute-done
  21.0 1.6 %collective-permute-start.1 = (bf16[256,512]{1,0:T(8,128)(2,1)S(1)}, bf16[256,512]{1,0:T(8,128)(2,1)S(1)}, u32[]{:S(2)}, u32[]{:S(2)}) collective-permute-start(bf16[256,512]{1,0:T(8,128)(2,1)S(1)} %pad_maximum_fusion.1), channel_id=1, source_target_pairs={{0,2},{1,3},{2,0},{3,1},{4,6},{5,7},{6,4},{7,5},{8,10},{9,11},{10,... | collective-permute-start | bytes 786440 | tf_op jit(solution)/shard_map/ppermute | solution.py:212
  22.5 1.0 %collective-permute-start.13 = (bf16[512,512]{1,0:T(8,128)(2,1)S(1)}, bf16[512,512]{1,0:T(8,128)(2,1)S(1)}, u32[]{:S(2)}, u32[]{:S(2)}) collective-permute-start(bf16[512,512]{1,0:T(8,128)(2,1)S(1)} %get-tuple-element.29), channel_id=1, source_target_pairs={{0,4},{1,5},{2,6},{3,7},{4,0},{5,1},{6,2},{7,3},{8,12},{9,13},{10,... | collective-permute-start | bytes 1572872 | tf_op jit(solution)/shard_map/ppermute | solution.py:212
  23.6 4.7 %collective-permute-done.6 = bf16[256,512]{1,0:T(8,128)(2,1)S(1)} collective-permute-done((bf16[256,512]{1,0:T(8,128)(2,1)S(1)}, bf16[256,512]{1,0:T(8,128)(2,1)S(1)}, u32[]{:S(2)}, u32[]{:S(2)}) %collective-permute-start.6) | collective-permute-done | bytes 262176 | tf_op jit(solution)/shard_map/ppermute | solution.py:212
  28.3 0.1 collective-permute-start.10
  28.4 0.0 collective-permute-done.12.refs_3_
  28.4 1.9 %collective-permute-start.7 = (bf16[512,512]{1,0:T(8,128)(2,1)S(1)}, bf16[512,512]{1,0:T(8,128)(2,1)S(1)}, u32[]{:S(2)}, u32[]{:S(2)}) collective-permute-start(bf16[512,512]{1,0:T(8,128)(2,1)S(1)} %constant_dynamic-update-slice_fusion.refs_1_), channel_id=1, source_target_pairs={{0,2},{1,3},{2,0},{3,1},{4,6},{5,7},{6,4},{7,5},{8,10},{9,11},{10,... | collective-permute-start | bytes 1572872 | tf_op jit(solution)/shard_map/ppermute | solution.py:212
  30.3 0.0 copy-done.5
  30.3 0.7 %shard_map.78 = (f32[256,512]{1,0:T(8,128)S(1)}, f32[256,512]{1,0:T(8,128)S(1)}, f32[256,512]{1,0:T(8,128)S(1)}, f32[256,512]{1,0:T(8,128)S(1)}) custom-call(bf16[256,1536]{1,0:T(8,128)(2,1)S(1)} %copy-done.1, bf16[256,1536]{1,0:T(8,128)(2,1)S(1)} %collective-permute-done.11.refs_1_, bf16[256,1024]{1,0:T(8,128)(2,1)S(1)} %copy-done.5, ...), custom_call_target="tpu_custom_call" | custom-call | flops 536870912 | bytes 4194304 | tf_op jit(solution)/shard_map/pallas_call | solution.py:259
  31.0 0.0 collective-permute-done.16
  31.0 0.1 add_convert_fusion.1
  31.1 1.6 %collective-permute-start.17 = (bf16[256,512]{1,0:T(8,128)(2,1)S(1)}, bf16[256,512]{1,0:T(8,128)(2,1)S(1)}, u32[]{:S(2)}, u32[]{:S(2)}) collective-permute-start(bf16[256,512]{1,0:T(8,128)(2,1)S(1)} %add_convert_fusion.1), channel_id=1, source_target_pairs={{0,4},{1,5},{2,6},{3,7},{4,0},{5,1},{6,2},{7,3},{8,12},{9,13},{10,... | collective-permute-start | bytes 786440 | tf_op jit(solution)/shard_map/ppermute | solution.py:212
  32.7 2.5 %collective-permute-done.1 = bf16[256,512]{1,0:T(8,128)(2,1)S(1)} collective-permute-done((bf16[256,512]{1,0:T(8,128)(2,1)S(1)}, bf16[256,512]{1,0:T(8,128)(2,1)S(1)}, u32[]{:S(2)}, u32[]{:S(2)}) %collective-permute-start.1) | collective-permute-done | bytes 262176 | tf_op jit(solution)/shard_map/ppermute | solution.py:212
  35.2 0.1 collective-permute-start.9
  35.3 4.2 %collective-permute-done.13 = bf16[512,512]{1,0:T(8,128)(2,1)S(1)} collective-permute-done((bf16[512,512]{1,0:T(8,128)(2,1)S(1)}, bf16[512,512]{1,0:T(8,128)(2,1)S(1)}, u32[]{:S(2)}, u32[]{:S(2)}) %collective-permute-start.13) | collective-permute-done | bytes 524320 | tf_op jit(solution)/shard_map/ppermute | solution.py:212
  39.5 1.8 %collective-permute-start.2 = (bf16[512,512]{1,0:T(8,128)(2,1)S(1)}, bf16[512,512]{1,0:T(8,128)(2,1)S(1)}, u32[]{:S(2)}, u32[]{:S(2)}) collective-permute-start(bf16[512,512]{1,0:T(8,128)(2,1)S(1)} %pad_maximum_fusion.refs_0_), channel_id=1, source_target_pairs={{0,4},{1,5},{2,6},{3,7},{4,0},{5,1},{6,2},{7,3},{8,12},{9,13},{10,... | collective-permute-start | bytes 1572872 | tf_op jit(solution)/shard_map/ppermute | solution.py:212
  41.3 0.1 add_convert_fusion.2
  41.4 0.0 copy-start.8
  41.4 3.7 %collective-permute-done.17 = bf16[256,512]{1,0:T(8,128)(2,1)S(1)} collective-permute-done((bf16[256,512]{1,0:T(8,128)(2,1)S(1)}, bf16[256,512]{1,0:T(8,128)(2,1)S(1)}, u32[]{:S(2)}, u32[]{:S(2)}) %collective-permute-start.17) | collective-permute-done | bytes 262176 | tf_op jit(solution)/shard_map/ppermute | solution.py:212
  45.1 1.8 %collective-permute-start.14 = (bf16[256,512]{1,0:T(8,128)(2,1)S(1)}, bf16[256,512]{1,0:T(8,128)(2,1)S(1)}, u32[]{:S(2)}, u32[]{:S(2)}) collective-permute-start(bf16[256,512]{1,0:T(8,128)(2,1)S(1)} %add_convert_fusion.2), channel_id=1, source_target_pairs={{0,2},{1,3},{2,0},{3,1},{4,6},{5,7},{6,4},{7,5},{8,10},{9,11},{10,... | collective-permute-start | bytes 786440 | tf_op jit(solution)/shard_map/ppermute | solution.py:212
  46.9 0.1 add_convert_fusion
  47.1 0.0 copy-start.3
  47.1 0.0 copy-start.6
  47.1 0.0 copy-start.7
  47.1 0.0 collective-permute-done.7.refs_1_
  47.1 4.9 %collective-permute-start.18 = (bf16[128,512]{1,0:T(8,128)(2,1)S(1)}, bf16[128,512]{1,0:T(8,128)(2,1)S(1)}, u32[]{:S(2)}, u32[]{:S(2)}) collective-permute-start(bf16[128,512]{1,0:T(8,128)(2,1)S(1)} %get-tuple-element.37), channel_id=1, source_target_pairs={{0,16},{1,17},{2,18},{3,19},{4,20},{5,21},{6,22},{7,23},{8,24},{9,... | collective-permute-start | bytes 393224 | tf_op jit(solution)/shard_map/ppermute | solution.py:212
  52.0 0.0 collective-permute-done.14
  52.0 0.5 collective-permute-start.19
  52.5 0.1 convert_add_fusion
  52.6 2.4 %collective-permute-done.2.refs_0_ = bf16[512,512]{1,0:T(8,128)(2,1)S(1)} collective-permute-done((bf16[512,512]{1,0:T(8,128)(2,1)S(1)}, bf16[512,512]{1,0:T(8,128)(2,1)S(1)}, u32[]{:S(2)}, u32[]{:S(2)}) %collective-permute-start.2) | collective-permute-done | bytes 524320 | tf_op jit(solution)/shard_map/ppermute | solution.py:212
  55.0 3.7 %collective-permute-start.15 = (bf16[128,512]{1,0:T(8,128)(2,1)S(1)}, bf16[128,512]{1,0:T(8,128)(2,1)S(1)}, u32[]{:S(2)}, u32[]{:S(2)}) collective-permute-start(bf16[128,512]{1,0:T(8,128)(2,1)S(1)} %slice.57), channel_id=1, source_target_pairs={{0,8},{1,9},{2,10},{3,11},{4,12},{5,13},{6,14},{7,15},{8,16},{9,17... | collective-permute-start | bytes 393224 | tf_op jit(solution)/shard_map/ppermute | solution.py:212
  58.7 0.0 collective-permute-done.18
  58.7 0.0 collective-permute-start.8
  58.7 1.1 %collective-permute-done.19 = bf16[128,512]{1,0:T(8,128)(2,1)S(1)} collective-permute-done((bf16[128,512]{1,0:T(8,128)(2,1)S(1)}, bf16[128,512]{1,0:T(8,128)(2,1)S(1)}, u32[]{:S(2)}, u32[]{:S(2)}) %collective-permute-start.19) | collective-permute-done | bytes 131104 | tf_op jit(solution)/shard_map/ppermute | solution.py:212
  59.8 0.0 collective-permute-start.3
  59.8 2.8 %collective-permute-done.15 = bf16[128,512]{1,0:T(8,128)(2,1)S(1)} collective-permute-done((bf16[128,512]{1,0:T(8,128)(2,1)S(1)}, bf16[128,512]{1,0:T(8,128)(2,1)S(1)}, u32[]{:S(2)}, u32[]{:S(2)}) %collective-permute-start.15) | collective-permute-done | bytes 131104 | tf_op jit(solution)/shard_map/ppermute | solution.py:212
  62.6 0.0 copy-done.8
  62.6 0.1 fusion.3.refs_5_
  62.7 0.0 copy-start.2
  62.7 0.1 collective-permute-start.20
  62.8 0.0 collective-permute-done.10.refs_3_
  62.8 0.0 collective-permute-done.9.refs_2_
  62.8 2.5 %shard_map.76 = (f32[256,512]{1,0:T(8,128)S(1)}, bf16[256,4096]{1,0:T(8,128)(2,1)}) custom-call(s32[16]{0:T(128)S(1)} %copy-done.6, bf16[256,512]{1,0:T(8,128)(2,1)S(1)} %bitcast.5, bf16[512,512]{1,0:T(8,128)(2,1)S(1)} %pad_maximum_fusion.refs_0_, bf16[512,512]{1,0:T(8,128)(2,1)S(1)} %constant_dynamic-update-slice_fusion.refs_1_, ...), custom_call_target="tpu_custom_call" | custom-call | flops 1073741824 | bytes 2097152 | tf_op jit(solution)/shard_map/pallas_call | solution.py:320
  65.3 1.9 %shard_map.77 = (f32[256,512]{1,0:T(8,128)S(1)}, bf16[256,4096]{1,0:T(8,128)(2,1)}) custom-call(s32[16]{0:T(128)S(1)} %copy-done.6, bf16[256,512]{1,0:T(8,128)(2,1)S(1)} %bitcast.6, bf16[512,512]{1,0:T(8,128)(2,1)S(1)} %collective-permute-done.2.refs_0_, bf16[512,512]{1,0:T(8,128)(2,1)S(1)} %collective-permute-done.7.refs_1_, ...), custom_call_target="tpu_custom_call", output_to_operand_aliasing={{1}: (6, {})} | custom-call | flops 536870912 | bytes 2097152 | tf_op jit(solution)/shard_map/pallas_call | solution.py:320
  67.3 0.0 collective-permute-done.8.refs_1_
  67.3 0.0 collective-permute-done.3.refs_0_
  67.3 0.0 collective-permute-done.20.refs_6_
  67.3 0.0 copy-done.4
  67.3 2.2 %shard_map.80 = (bf16[256,512]{1,0:T(8,128)(2,1)}, bf16[256,4096]{1,0:T(8,128)(2,1)}, f32[256,512]{1,0:T(8,128)}) custom-call(s32[16]{0:T(128)S(1)} %copy-done.6, bf16[256,512]{1,0:T(8,128)(2,1)S(1)} %bitcast.7, bf16[512,512]{1,0:T(8,128)(2,1)S(1)} %collective-permute-done.3.refs_0_, ...), custom_call_target="tpu_custom_call", output_to_operand_aliasing={{1}: (6, {})} | custom-call | flops 536870912 | bytes 2097152 | tf_op jit(solution)/shard_map/pallas_call | solution.py:320
  (16 shorter events, 0.2 us)
Async XLA Ops:
  0.6 4.7 %copy-start = (bf16[256,512]{1,0:T(8,128)(2,1)S(1)}, bf16[256,512]{1,0:T(8,128)(2,1)}, u32[]{:S(2)}) copy-start(bf16[256,512]{1,0:T(8,128)(2,1)} %param.7) | copy-start | bytes 786436
  4.7 8.1 %collective-permute-start.11 = (bf16[256,1536]{1,0:T(8,128)(2,1)}, bf16[256,1536]{1,0:T(8,128)(2,1)S(1)}, u32[]{:S(2)}, u32[]{:S(2)}) collective-permute-start(bf16[256,1536]{1,0:T(8,128)(2,1)} %get-tuple-element.20.refs_2_), channel_id=1, source_target_pairs={{0,1},{1,0},{2,3},{3,2},{4,5},{5,4},{6,7},{7,6},{8,9},{9,8},{10,11... | collective-permute-start | bytes 2359304 | tf_op jit(solution)/shard_map/ppermute | solution.py:212
  5.3 13.7 %collective-permute-start.4 = (bf16[128,512]{1,0:T(8,128)(2,1)S(1)}, bf16[128,512]{1,0:T(8,128)(2,1)S(1)}, u32[]{:S(2)}, u32[]{:S(2)}) collective-permute-start(bf16[128,512]{1,0:T(8,128)(2,1)S(1)} %constant_dynamic-slice_fusion), channel_id=1, source_target_pairs={{0,16},{1,17},{2,18},{3,19},{4,20},{5,21},{6,22},{7,23},{8,24},{9,... | collective-permute-start | bytes 393224 | tf_op jit(solution)/shard_map/ppermute | solution.py:212
  9.0 10.0 %collective-permute-start.5 = (bf16[128,512]{1,0:T(8,128)(2,1)S(1)}, bf16[128,512]{1,0:T(8,128)(2,1)S(1)}, u32[]{:S(2)}, u32[]{:S(2)}) collective-permute-start(bf16[128,512]{1,0:T(8,128)(2,1)S(1)} %constant_dynamic-slice_fusion), channel_id=1, source_target_pairs={{0,8},{1,9},{2,10},{3,11},{4,12},{5,13},{6,14},{7,15},{8,16},{9,17... | collective-permute-start | bytes 393224 | tf_op jit(solution)/shard_map/ppermute | solution.py:212
  10.6 10.4 %collective-permute-start = (bf16[128,512]{1,0:T(8,128)(2,1)S(1)}, bf16[128,512]{1,0:T(8,128)(2,1)S(1)}, u32[]{:S(2)}, u32[]{:S(2)}) collective-permute-start(bf16[128,512]{1,0:T(8,128)(2,1)S(1)} %constant_dynamic-slice_fusion), channel_id=1, source_target_pairs={{0,24},{1,25},{2,26},{3,27},{4,28},{5,29},{6,30},{7,31},{8,0},{9,1... | collective-permute-start | bytes 393224 | tf_op jit(solution)/shard_map/ppermute | solution.py:212
  12.8 15.6 %collective-permute-start.12 = (bf16[256,1024]{1,0:T(8,128)(2,1)}, bf16[256,1024]{1,0:T(8,128)(2,1)S(1)}, u32[]{:S(2)}, u32[]{:S(2)}) collective-permute-start(bf16[256,1024]{1,0:T(8,128)(2,1)} %get-tuple-element.23.refs_5_), channel_id=1, source_target_pairs={{0,1},{1,0},{2,3},{3,2},{4,5},{5,4},{6,7},{7,6},{8,9},{9,8},{10,11... | collective-permute-start | bytes 1572872 | tf_op jit(solution)/shard_map/ppermute | solution.py:212
  12.8 1.1 %copy-start.1 = (bf16[256,1536]{1,0:T(8,128)(2,1)S(1)}, bf16[256,1536]{1,0:T(8,128)(2,1)}, u32[]{:S(2)}) copy-start(bf16[256,1536]{1,0:T(8,128)(2,1)} %get-tuple-element.21.refs_2_.refs_0_) | copy-start | bytes 2359300
  13.9 16.3 %copy-start.5 = (bf16[256,1024]{1,0:T(8,128)(2,1)S(1)}, bf16[256,1024]{1,0:T(8,128)(2,1)}, u32[]{:S(2)}) copy-start(bf16[256,1024]{1,0:T(8,128)(2,1)} %get-tuple-element.22.refs_4_.refs_2_) | copy-start | bytes 1572868
  14.7 16.3 %collective-permute-start.16 = (bf16[512,512]{1,0:T(8,128)(2,1)S(1)}, bf16[512,512]{1,0:T(8,128)(2,1)S(1)}, u32[]{:S(2)}, u32[]{:S(2)}) collective-permute-start(bf16[512,512]{1,0:T(8,128)(2,1)S(1)} %get-tuple-element.32), channel_id=1, source_target_pairs={{0,2},{1,3},{2,0},{3,1},{4,6},{5,7},{6,4},{7,5},{8,10},{9,11},{10,... | collective-permute-start | bytes 1572872 | tf_op jit(solution)/shard_map/ppermute | solution.py:212
  19.0 9.2 %collective-permute-start.6 = (bf16[256,512]{1,0:T(8,128)(2,1)S(1)}, bf16[256,512]{1,0:T(8,128)(2,1)S(1)}, u32[]{:S(2)}, u32[]{:S(2)}) collective-permute-start(bf16[256,512]{1,0:T(8,128)(2,1)S(1)} %pad_maximum_fusion.2), channel_id=1, source_target_pairs={{0,4},{1,5},{2,6},{3,7},{4,0},{5,1},{6,2},{7,3},{8,12},{9,13},{10,... | collective-permute-start | bytes 786440 | tf_op jit(solution)/shard_map/ppermute | solution.py:212
  21.0 14.2 %collective-permute-start.1 = (bf16[256,512]{1,0:T(8,128)(2,1)S(1)}, bf16[256,512]{1,0:T(8,128)(2,1)S(1)}, u32[]{:S(2)}, u32[]{:S(2)}) collective-permute-start(bf16[256,512]{1,0:T(8,128)(2,1)S(1)} %pad_maximum_fusion.1), channel_id=1, source_target_pairs={{0,2},{1,3},{2,0},{3,1},{4,6},{5,7},{6,4},{7,5},{8,10},{9,11},{10,... | collective-permute-start | bytes 786440 | tf_op jit(solution)/shard_map/ppermute | solution.py:212
  22.5 16.9 %collective-permute-start.13 = (bf16[512,512]{1,0:T(8,128)(2,1)S(1)}, bf16[512,512]{1,0:T(8,128)(2,1)S(1)}, u32[]{:S(2)}, u32[]{:S(2)}) collective-permute-start(bf16[512,512]{1,0:T(8,128)(2,1)S(1)} %get-tuple-element.29), channel_id=1, source_target_pairs={{0,4},{1,5},{2,6},{3,7},{4,0},{5,1},{6,2},{7,3},{8,12},{9,13},{10,... | collective-permute-start | bytes 1572872 | tf_op jit(solution)/shard_map/ppermute | solution.py:212
  28.3 34.5 %collective-permute-start.10 = (bf16[512,512]{1,0:T(8,128)(2,1)S(1)}, bf16[512,512]{1,0:T(8,128)(2,1)S(1)}, u32[]{:S(2)}, u32[]{:S(2)}) collective-permute-start(bf16[512,512]{1,0:T(8,128)(2,1)S(1)} %constant_dynamic-update-slice_fusion.refs_1_), channel_id=1, source_target_pairs={{0,1},{1,0},{2,3},{3,2},{4,5},{5,4},{6,7},{7,6},{8,9},{9,8},{10,11... | collective-permute-start | bytes 1572872 | tf_op jit(solution)/shard_map/ppermute | solution.py:212
  28.4 18.7 %collective-permute-start.7 = (bf16[512,512]{1,0:T(8,128)(2,1)S(1)}, bf16[512,512]{1,0:T(8,128)(2,1)S(1)}, u32[]{:S(2)}, u32[]{:S(2)}) collective-permute-start(bf16[512,512]{1,0:T(8,128)(2,1)S(1)} %constant_dynamic-update-slice_fusion.refs_1_), channel_id=1, source_target_pairs={{0,2},{1,3},{2,0},{3,1},{4,6},{5,7},{6,4},{7,5},{8,10},{9,11},{10,... | collective-permute-start | bytes 1572872 | tf_op jit(solution)/shard_map/ppermute | solution.py:212
  31.1 14.0 %collective-permute-start.17 = (bf16[256,512]{1,0:T(8,128)(2,1)S(1)}, bf16[256,512]{1,0:T(8,128)(2,1)S(1)}, u32[]{:S(2)}, u32[]{:S(2)}) collective-permute-start(bf16[256,512]{1,0:T(8,128)(2,1)S(1)} %add_convert_fusion.1), channel_id=1, source_target_pairs={{0,4},{1,5},{2,6},{3,7},{4,0},{5,1},{6,2},{7,3},{8,12},{9,13},{10,... | collective-permute-start | bytes 786440 | tf_op jit(solution)/shard_map/ppermute | solution.py:212
  35.2 27.6 %collective-permute-start.9 = (bf16[512,512]{1,0:T(8,128)(2,1)S(1)}, bf16[512,512]{1,0:T(8,128)(2,1)S(1)}, u32[]{:S(2)}, u32[]{:S(2)}) collective-permute-start(bf16[512,512]{1,0:T(8,128)(2,1)S(1)} %pad_maximum_fusion.refs_0_), channel_id=1, source_target_pairs={{0,1},{1,0},{2,3},{3,2},{4,5},{5,4},{6,7},{7,6},{8,9},{9,8},{10,11... | collective-permute-start | bytes 1572872 | tf_op jit(solution)/shard_map/ppermute | solution.py:212
  39.5 15.5 %collective-permute-start.2 = (bf16[512,512]{1,0:T(8,128)(2,1)S(1)}, bf16[512,512]{1,0:T(8,128)(2,1)S(1)}, u32[]{:S(2)}, u32[]{:S(2)}) collective-permute-start(bf16[512,512]{1,0:T(8,128)(2,1)S(1)} %pad_maximum_fusion.refs_0_), channel_id=1, source_target_pairs={{0,4},{1,5},{2,6},{3,7},{4,0},{5,1},{6,2},{7,3},{8,12},{9,13},{10,... | collective-permute-start | bytes 1572872 | tf_op jit(solution)/shard_map/ppermute | solution.py:212
  41.4 21.2 %copy-start.8 = (f32[256,512]{1,0:T(8,128)S(1)}, f32[256,512]{1,0:T(8,128)}, u32[]{:S(2)}) copy-start(f32[256,512]{1,0:T(8,128)} %param.8) | copy-start | bytes 1572868
  45.1 6.9 %collective-permute-start.14 = (bf16[256,512]{1,0:T(8,128)(2,1)S(1)}, bf16[256,512]{1,0:T(8,128)(2,1)S(1)}, u32[]{:S(2)}, u32[]{:S(2)}) collective-permute-start(bf16[256,512]{1,0:T(8,128)(2,1)S(1)} %add_convert_fusion.2), channel_id=1, source_target_pairs={{0,2},{1,3},{2,0},{3,1},{4,6},{5,7},{6,4},{7,5},{8,10},{9,11},{10,... | collective-permute-start | bytes 786440 | tf_op jit(solution)/shard_map/ppermute | solution.py:212
  47.1 15.8 %copy-start.3 = (bf16[2,128,512]{2,1,0:T(8,128)(2,1)S(1)}, bf16[2,128,512]{2,1,0:T(8,128)(2,1)}, u32[]{:S(2)}) copy-start(bf16[2,128,512]{2,1,0:T(8,128)(2,1)} %param.6) | copy-start | bytes 786436
  47.1 15.8 %copy-start.6 = (s32[16]{0:T(128)S(1)}, s32[16]{0:T(128)}, u32[]{:S(2)}) copy-start(s32[16]{0:T(128)} %order_ref.7) | copy-start | bytes 196
  47.1 15.8 %copy-start.7 = (bf16[256,1024]{1,0:T(8,128)(2,1)S(1)}, bf16[256,1024]{1,0:T(8,128)(2,1)}, u32[]{:S(2)}) copy-start(bf16[256,1024]{1,0:T(8,128)(2,1)} %get-tuple-element.23.refs_5_) | copy-start | bytes 1572868
  47.1 11.6 %collective-permute-start.18 = (bf16[128,512]{1,0:T(8,128)(2,1)S(1)}, bf16[128,512]{1,0:T(8,128)(2,1)S(1)}, u32[]{:S(2)}, u32[]{:S(2)}) collective-permute-start(bf16[128,512]{1,0:T(8,128)(2,1)S(1)} %get-tuple-element.37), channel_id=1, source_target_pairs={{0,16},{1,17},{2,18},{3,19},{4,20},{5,21},{6,22},{7,23},{8,24},{9,... | collective-permute-start | bytes 393224 | tf_op jit(solution)/shard_map/ppermute | solution.py:212
  52.0 7.7 %collective-permute-start.19 = (bf16[128,512]{1,0:T(8,128)(2,1)S(1)}, bf16[128,512]{1,0:T(8,128)(2,1)S(1)}, u32[]{:S(2)}, u32[]{:S(2)}) collective-permute-start(bf16[128,512]{1,0:T(8,128)(2,1)S(1)} %get-tuple-element.38), channel_id=1, source_target_pairs={{0,24},{1,25},{2,26},{3,27},{4,28},{5,29},{6,30},{7,31},{8,0},{9,1... | collective-permute-start | bytes 393224 | tf_op jit(solution)/shard_map/ppermute | solution.py:212
  55.0 7.6 %collective-permute-start.15 = (bf16[128,512]{1,0:T(8,128)(2,1)S(1)}, bf16[128,512]{1,0:T(8,128)(2,1)S(1)}, u32[]{:S(2)}, u32[]{:S(2)}) collective-permute-start(bf16[128,512]{1,0:T(8,128)(2,1)S(1)} %slice.57), channel_id=1, source_target_pairs={{0,8},{1,9},{2,10},{3,11},{4,12},{5,13},{6,14},{7,15},{8,16},{9,17... | collective-permute-start | bytes 393224 | tf_op jit(solution)/shard_map/ppermute | solution.py:212
  58.7 8.5 %collective-permute-start.8 = (bf16[512,512]{1,0:T(8,128)(2,1)S(1)}, bf16[512,512]{1,0:T(8,128)(2,1)S(1)}, u32[]{:S(2)}, u32[]{:S(2)}) collective-permute-start(bf16[512,512]{1,0:T(8,128)(2,1)S(1)} %collective-permute-done.7.refs_1_), channel_id=1, source_target_pairs={{0,1},{1,0},{2,3},{3,2},{4,5},{5,4},{6,7},{7,6},{8,9},{9,8},{10,11... | collective-permute-start | bytes 1572872 | tf_op jit(solution)/shard_map/ppermute | solution.py:212
  59.8 7.5 %collective-permute-start.3 = (bf16[512,512]{1,0:T(8,128)(2,1)S(1)}, bf16[512,512]{1,0:T(8,128)(2,1)S(1)}, u32[]{:S(2)}, u32[]{:S(2)}) collective-permute-start(bf16[512,512]{1,0:T(8,128)(2,1)S(1)} %collective-permute-done.2.refs_0_), channel_id=1, source_target_pairs={{0,1},{1,0},{2,3},{3,2},{4,5},{5,4},{6,7},{7,6},{8,9},{9,8},{10,11... | collective-permute-start | bytes 1572872 | tf_op jit(solution)/shard_map/ppermute | solution.py:212
  62.7 2.6 %copy-start.2 = (bf16[256,1536]{1,0:T(8,128)(2,1)S(1)}, bf16[256,1536]{1,0:T(8,128)(2,1)}, u32[]{:S(2)}) copy-start(bf16[256,1536]{1,0:T(8,128)(2,1)} %get-tuple-element.21.refs_2_.refs_0_) | copy-start | bytes 2359300
  62.7 4.6 %collective-permute-start.20 = (f32[128,512]{1,0:T(8,128)S(1)}, f32[128,512]{1,0:T(8,128)S(1)}, u32[]{:S(2)}, u32[]{:S(2)}) collective-permute-start(f32[128,512]{1,0:T(8,128)S(1)} %fusion.3.refs_5_), channel_id=1, source_target_pairs={{0,1},{1,0},{2,3},{3,2},{4,5},{5,4},{6,7},{7,6},{8,9},{9,8},{10,11... | collective-permute-start | bytes 786440 | tf_op jit(solution)/shard_map/ppermute | solution.py:212
  65.3 1.9 %copy-start.4 = (bf16[256,1536]{1,0:T(8,128)(2,1)S(1)}, bf16[256,1536]{1,0:T(8,128)(2,1)}, u32[]{:S(2)}) copy-start(bf16[256,1536]{1,0:T(8,128)(2,1)} %get-tuple-element.20.refs_2_) | copy-start | bytes 2359300

commit v2 on v1

--- a/solution.py
+++ b/solution.py
@@ -10,7 +10,7 @@
 
 
 LANES = 128
-TIGHT_BYTES = 62 << 20
+TIGHT_BYTES = (62 << 20) + (16 << 10)
 
 
 def plain_body(normed, kv_cotangent, kv_weight, main_grad, owner_order):
@@ -63,54 +63,58 @@
     return tuple(sizes)
 
 
+def partner_of(at, step, size):
+    return at ^ step if size & (size - 1) == 0 else (at + step) % size
+
+
 def owner_at(grid, spot):
     nz, ny, nx = grid
+    dz, dy, dx = spot
     me = lax.axis_index("fsdp")
     z, y, x = me // (ny * nx), me // nx % ny, me % nx
-    dz, dy, dx = spot
-    return (((z + dz) % nz) * ny + (y + dy) % ny) * nx + (x + dx) % nx
-
-
-def stage_kernel(grid, lists, order_ref, x_ref, cot_ref, *refs):
-    outs, (buf, x_sems, cot_sems) = refs[: 2 * len(lists)], refs[2 * len(lists) :]
+    z, y, x = partner_of(z, dz, nz), partner_of(y, dy, ny), partner_of(x, dx, nx)
+    return (z * ny + y) * nx + x
+
+
+def stage_kernel(grid, lists, order_hbm, x_ref, *refs):
+    refs = list(refs)
+    cot_ref = refs.pop(0) if len(refs) == 5 + 2 * len(lists) else None
+    outs, (buf, order_ref, x_sems, sems) = refs[:-4], refs[-4:]
     chunks, step, _ = buf.shape
     half = lax.axis_index("dp") % 2
     loads = []
     for c in range(chunks):
-        rows = pl.ds(c * step, step)
-        loads.append(pltpu.make_async_copy(x_ref.at[rows], buf.at[c], x_sems.at[c]))
+        loads.append(
+            pltpu.make_async_copy(x_ref.at[pl.ds(c * step, step)], buf.at[c], x_sems.at[c])
+        )
         loads[-1].start()
+    fetch = pltpu.make_async_copy(order_hbm, order_ref, sems.at[0])
+    fetch.start()
     stores = []
-    for side in range(2):
-        to_ref = outs[side * len(lists)]
-        to = to_ref.at[:, len(lists[0]) * LANES :]
-        stores.append(pltpu.make_async_copy(cot_ref, to, cot_sems.at[side]))
-        stores[-1].start()
-    starts = []
-    for spots in lists:
-        cols = [order_ref[owner_at(grid, spot)] for spot in spots]
-        starts.append(cols)
+    if cot_ref is not None:
+        for k, to_ref in enumerate(outs[:2]):
+            to = to_ref.at[:, len(lists[0]) * LANES :]
+            stores.append(pltpu.make_async_copy(cot_ref, to, sems.at[1 + k]))
+            stores[-1].start()
+    fetch.wait()
+    cols = [[order_ref[owner_at(grid, spot)] for spot in spots] for spots in lists]
     for c in range(chunks):
         loads[c].wait()
         rows = slice(c * step, (c + 1) * step)
-        for side in range(2):
-            which = half if side == 0 else 1 - half
-            for cols, to_ref in zip(starts, outs[side * len(lists) :]):
-                for k, col in enumerate(cols):
-                    at = pl.ds(pl.multiple_of((2 * col + which) * LANES, LANES), LANES)
-                    to_ref[rows, k * LANES : (k + 1) * LANES] = buf[c, :, at]
+        for i, to_ref in enumerate(outs):
+            side = half if i % 2 == 0 else 1 - half
+            for k, col in enumerate(cols[i // 2]):
+                at = pl.ds(pl.multiple_of((2 * col + side) * LANES, LANES), LANES)
+                to_ref[rows, k * LANES : (k + 1) * LANES] = buf[c, :, at]
     for store in stores:
         store.wait()
 
 
-def wgrad_kernel(cot_at, keep, *refs):
-    first, refs = refs[:2], refs[2:]
-    cot = jnp.concatenate([r[:, cot_at:] for r in first], axis=0)
-    sources = first
-    if keep:
-        sources, refs = refs[:2], refs[2:]
+def wgrad_kernel(cot_at, *refs):
+    sources, outs = refs[:2], refs[2:]
+    cot = jnp.concatenate([r[:, cot_at:] for r in sources], axis=0)
     begin = 0
-    for out in refs:
+    for out in outs:
         at = slice(begin, begin + out.shape[0])
         out[...] = lax.dot_general(
             jnp.concatenate([r[:, at] for r in sources], axis=0),
@@ -212,52 +216,59 @@
         return lax.ppermute(value, ("fsdp", "dp"), pairs)
 
     def over_x(value):
-        return send(value, lambda z, y, x, r: (z, y, x + 1, r))
+        return send(value, lambda z, y, x, r: (z, y, partner_of(x, 1, nx), r))
 
     def over_y(value):
-        return send(value, lambda z, y, x, r: (z, y + 1, x, r))
-
-    def over_z(value, far):
-        return send(value, lambda z, y, x, r: (z + far, y, x, r))
+        return send(value, lambda z, y, x, r: (z, partner_of(y, 1, ny), x, r))
+
+    def over_z(value, step):
+        return send(value, lambda z, y, x, r: (partner_of(z, step, nz), y, x, r))
 
     def to_core(value):
         return send(value, lambda z, y, x, r: (z, y, x, r ^ 1))
 
     flat = normed.reshape(rows, width)
     cot = kv_cotangent.reshape(rows, key_width)
-    cut = nz // 2
-    near, far = range(cut), range(cut, nz)
+    doubling = [nz >> k for k in range(1, nz.bit_length())]
+    near = [0]
+    for d in doubling[:-1]:
+        near = near + [d + k for k in near]
+    far = [1 + k for k in near]
     red_rows, blue_rows = part * len(near), part * len(far)
 
     far_spots = [(k, 1, dx) for dx in (0, 1) for k in near]
     far_spots += [(k, dy, 1) for dy in (0, 1) for k in far]
     near_spots = [(k, 0, dx) for dx in (0, 1) for k in near]
     near_spots += [(k, dy, 0) for dy in (0, 1) for k in far]
-    far_wide, near_wide = part * len(far_spots), part * len(near_spots)
-    shapes = [
-        jax.ShapeDtypeStruct((rows, far_wide + key_width), bf16),
-        jax.ShapeDtypeStruct((rows, near_wide), bf16),
-    ]
     chunks = 4
-    far_own, near_own, far_partner, near_partner = pl.pallas_call(
-        functools.partial(stage_kernel, grid, [far_spots, near_spots]),
-        in_specs=[smem, hbm, hbm],
-        out_specs=[vmem] * 4,
-        out_shape=shapes * 2,
-        scratch_shapes=[
-            pltpu.VMEM((chunks, rows // chunks, width), bf16),
-            pltpu.SemaphoreType.DMA((chunks,)),
-            pltpu.SemaphoreType.DMA((2,)),
-        ],
-        compiler_params=pltpu.CompilerParams(vmem_limit_bytes=TIGHT_BYTES),
-        name="stage",
-    )(owner_order, flat, cot)
-    far_got = to_core(far_partner)
+
+    def stage(lists, extra, limit):
+        shapes = []
+        for spots in lists:
+            wide = part * len(spots) + (extra[0].shape[1] if extra and spots is lists[0] else 0)
+            shapes += [jax.ShapeDtypeStruct((rows, wide), bf16)] * 2
+        return pl.pallas_call(
+            functools.partial(stage_kernel, grid, lists),
+            in_specs=[hbm] * (2 + len(extra)),
+            out_specs=[vmem] * len(shapes),
+            out_shape=shapes,
+            scratch_shapes=[
+                pltpu.VMEM((chunks, rows // chunks, width), bf16),
+                pltpu.SMEM(owner_order.shape, jnp.int32),
+                pltpu.SemaphoreType.DMA((chunks,)),
+                pltpu.SemaphoreType.DMA((3,)),
+            ],
+            compiler_params=pltpu.CompilerParams(vmem_limit_bytes=limit),
+        )(owner_order, flat, *extra)
+
+    first_own, first_partner = stage([far_spots], [cot], TIGHT_BYTES)
+    first_got = to_core(first_partner)
+    near_own, near_partner, far_own, far_partner = stage([near_spots, far_spots], [cot], 8 << 20)
     near_got = to_core(near_partner)
 
     def wgrad(sources, sizes, dtype):
         return pl.pallas_call(
-            functools.partial(wgrad_kernel, far_wide, len(sources) > 2),
+            functools.partial(wgrad_kernel, sources[0].shape[1] - key_width),
             in_specs=[vmem] * len(sources),
             out_specs=[vmem] * len(sizes),
             out_shape=[jax.ShapeDtypeStruct((size, key_width), dtype) for size in sizes],
@@ -269,15 +280,16 @@
             compiler_params=pltpu.CompilerParams(vmem_limit_bytes=24 << 20),
         )(*sources)
 
-    red_out, blue_out = wgrad([far_own, far_got], [2 * red_rows, 2 * blue_rows], bf16)
+    red_out, blue_out = wgrad([first_own, first_got], [2 * red_rows, 2 * blue_rows], bf16)
     red_keep, red_on, blue_keep, blue_on = wgrad(
-        [far_own, far_got, near_own, near_got], [red_rows, red_rows, blue_rows, blue_rows], f32
+        [near_own, near_got], [red_rows, red_rows, blue_rows, blue_rows], f32
     )
 
     own = lax.dynamic_slice_in_dim(kv_weight, half * part, part, axis=0)
-    line = [own] + [over_z(own, -d) for d in range(1, nz)]
-    red = jnp.concatenate(line[:cut], axis=0)
-    blue = jnp.concatenate(line[cut:], axis=0)
+    red = own
+    for d in doubling[:-1]:
+        red = jnp.concatenate([red, over_z(red, d)], axis=0)
+    blue = over_z(red, 1)
     red = jnp.concatenate([red, over_x(red)], axis=0)
     blue = jnp.concatenate([blue, over_y(blue)], axis=0)
     red_y = over_y(red)
@@ -291,8 +303,10 @@
     blue_far = (blue_on + blue_in[blue_rows:]).astype(bf16)
     red_sum = red_keep + red_in[:red_rows] + over_x(red_far)
     blue_sum = blue_keep + blue_in[:blue_rows] + over_y(blue_far)
-    along = [red_sum[k * part : (k + 1) * part] for k in range(len(near))]
-    along += [blue_sum[k * part : (k + 1) * part] for k in range(len(far))]
+    along = {}
+    for places, sums in ((near, red_sum), (far, blue_sum)):
+        for at, k in enumerate(places):
+            along[k] = sums[at * part : (at + 1) * part]
     total = along[0]
     for d in range(1, nz):
         total = total + over_z(along[d].astype(bf16), d)
@@ -376,6 +390,7 @@
     out_specs = (P(None, ("fsdp", "dp"), None), P(None, ("fsdp", "dp"), None), P("fsdp", None))
     grid = grid_of(mesh)
     staged = grid is not None and len(grid) == 3 and grid[1:] == (2, 2)
+    staged = staged and grid[0] & (grid[0] - 1) == 0 and grid[0] > 2
     staged = staged and mesh.shape["dp"] % 2 == 0
 
     def body(normed, kv_cotangent, kv_weight, main_grad, owner_order):

time: 69.7 us -> 101 us (1.45)
  waiting for transfers between devices: 24.2 us -> 60.5 us
  starting transfers between devices: 30.5 us -> 20 us
  Pallas kernels: 12.1 us -> 16.2 us
  local copies, waits for them, and re-layouts: 1.27 us -> 2.84 us
    ppermute x21 -> x20, waiting for transfers between devices: 24.2 us -> 60.5 us  [send(): return lax.ppermute(value, ('fsdp', 'dp'), pairs)]
    ppermute x21 -> x20, starting transfers between devices: 30.5 us -> 20 us  [send(): return lax.ppermute(value, ('fsdp', 'dp'), pairs)]
    pallas_call x3 -> x4, Pallas kernels: 5.55 us -> 8.93 us  [the longest x2 5.2 us: stage(): pl.pallas_call(functools.partial(stage_kernel, grid, lists), in_specs=[hb...]
    unnamed x20 -> x13, local copies, waits for them, and re-layouts: 1.2 us -> 2.77 us
  transfers between devices with their start and end apart: 21 -> 20, of which waited for: 8 -> 9; matrix products, arithmetic and copies ran while one was open for 1% -> 1% of each run, Pallas kernels for 8% -> 11%
where the time goes in v2:
time: 101 us
  waiting for transfers between devices  60.5 us (60%)
  starting transfers between devices  20 us (20%)
  Pallas kernels  16.2 us (16%)
  local copies, waits for them, and re-layouts  2.84 us (3%)
    ppermute x20, waiting for transfers between devices, send(): return lax.ppermute(value, ('fsdp', 'dp'), pairs)  60.5 us
    ppermute x20, starting transfers between devices, send(): return lax.ppermute(value, ('fsdp', 'dp'), pairs)  20 us
    pallas_call x3, Pallas kernels, apply(): pl.pallas_call(functools.partial(apply_kernel, grid, [p[1:] for p in piec...  7.25 us
    pallas_call x2, Pallas kernels, stage(): pl.pallas_call(functools.partial(stage_kernel, grid, lists), in_specs=[hb...  5.2 us
    pallas_call x2, Pallas kernels, wgrad(): pl.pallas_call(functools.partial(wgrad_kernel, sources[0].shape[1] - key_...  3.73 us
    unnamed x13, local copies, waits for them, and re-layouts  2.77 us
  transfers between devices with their start and end apart: 20, of which 9 were waited for; matrix products, arithmetic and copies ran while one was open for 1% of the time, Pallas kernels for 11%

profile of v2, /device:TPU:0, one launch (start us, length us, event | category | flops | bytes accessed | tf_op | source)
XLA Modules:
  0.0 101.0 jit_solution(9631544360058141781)
XLA Ops:
  0.6 0.0 copy-start
  0.6 0.0 copy-start.2
  0.7 0.0 copy-start.3
  0.7 3.0 %shard_map.80 = (bf16[256,1536]{1,0:T(8,128)(2,1)}, bf16[256,1536]{1,0:T(8,128)(2,1)}) custom-call(s32[16]{0:T(128)} %order_ref.5, bf16[256,4096]{1,0:T(8,128)(2,1)} %bitcast.4, bf16[256,512]{1,0:T(8,128)(2,1)} %bitcast.6), custom_call_target="tpu_custom_call" | custom-call | tf_op jit(solution)/shard_map/pallas_call | solution.py:250
  3.6 0.6 collective-permute-start.11
  4.2 0.0 copy-done.2
  4.2 0.0 copy-done.3
  4.2 0.0 copy-start.1
  4.2 1.6 %copy-done.1 = bf16[2,128,4096]{2,1,0:T(8,128)(2,1)S(1)} copy-done((bf16[2,128,4096]{2,1,0:T(8,128)(2,1)S(1)}, bf16[2,128,4096]{2,1,0:T(8,128)(2,1)}, u32[]{:S(2)}) %copy-start.1) | copy-done | bytes 2097176
  5.8 2.2 %shard_map.76 = (bf16[256,1536]{1,0:T(8,128)(2,1)S(1)}, bf16[256,1536]{1,0:T(8,128)(2,1)}, bf16[256,1024]{1,0:T(8,128)(2,1)S(1)}, bf16[256,1024]{1,0:T(8,128)(2,1)S(1)}) custom-call(s32[16]{0:T(128)S(1)} %copy-done.3, bf16[256,4096]{1,0:T(8,128)(2,1)S(1)} %bitcast.5, bf16[256,512]{1,0:T(8,128)(2,1)S(1)} %bitcast.7), custom_call_target="tpu_custom_call" | custom-call | tf_op jit(solution)/shard_map/pallas_call | solution.py:250
  8.0 0.1 collective-permute-start.10
  8.1 0.0 copy-done
  8.2 4.1 %collective-permute-start = (bf16[128,512]{1,0:T(8,128)(2,1)S(1)}, bf16[128,512]{1,0:T(8,128)(2,1)S(1)}, u32[]{:S(2)}, u32[]{:S(2)}) collective-permute-start(bf16[128,512]{1,0:T(8,128)(2,1)S(1)} %constant_dynamic-slice_fusion), channel_id=1, source_target_pairs={{0,16},{1,17},{2,18},{3,19},{4,20},{5,21},{6,22},{7,23},{8,24},{9,... | collective-permute-start | bytes 393224 | tf_op jit(solution)/shard_map/ppermute | solution.py:216
  12.3 6.5 %collective-permute-done = bf16[128,512]{1,0:T(8,128)(2,1)S(1)} collective-permute-done((bf16[128,512]{1,0:T(8,128)(2,1)S(1)}, bf16[128,512]{1,0:T(8,128)(2,1)S(1)}, u32[]{:S(2)}, u32[]{:S(2)}) %collective-permute-start) | collective-permute-done | bytes 131104 | tf_op jit(solution)/shard_map/ppermute | solution.py:216
  18.8 1.6 %collective-permute-start.1 = (bf16[256,512]{1,0:T(8,128)(2,1)S(1)}, bf16[256,512]{1,0:T(8,128)(2,1)S(1)}, u32[]{:S(2)}, u32[]{:S(2)}) collective-permute-start(bf16[256,512]{1,0:T(8,128)(2,1)S(1)} %pad_maximum_fusion.1), channel_id=1, source_target_pairs={{0,2},{1,3},{2,0},{3,1},{4,6},{5,7},{6,4},{7,5},{8,10},{9,11},{10,... | collective-permute-start | bytes 786440 | tf_op jit(solution)/shard_map/ppermute | solution.py:216
  20.4 0.0 collective-permute-done.11.refs_1_
  20.4 0.0 copy-start.4
  20.4 1.1 %copy-done.4 = bf16[256,1536]{1,0:T(8,128)(2,1)S(1)} copy-done((bf16[256,1536]{1,0:T(8,128)(2,1)S(1)}, bf16[256,1536]{1,0:T(8,128)(2,1)}, u32[]{:S(2)}) %copy-start.4) | copy-done | bytes 786456
  21.6 1.9 %shard_map.81 = (bf16[512,512]{1,0:T(8,128)(2,1)S(1)}, bf16[512,512]{1,0:T(8,128)(2,1)S(1)}) custom-call(bf16[256,1536]{1,0:T(8,128)(2,1)S(1)} %copy-done.4, bf16[256,1536]{1,0:T(8,128)(2,1)} %collective-permute-done.11.refs_1_), custom_call_target="tpu_custom_call" | custom-call | flops 536870912 | bytes 4194304 | tf_op jit(solution)/shard_map/pallas_call | solution.py:270
  23.4 0.5 collective-permute-start.14
  24.0 0.7 collective-permute-start.4
  24.7 3.4 %collective-permute-done.1 = bf16[256,512]{1,0:T(8,128)(2,1)S(1)} collective-permute-done((bf16[256,512]{1,0:T(8,128)(2,1)S(1)}, bf16[256,512]{1,0:T(8,128)(2,1)S(1)}, u32[]{:S(2)}, u32[]{:S(2)}) %collective-permute-start.1) | collective-permute-done | bytes 262176 | tf_op jit(solution)/shard_map/ppermute | solution.py:216
  28.1 0.1 collective-permute-start.8
  28.2 1.2 %collective-permute-start.2 = (bf16[512,512]{1,0:T(8,128)(2,1)S(1)}, bf16[512,512]{1,0:T(8,128)(2,1)S(1)}, u32[]{:S(2)}, u32[]{:S(2)}) collective-permute-start(bf16[512,512]{1,0:T(8,128)(2,1)S(1)} %pad_maximum_fusion.refs_0_), channel_id=1, source_target_pairs={{0,4},{1,5},{2,6},{3,7},{4,0},{5,1},{6,2},{7,3},{8,12},{9,13},{10,... | collective-permute-start | bytes 1572872 | tf_op jit(solution)/shard_map/ppermute | solution.py:216
  29.3 1.7 %collective-permute-done.4 = bf16[256,512]{1,0:T(8,128)(2,1)S(1)} collective-permute-done((bf16[256,512]{1,0:T(8,128)(2,1)S(1)}, bf16[256,512]{1,0:T(8,128)(2,1)S(1)}, u32[]{:S(2)}, u32[]{:S(2)}) %collective-permute-start.4) | collective-permute-done | bytes 262176 | tf_op jit(solution)/shard_map/ppermute | solution.py:216
  31.1 1.3 %collective-permute-start.12 = (bf16[512,512]{1,0:T(8,128)(2,1)S(1)}, bf16[512,512]{1,0:T(8,128)(2,1)S(1)}, u32[]{:S(2)}, u32[]{:S(2)}) collective-permute-start(bf16[512,512]{1,0:T(8,128)(2,1)S(1)} %get-tuple-element.33), channel_id=1, source_target_pairs={{0,4},{1,5},{2,6},{3,7},{4,0},{5,1},{6,2},{7,3},{8,12},{9,13},{10,... | collective-permute-start | bytes 1572872 | tf_op jit(solution)/shard_map/ppermute | solution.py:216
  32.4 0.0 collective-permute-done.10.refs_1_
  32.4 0.8 collective-permute-start.5
  33.2 1.9 %shard_map.79 = (f32[256,512]{1,0:T(8,128)S(1)}, f32[256,512]{1,0:T(8,128)S(1)}, f32[256,512]{1,0:T(8,128)S(1)}, f32[256,512]{1,0:T(8,128)S(1)}) custom-call(bf16[256,1536]{1,0:T(8,128)(2,1)S(1)} %get-tuple-element.24.refs_4_.refs_0_, bf16[256,1536]{1,0:T(8,128)(2,1)} %collective-permute-done.10.refs_1_), custom_call_target="tpu_custom_call" | custom-call | flops 536870912 | bytes 4194304 | tf_op jit(solution)/shard_map/pallas_call | solution.py:270
  35.1 2.7 %collective-permute-done.14 = bf16[512,512]{1,0:T(8,128)(2,1)S(1)} collective-permute-done((bf16[512,512]{1,0:T(8,128)(2,1)S(1)}, bf16[512,512]{1,0:T(8,128)(2,1)S(1)}, u32[]{:S(2)}, u32[]{:S(2)}) %collective-permute-start.14) | collective-permute-done | bytes 524320 | tf_op jit(solution)/shard_map/ppermute | solution.py:216
  37.8 0.1 add_convert_fusion.1
  37.9 1.4 %collective-permute-start.15 = (bf16[256,512]{1,0:T(8,128)(2,1)S(1)}, bf16[256,512]{1,0:T(8,128)(2,1)S(1)}, u32[]{:S(2)}, u32[]{:S(2)}) collective-permute-start(bf16[256,512]{1,0:T(8,128)(2,1)S(1)} %add_convert_fusion.1), channel_id=1, source_target_pairs={{0,4},{1,5},{2,6},{3,7},{4,0},{5,1},{6,2},{7,3},{8,12},{9,13},{10,... | collective-permute-start | bytes 786440 | tf_op jit(solution)/shard_map/ppermute | solution.py:216
  39.2 20.7 %collective-permute-done.5 = bf16[256,512]{1,0:T(8,128)(2,1)S(1)} collective-permute-done((bf16[256,512]{1,0:T(8,128)(2,1)S(1)}, bf16[256,512]{1,0:T(8,128)(2,1)S(1)}, u32[]{:S(2)}, u32[]{:S(2)}) %collective-permute-start.5) | collective-permute-done | bytes 262176 | tf_op jit(solution)/shard_map/ppermute | solution.py:216
  59.9 0.1 collective-permute-start.9
  60.0 0.0 collective-permute-done.12
  60.0 1.6 %collective-permute-start.6 = (bf16[512,512]{1,0:T(8,128)(2,1)S(1)}, bf16[512,512]{1,0:T(8,128)(2,1)S(1)}, u32[]{:S(2)}, u32[]{:S(2)}) collective-permute-start(bf16[512,512]{1,0:T(8,128)(2,1)S(1)} %constant_dynamic-update-slice_fusion.refs_1_), channel_id=1, source_target_pairs={{0,2},{1,3},{2,0},{3,1},{4,6},{5,7},{6,4},{7,5},{8,10},{9,11},{10,... | collective-permute-start | bytes 1572872 | tf_op jit(solution)/shard_map/ppermute | solution.py:216
  61.6 0.1 add_convert_fusion.2
  61.7 0.0 copy-start.5
  61.7 3.3 %collective-permute-done.15 = bf16[256,512]{1,0:T(8,128)(2,1)S(1)} collective-permute-done((bf16[256,512]{1,0:T(8,128)(2,1)S(1)}, bf16[256,512]{1,0:T(8,128)(2,1)S(1)}, u32[]{:S(2)}, u32[]{:S(2)}) %collective-permute-start.15) | collective-permute-done | bytes 262176 | tf_op jit(solution)/shard_map/ppermute | solution.py:216
  65.0 1.5 %collective-permute-start.13 = (bf16[256,512]{1,0:T(8,128)(2,1)S(1)}, bf16[256,512]{1,0:T(8,128)(2,1)S(1)}, u32[]{:S(2)}, u32[]{:S(2)}) collective-permute-start(bf16[256,512]{1,0:T(8,128)(2,1)S(1)} %add_convert_fusion.2), channel_id=1, source_target_pairs={{0,2},{1,3},{2,0},{3,1},{4,6},{5,7},{6,4},{7,5},{8,10},{9,11},{10,... | collective-permute-start | bytes 786440 | tf_op jit(solution)/shard_map/ppermute | solution.py:216
  66.5 0.1 add_convert_fusion
  66.6 0.0 collective-permute-done.2.refs_0_
  66.7 0.7 collective-permute-start.16
  67.4 12.5 %collective-permute-done.13 = bf16[256,512]{1,0:T(8,128)(2,1)S(1)} collective-permute-done((bf16[256,512]{1,0:T(8,128)(2,1)S(1)}, bf16[256,512]{1,0:T(8,128)(2,1)S(1)}, u32[]{:S(2)}, u32[]{:S(2)}) %collective-permute-start.13) | collective-permute-done | bytes 262176 | tf_op jit(solution)/shard_map/ppermute | solution.py:216
  79.9 3.5 %collective-permute-start.18 = (bf16[128,512]{1,0:T(8,128)(2,1)S(1)}, bf16[128,512]{1,0:T(8,128)(2,1)S(1)}, u32[]{:S(2)}, u32[]{:S(2)}) collective-permute-start(bf16[128,512]{1,0:T(8,128)(2,1)S(1)} %get-tuple-element.42), channel_id=1, source_target_pairs={{0,24},{1,25},{2,26},{3,27},{4,28},{5,29},{6,30},{7,31},{8,16},{9,... | collective-permute-start | bytes 393224 | tf_op jit(solution)/shard_map/ppermute | solution.py:216
  83.5 0.1 convert_add_fusion
  83.6 0.0 collective-permute-done.6.refs_1_
  83.6 0.1 collective-permute-start.17
  83.7 0.0 collective-permute-done.16
  83.7 0.1 collective-permute-start.3
  83.8 4.4 %collective-permute-done.18 = bf16[128,512]{1,0:T(8,128)(2,1)S(1)} collective-permute-done((bf16[128,512]{1,0:T(8,128)(2,1)S(1)}, bf16[128,512]{1,0:T(8,128)(2,1)S(1)}, u32[]{:S(2)}, u32[]{:S(2)}) %collective-permute-start.18) | collective-permute-done | bytes 131104 | tf_op jit(solution)/shard_map/ppermute | solution.py:216
  88.2 0.0 collective-permute-start.7
  88.2 5.3 %collective-permute-done.17 = bf16[128,512]{1,0:T(8,128)(2,1)S(1)} collective-permute-done((bf16[128,512]{1,0:T(8,128)(2,1)S(1)}, bf16[128,512]{1,0:T(8,128)(2,1)S(1)}, u32[]{:S(2)}, u32[]{:S(2)}) %collective-permute-start.17) | collective-permute-done | bytes 131104 | tf_op jit(solution)/shard_map/ppermute | solution.py:216
  93.5 0.0 copy-done.5
  93.5 0.1 fusion.3.refs_5_
  93.6 0.1 collective-permute-start.19
  93.7 0.0 collective-permute-done.8.refs_2_
  93.7 0.0 collective-permute-done.9.refs_3_
  93.7 3.1 %shard_map.77 = (f32[256,512]{1,0:T(8,128)S(1)}, bf16[256,4096]{1,0:T(8,128)(2,1)}) custom-call(s32[16]{0:T(128)S(1)} %copy-done.3, bf16[256,512]{1,0:T(8,128)(2,1)S(1)} %bitcast.8, bf16[512,512]{1,0:T(8,128)(2,1)S(1)} %pad_maximum_fusion.refs_0_, bf16[512,512]{1,0:T(8,128)(2,1)S(1)} %constant_dynamic-update-slice_fusion.refs_1_, ...), custom_call_target="tpu_custom_call" | custom-call | flops 1073741824 | bytes 2097152 | tf_op jit(solution)/shard_map/pallas_call | solution.py:334
  96.8 1.9 %shard_map.78 = (f32[256,512]{1,0:T(8,128)S(1)}, bf16[256,4096]{1,0:T(8,128)(2,1)}) custom-call(s32[16]{0:T(128)S(1)} %copy-done.3, bf16[256,512]{1,0:T(8,128)(2,1)S(1)} %bitcast.9, bf16[512,512]{1,0:T(8,128)(2,1)S(1)} %collective-permute-done.2.refs_0_, bf16[512,512]{1,0:T(8,128)(2,1)S(1)} %collective-permute-done.6.refs_1_, ...), custom_call_target="tpu_custom_call", output_to_operand_aliasing={{1}: (6, {})} | custom-call | flops 536870912 | bytes 2097152 | tf_op jit(solution)/shard_map/pallas_call | solution.py:334
  98.7 0.0 collective-permute-done.3.refs_0_
  98.7 0.0 collective-permute-done.7.refs_1_
  98.7 0.0 collective-permute-done.19.refs_6_
  98.8 2.2 %shard_map.82 = (bf16[256,512]{1,0:T(8,128)(2,1)}, bf16[256,4096]{1,0:T(8,128)(2,1)}, f32[256,512]{1,0:T(8,128)}) custom-call(s32[16]{0:T(128)S(1)} %copy-done.3, bf16[256,512]{1,0:T(8,128)(2,1)S(1)} %bitcast.10, bf16[512,512]{1,0:T(8,128)(2,1)S(1)} %collective-permute-done.3.refs_0_, ...), custom_call_target="tpu_custom_call", output_to_operand_aliasing={{1}: (6, {})} | custom-call | flops 536870912 | bytes 2097152 | tf_op jit(solution)/shard_map/pallas_call | solution.py:334
  (7 shorter events, 0.1 us)
Async XLA Ops:
  0.6 7.5 %copy-start = (bf16[256,512]{1,0:T(8,128)(2,1)S(1)}, bf16[256,512]{1,0:T(8,128)(2,1)}, u32[]{:S(2)}) copy-start(bf16[256,512]{1,0:T(8,128)(2,1)} %param.7) | copy-start | bytes 786436
  0.6 3.6 %copy-start.2 = (bf16[2,128,512]{2,1,0:T(8,128)(2,1)S(1)}, bf16[2,128,512]{2,1,0:T(8,128)(2,1)}, u32[]{:S(2)}) copy-start(bf16[2,128,512]{2,1,0:T(8,128)(2,1)} %param.6) | copy-start | bytes 786436
  0.7 3.5 %copy-start.3 = (s32[16]{0:T(128)S(1)}, s32[16]{0:T(128)}, u32[]{:S(2)}) copy-start(s32[16]{0:T(128)} %order_ref.5) | copy-start | bytes 196
  3.6 16.8 %collective-permute-start.11 = (bf16[256,1536]{1,0:T(8,128)(2,1)}, bf16[256,1536]{1,0:T(8,128)(2,1)}, u32[]{:S(2)}, u32[]{:S(2)}) collective-permute-start(bf16[256,1536]{1,0:T(8,128)(2,1)} %get-tuple-element.32), channel_id=1, source_target_pairs={{0,1},{1,0},{2,3},{3,2},{4,5},{5,4},{6,7},{7,6},{8,9},{9,8},{10,11... | collective-permute-start | bytes 2359304 | tf_op jit(solution)/shard_map/ppermute | solution.py:216
  4.2 1.6 %copy-start.1 = (bf16[2,128,4096]{2,1,0:T(8,128)(2,1)S(1)}, bf16[2,128,4096]{2,1,0:T(8,128)(2,1)}, u32[]{:S(2)}) copy-start(bf16[2,128,4096]{2,1,0:T(8,128)(2,1)} %param.5) | copy-start | bytes 6291460
  8.0 24.4 %collective-permute-start.10 = (bf16[256,1536]{1,0:T(8,128)(2,1)}, bf16[256,1536]{1,0:T(8,128)(2,1)}, u32[]{:S(2)}, u32[]{:S(2)}) collective-permute-start(bf16[256,1536]{1,0:T(8,128)(2,1)} %get-tuple-element.25.refs_5_), channel_id=1, source_target_pairs={{0,1},{1,0},{2,3},{3,2},{4,5},{5,4},{6,7},{7,6},{8,9},{9,8},{10,11... | collective-permute-start | bytes 2359304 | tf_op jit(solution)/shard_map/ppermute | solution.py:216
  8.2 10.6 %collective-permute-start = (bf16[128,512]{1,0:T(8,128)(2,1)S(1)}, bf16[128,512]{1,0:T(8,128)(2,1)S(1)}, u32[]{:S(2)}, u32[]{:S(2)}) collective-permute-start(bf16[128,512]{1,0:T(8,128)(2,1)S(1)} %constant_dynamic-slice_fusion), channel_id=1, source_target_pairs={{0,16},{1,17},{2,18},{3,19},{4,20},{5,21},{6,22},{7,23},{8,24},{9,... | collective-permute-start | bytes 393224 | tf_op jit(solution)/shard_map/ppermute | solution.py:216
  18.8 9.2 %collective-permute-start.1 = (bf16[256,512]{1,0:T(8,128)(2,1)S(1)}, bf16[256,512]{1,0:T(8,128)(2,1)S(1)}, u32[]{:S(2)}, u32[]{:S(2)}) collective-permute-start(bf16[256,512]{1,0:T(8,128)(2,1)S(1)} %pad_maximum_fusion.1), channel_id=1, source_target_pairs={{0,2},{1,3},{2,0},{3,1},{4,6},{5,7},{6,4},{7,5},{8,10},{9,11},{10,... | collective-permute-start | bytes 786440 | tf_op jit(solution)/shard_map/ppermute | solution.py:216
  20.4 1.1 %copy-start.4 = (bf16[256,1536]{1,0:T(8,128)(2,1)S(1)}, bf16[256,1536]{1,0:T(8,128)(2,1)}, u32[]{:S(2)}) copy-start(bf16[256,1536]{1,0:T(8,128)(2,1)} %get-tuple-element.31.refs_0_) | copy-start | bytes 2359300
  23.4 14.4 %collective-permute-start.14 = (bf16[512,512]{1,0:T(8,128)(2,1)S(1)}, bf16[512,512]{1,0:T(8,128)(2,1)S(1)}, u32[]{:S(2)}, u32[]{:S(2)}) collective-permute-start(bf16[512,512]{1,0:T(8,128)(2,1)S(1)} %get-tuple-element.36), channel_id=1, source_target_pairs={{0,2},{1,3},{2,0},{3,1},{4,6},{5,7},{6,4},{7,5},{8,10},{9,11},{10,... | collective-permute-start | bytes 1572872 | tf_op jit(solution)/shard_map/ppermute | solution.py:216
  24.0 7.1 %collective-permute-start.4 = (bf16[256,512]{1,0:T(8,128)(2,1)S(1)}, bf16[256,512]{1,0:T(8,128)(2,1)S(1)}, u32[]{:S(2)}, u32[]{:S(2)}) collective-permute-start(bf16[256,512]{1,0:T(8,128)(2,1)S(1)} %pad_maximum_fusion.1), channel_id=1, source_target_pairs={{0,8},{1,9},{2,10},{3,11},{4,12},{5,13},{6,14},{7,15},{8,0},{9,1},... | collective-permute-start | bytes 786440 | tf_op jit(solution)/shard_map/ppermute | solution.py:216
  28.1 65.6 %collective-permute-start.8 = (bf16[512,512]{1,0:T(8,128)(2,1)S(1)}, bf16[512,512]{1,0:T(8,128)(2,1)S(1)}, u32[]{:S(2)}, u32[]{:S(2)}) collective-permute-start(bf16[512,512]{1,0:T(8,128)(2,1)S(1)} %pad_maximum_fusion.refs_0_), channel_id=1, source_target_pairs={{0,1},{1,0},{2,3},{3,2},{4,5},{5,4},{6,7},{7,6},{8,9},{9,8},{10,11... | collective-permute-start | bytes 1572872 | tf_op jit(solution)/shard_map/ppermute | solution.py:216
  28.2 38.5 %collective-permute-start.2 = (bf16[512,512]{1,0:T(8,128)(2,1)S(1)}, bf16[512,512]{1,0:T(8,128)(2,1)S(1)}, u32[]{:S(2)}, u32[]{:S(2)}) collective-permute-start(bf16[512,512]{1,0:T(8,128)(2,1)S(1)} %pad_maximum_fusion.refs_0_), channel_id=1, source_target_pairs={{0,4},{1,5},{2,6},{3,7},{4,0},{5,1},{6,2},{7,3},{8,12},{9,13},{10,... | collective-permute-start | bytes 1572872 | tf_op jit(solution)/shard_map/ppermute | solution.py:216
  31.1 28.9 %collective-permute-start.12 = (bf16[512,512]{1,0:T(8,128)(2,1)S(1)}, bf16[512,512]{1,0:T(8,128)(2,1)S(1)}, u32[]{:S(2)}, u32[]{:S(2)}) collective-permute-start(bf16[512,512]{1,0:T(8,128)(2,1)S(1)} %get-tuple-element.33), channel_id=1, source_target_pairs={{0,4},{1,5},{2,6},{3,7},{4,0},{5,1},{6,2},{7,3},{8,12},{9,13},{10,... | collective-permute-start | bytes 1572872 | tf_op jit(solution)/shard_map/ppermute | solution.py:216
  32.4 27.5 %collective-permute-start.5 = (bf16[256,512]{1,0:T(8,128)(2,1)S(1)}, bf16[256,512]{1,0:T(8,128)(2,1)S(1)}, u32[]{:S(2)}, u32[]{:S(2)}) collective-permute-start(bf16[256,512]{1,0:T(8,128)(2,1)S(1)} %collective-permute-done.4), channel_id=1, source_target_pairs={{0,4},{1,5},{2,6},{3,7},{4,0},{5,1},{6,2},{7,3},{8,12},{9,13},{10,... | collective-permute-start | bytes 786440 | tf_op jit(solution)/shard_map/ppermute | solution.py:216
  37.9 27.1 %collective-permute-start.15 = (bf16[256,512]{1,0:T(8,128)(2,1)S(1)}, bf16[256,512]{1,0:T(8,128)(2,1)S(1)}, u32[]{:S(2)}, u32[]{:S(2)}) collective-permute-start(bf16[256,512]{1,0:T(8,128)(2,1)S(1)} %add_convert_fusion.1), channel_id=1, source_target_pairs={{0,4},{1,5},{2,6},{3,7},{4,0},{5,1},{6,2},{7,3},{8,12},{9,13},{10,... | collective-permute-start | bytes 786440 | tf_op jit(solution)/shard_map/ppermute | solution.py:216
  59.9 33.8 %collective-permute-start.9 = (bf16[512,512]{1,0:T(8,128)(2,1)S(1)}, bf16[512,512]{1,0:T(8,128)(2,1)S(1)}, u32[]{:S(2)}, u32[]{:S(2)}) collective-permute-start(bf16[512,512]{1,0:T(8,128)(2,1)S(1)} %constant_dynamic-update-slice_fusion.refs_1_), channel_id=1, source_target_pairs={{0,1},{1,0},{2,3},{3,2},{4,5},{5,4},{6,7},{7,6},{8,9},{9,8},{10,11... | collective-permute-start | bytes 1572872 | tf_op jit(solution)/shard_map/ppermute | solution.py:216
  60.0 23.6 %collective-permute-start.6 = (bf16[512,512]{1,0:T(8,128)(2,1)S(1)}, bf16[512,512]{1,0:T(8,128)(2,1)S(1)}, u32[]{:S(2)}, u32[]{:S(2)}) collective-permute-start(bf16[512,512]{1,0:T(8,128)(2,1)S(1)} %constant_dynamic-update-slice_fusion.refs_1_), channel_id=1, source_target_pairs={{0,2},{1,3},{2,0},{3,1},{4,6},{5,7},{6,4},{7,5},{8,10},{9,11},{10,... | collective-permute-start | bytes 1572872 | tf_op jit(solution)/shard_map/ppermute | solution.py:216
  61.7 31.8 %copy-start.5 = (f32[256,512]{1,0:T(8,128)S(1)}, f32[256,512]{1,0:T(8,128)}, u32[]{:S(2)}) copy-start(f32[256,512]{1,0:T(8,128)} %param.8) | copy-start | bytes 1572868
  65.0 15.0 %collective-permute-start.13 = (bf16[256,512]{1,0:T(8,128)(2,1)S(1)}, bf16[256,512]{1,0:T(8,128)(2,1)S(1)}, u32[]{:S(2)}, u32[]{:S(2)}) collective-permute-start(bf16[256,512]{1,0:T(8,128)(2,1)S(1)} %add_convert_fusion.2), channel_id=1, source_target_pairs={{0,2},{1,3},{2,0},{3,1},{4,6},{5,7},{6,4},{7,5},{8,10},{9,11},{10,... | collective-permute-start | bytes 786440 | tf_op jit(solution)/shard_map/ppermute | solution.py:216
  66.7 17.0 %collective-permute-start.16 = (bf16[128,512]{1,0:T(8,128)(2,1)S(1)}, bf16[128,512]{1,0:T(8,128)(2,1)S(1)}, u32[]{:S(2)}, u32[]{:S(2)}) collective-permute-start(bf16[128,512]{1,0:T(8,128)(2,1)S(1)} %get-tuple-element.41), channel_id=1, source_target_pairs={{0,8},{1,9},{2,10},{3,11},{4,12},{5,13},{6,14},{7,15},{8,0},{9,1},... | collective-permute-start | bytes 393224 | tf_op jit(solution)/shard_map/ppermute | solution.py:216
  79.9 8.2 %collective-permute-start.18 = (bf16[128,512]{1,0:T(8,128)(2,1)S(1)}, bf16[128,512]{1,0:T(8,128)(2,1)S(1)}, u32[]{:S(2)}, u32[]{:S(2)}) collective-permute-start(bf16[128,512]{1,0:T(8,128)(2,1)S(1)} %get-tuple-element.42), channel_id=1, source_target_pairs={{0,24},{1,25},{2,26},{3,27},{4,28},{5,29},{6,30},{7,31},{8,16},{9,... | collective-permute-start | bytes 393224 | tf_op jit(solution)/shard_map/ppermute | solution.py:216
  83.6 9.9 %collective-permute-start.17 = (bf16[128,512]{1,0:T(8,128)(2,1)S(1)}, bf16[128,512]{1,0:T(8,128)(2,1)S(1)}, u32[]{:S(2)}, u32[]{:S(2)}) collective-permute-start(bf16[128,512]{1,0:T(8,128)(2,1)S(1)} %slice.57), channel_id=1, source_target_pairs={{0,16},{1,17},{2,18},{3,19},{4,20},{5,21},{6,22},{7,23},{8,24},{9,... | collective-permute-start | bytes 393224 | tf_op jit(solution)/shard_map/ppermute | solution.py:216
  83.7 15.0 %collective-permute-start.3 = (bf16[512,512]{1,0:T(8,128)(2,1)S(1)}, bf16[512,512]{1,0:T(8,128)(2,1)S(1)}, u32[]{:S(2)}, u32[]{:S(2)}) collective-permute-start(bf16[512,512]{1,0:T(8,128)(2,1)S(1)} %collective-permute-done.2.refs_0_), channel_id=1, source_target_pairs={{0,1},{1,0},{2,3},{3,2},{4,5},{5,4},{6,7},{7,6},{8,9},{9,8},{10,11... | collective-permute-start | bytes 1572872 | tf_op jit(solution)/shard_map/ppermute | solution.py:216
  88.2 10.6 %collective-permute-start.7 = (bf16[512,512]{1,0:T(8,128)(2,1)S(1)}, bf16[512,512]{1,0:T(8,128)(2,1)S(1)}, u32[]{:S(2)}, u32[]{:S(2)}) collective-permute-start(bf16[512,512]{1,0:T(8,128)(2,1)S(1)} %collective-permute-done.6.refs_1_), channel_id=1, source_target_pairs={{0,1},{1,0},{2,3},{3,2},{4,5},{5,4},{6,7},{7,6},{8,9},{9,8},{10,11... | collective-permute-start | bytes 1572872 | tf_op jit(solution)/shard_map/ppermute | solution.py:216
  93.6 5.2 %collective-permute-start.19 = (f32[128,512]{1,0:T(8,128)S(1)}, f32[128,512]{1,0:T(8,128)S(1)}, u32[]{:S(2)}, u32[]{:S(2)}) collective-permute-start(f32[128,512]{1,0:T(8,128)S(1)} %fusion.3.refs_5_), channel_id=1, source_target_pairs={{0,1},{1,0},{2,3},{3,2},{4,5},{5,4},{6,7},{7,6},{8,9},{9,8},{10,11... | collective-permute-start | bytes 786440 | tf_op jit(solution)/shard_map/ppermute | solution.py:216

commit v3 on v2

--- a/solution.py
+++ b/solution.py
@@ -67,13 +67,13 @@
     return at ^ step if size & (size - 1) == 0 else (at + step) % size
 
 
-def owner_at(grid, spot):
+def owner_at(grid, spot, core):
     nz, ny, nx = grid
-    dz, dy, dx = spot
+    dz, da, db = spot
     me = lax.axis_index("fsdp")
     z, y, x = me // (ny * nx), me // nx % ny, me % nx
-    z, y, x = partner_of(z, dz, nz), partner_of(y, dy, ny), partner_of(x, dx, nx)
-    return (z * ny + y) * nx + x
+    dy, dx = jnp.where(core == 0, da, db), jnp.where(core == 0, db, da)
+    return (partner_of(z, dz, nz) * ny + (y ^ dy)) * nx + (x ^ dx)
 
 
 def stage_kernel(grid, lists, order_hbm, x_ref, *refs):
@@ -97,42 +97,42 @@
             stores.append(pltpu.make_async_copy(cot_ref, to, sems.at[1 + k]))
             stores[-1].start()
     fetch.wait()
-    cols = [[order_ref[owner_at(grid, spot)] for spot in spots] for spots in lists]
+    sides = (half, 1 - half)
+    cols = [
+        [order_ref[owner_at(grid, spot, side)] for spot in spots]
+        for spots in lists
+        for side in sides
+    ]
     for c in range(chunks):
         loads[c].wait()
         rows = slice(c * step, (c + 1) * step)
         for i, to_ref in enumerate(outs):
-            side = half if i % 2 == 0 else 1 - half
-            for k, col in enumerate(cols[i // 2]):
-                at = pl.ds(pl.multiple_of((2 * col + side) * LANES, LANES), LANES)
+            for k, col in enumerate(cols[i]):
+                at = pl.ds(pl.multiple_of((2 * col + sides[i % 2]) * LANES, LANES), LANES)
                 to_ref[rows, k * LANES : (k + 1) * LANES] = buf[c, :, at]
     for store in stores:
         store.wait()
 
 
-def wgrad_kernel(cot_at, *refs):
+def wgrad_kernel(cot_at, lists, *refs):
     sources, outs = refs[:2], refs[2:]
     cot = jnp.concatenate([r[:, cot_at:] for r in sources], axis=0)
-    begin = 0
-    for out in outs:
-        at = slice(begin, begin + out.shape[0])
+    for places, out in zip(lists, outs):
+        columns = [slice(p * LANES, (p + 1) * LANES) for p in places]
+        both = [jnp.concatenate([r[:, c] for c in columns], axis=1) for r in sources]
         out[...] = lax.dot_general(
-            jnp.concatenate([r[:, at] for r in sources], axis=0),
+            jnp.concatenate(both, axis=0),
             cot,
             (((0,), (0,)), ((), ())),
             preferred_element_type=jnp.float32,
         ).astype(out.dtype)
-        begin += out.shape[0]
 
 
 def apply_kernel(grid, pieces, first, last, order_ref, cot_ref, *refs):
     half = lax.axis_index("dp") % 2
     refs = list(refs)
     weights = [refs.pop(0) for _ in pieces]
-    columns = {}
-    for _, partner in pieces:
-        if partner not in columns:
-            columns[partner] = [refs.pop(0), 0]
+    columns = [refs.pop(0) for _ in range(1 + max(p[2] for p in pieces))]
     before_ref = None if first else refs.pop(0)
     if not first:
         refs.pop(0)
@@ -155,14 +155,14 @@
         stores[-1].start()
     cot = cot_ref[...]
     count = 0
-    for place, (spots, partner) in enumerate(pieces):
+    for place, (spots, partner, _, _) in enumerate(pieces):
         side = 1 - half if partner else half
         back = lax.dot_general(
             cot, weights[place][...], (((1,), (1,)), ((), ())), preferred_element_type=jnp.float32
         )
         scratch[place] = back.astype(scratch.dtype)
         for k, spot in enumerate(spots):
-            col = order_ref[owner_at(grid, spot)]
+            col = order_ref[owner_at(grid, spot, side)]
             start = pl.multiple_of((2 * col + side) * LANES, LANES)
             stores.append(
                 pltpu.make_async_copy(
@@ -174,12 +174,9 @@
             stores[-1].start()
             count += 1
     total = None
-    for place, (spots, partner) in enumerate(pieces):
-        source, begin = columns[partner]
-        columns[partner][1] = end = begin + len(spots) * LANES
-        term = jnp.dot(
-            source[:, begin:end], weights[place][...], preferred_element_type=jnp.float32
-        )
+    for place, (spots, _, source, begin) in enumerate(pieces):
+        source = columns[source][:, begin : begin + len(spots) * LANES]
+        term = jnp.dot(source, weights[place][...], preferred_element_type=jnp.float32)
         total = term if total is None else total + term
     if not first:
         fetch.wait()
@@ -215,11 +212,11 @@
                         pairs.append((((z * ny + y) * nx + x) * replicas + r, to * replicas + tr))
         return lax.ppermute(value, ("fsdp", "dp"), pairs)
 
-    def over_x(value):
-        return send(value, lambda z, y, x, r: (z, y, partner_of(x, 1, nx), r))
-
-    def over_y(value):
-        return send(value, lambda z, y, x, r: (z, partner_of(y, 1, ny), x, r))
+    def over_first(value):
+        return send(value, lambda z, y, x, r: (z, y, x ^ 1, r) if r % 2 else (z, y ^ 1, x, r))
+
+    def over_second(value):
+        return send(value, lambda z, y, x, r: (z, y ^ 1, x, r) if r % 2 else (z, y, x ^ 1, r))
 
     def over_z(value, step):
         return send(value, lambda z, y, x, r: (partner_of(z, step, nz), y, x, r))
@@ -230,16 +227,14 @@
     flat = normed.reshape(rows, width)
     cot = kv_cotangent.reshape(rows, key_width)
     doubling = [nz >> k for k in range(1, nz.bit_length())]
-    near = [0]
-    for d in doubling[:-1]:
-        near = near + [d + k for k in near]
-    far = [1 + k for k in near]
-    red_rows, blue_rows = part * len(near), part * len(far)
-
-    far_spots = [(k, 1, dx) for dx in (0, 1) for k in near]
-    far_spots += [(k, dy, 1) for dy in (0, 1) for k in far]
-    near_spots = [(k, 0, dx) for dx in (0, 1) for k in near]
-    near_spots += [(k, dy, 0) for dy in (0, 1) for k in far]
+    line = [0]
+    for d in doubling:
+        line = line + [d + k for k in line]
+    line_rows = part * nz
+    groups = [[k for k in line if k >= nz // 2], [k for k in line if k < nz // 2]]
+    group_rows = line_rows // 2
+
+    near_spots, far_spots = ([(k, da, db) for db in (0, 1) for k in line] for da in (0, 1))
     chunks = 4
 
     def stage(lists, extra, limit):
@@ -261,17 +256,22 @@
             compiler_params=pltpu.CompilerParams(vmem_limit_bytes=limit),
         )(owner_order, flat, *extra)
 
-    first_own, first_partner = stage([far_spots], [cot], TIGHT_BYTES)
+    first_spots = [(k, 1, db) for ks in groups for db in (0, 1) for k in ks]
+    first_own, first_partner = stage([first_spots], [cot], TIGHT_BYTES)
     first_got = to_core(first_partner)
     near_own, near_partner, far_own, far_partner = stage([near_spots, far_spots], [cot], 8 << 20)
     near_got = to_core(near_partner)
 
-    def wgrad(sources, sizes, dtype):
+    def wgrad(sources, order, lists, dtype):
+        places = [[order.index(spot) for spot in spots] for spots in lists]
+        cot_at = sources[0].shape[1] - key_width
         return pl.pallas_call(
-            functools.partial(wgrad_kernel, sources[0].shape[1] - key_width),
-            in_specs=[vmem] * len(sources),
-            out_specs=[vmem] * len(sizes),
-            out_shape=[jax.ShapeDtypeStruct((size, key_width), dtype) for size in sizes],
+            functools.partial(wgrad_kernel, cot_at, places),
+            in_specs=[vmem] * 2,
+            out_specs=[vmem] * len(lists),
+            out_shape=[
+                jax.ShapeDtypeStruct((part * len(s), key_width), dtype) for s in lists
+            ],
             cost_estimate=pl.CostEstimate(
                 flops=rows * width * key_width,
                 bytes_accessed=4 * rows * width,
@@ -280,36 +280,39 @@
             compiler_params=pltpu.CompilerParams(vmem_limit_bytes=24 << 20),
         )(*sources)
 
-    red_out, blue_out = wgrad([first_own, first_got], [2 * red_rows, 2 * blue_rows], bf16)
-    red_keep, red_on, blue_keep, blue_on = wgrad(
-        [near_own, near_got], [red_rows, red_rows, blue_rows, blue_rows], f32
-    )
-
-    own = lax.dynamic_slice_in_dim(kv_weight, half * part, part, axis=0)
-    red = own
-    for d in doubling[:-1]:
-        red = jnp.concatenate([red, over_z(red, d)], axis=0)
-    blue = over_z(red, 1)
-    red = jnp.concatenate([red, over_x(red)], axis=0)
-    blue = jnp.concatenate([blue, over_y(blue)], axis=0)
-    red_y = over_y(red)
-    blue_x = over_x(blue)
-    red_spots, blue_spots = near_spots[: 2 * len(near)], near_spots[2 * len(near) :]
-    red_y_spots, blue_x_spots = far_spots[: 2 * len(near)], far_spots[2 * len(near) :]
-
-    red_in = over_y(red_out)
-    blue_in = over_x(blue_out)
-    red_far = (red_on + red_in[red_rows:]).astype(bf16)
-    blue_far = (blue_on + blue_in[blue_rows:]).astype(bf16)
-    red_sum = red_keep + red_in[:red_rows] + over_x(red_far)
-    blue_sum = blue_keep + blue_in[:blue_rows] + over_y(blue_far)
+    outs = wgrad(
+        [first_own, first_got],
+        first_spots,
+        [[(k, 1, db) for db in (0, 1) for k in ks] for ks in groups],
+        bf16,
+    )
+    kept_terms = wgrad(
+        [near_own, near_got],
+        near_spots,
+        [[(k, 0, db) for k in ks] for ks in groups for db in (0, 1)],
+        f32,
+    )
+
+    held = lax.dynamic_slice_in_dim(kv_weight, half * part, part, axis=0)
+    for d in doubling:
+        held = jnp.concatenate([held, over_z(held, d)], axis=0)
+    beside = over_first(held)
+    across = over_second(held)
+    corner = over_second(beside)
+
     along = {}
-    for places, sums in ((near, red_sum), (far, blue_sum)):
-        for at, k in enumerate(places):
-            along[k] = sums[at * part : (at + 1) * part]
+    for i, ks in enumerate(groups):
+        keep, on = kept_terms[2 * i : 2 * i + 2]
+        arrived = over_first(outs[i])
+        onward = (on + arrived[group_rows:]).astype(bf16)
+        last = over_second(onward)
+        sums = keep + arrived[:group_rows] + last
+        for at, k in enumerate(ks):
+            piece = sums[at * part : (at + 1) * part]
+            along[k] = piece.astype(bf16) if k else piece
     total = along[0]
-    for d in range(1, nz):
-        total = total + over_z(along[d].astype(bf16), d)
+    for d in range(nz - 1, 0, -1):
+        total = total + over_z(along[d], d)
     if replicas > 2:
         groups = [[r for r in range(replicas) if r % 2 == h] for h in (0, 1)]
         total = lax.psum(total, "dp", axis_index_groups=groups)
@@ -318,11 +321,11 @@
     there = to_core(kept)
 
     def apply(pieces, columns, before, halves):
-        weights = [w for w, _, _ in pieces]
+        weights = [p[0] for p in pieces]
         inputs = [owner_order, cot, *weights, *columns, *before, *halves]
         specs = [smem] + [vmem] * (1 + len(pieces) + len(columns)) + [hbm, hbm][: len(before)]
         specs += [vmem] * len(halves)
-        count = sum(len(spots) for _, spots, _ in pieces)
+        count = sum(len(p[1]) for p in pieces)
         wide = max(w.shape[0] for w in weights)
         key_type = bf16 if halves else f32
         shapes = [
@@ -354,23 +357,30 @@
             compiler_params=pltpu.CompilerParams(vmem_limit_bytes=24 << 20),
         )(*inputs)
 
+    spots = {(da, db): [(k, da, db) for k in line] for da in (0, 1) for db in (0, 1)}
     done = apply(
         [
-            (red, red_spots, False),
-            (blue, blue_spots, False),
-            (to_core(red), red_spots, True),
-            (to_core(blue), blue_spots, True),
+            (held, spots[0, 0], False, 0, 0),
+            (beside, spots[1, 0], False, 1, 0),
+            (to_core(held), spots[0, 0], True, 2, 0),
+            (to_core(beside), spots[1, 0], True, 3, 0),
+        ],
+        [near_own, far_own, near_partner, far_partner],
+        (),
+        (),
+    )
+    done = apply(
+        [
+            (across, spots[0, 1], False, 0, line_rows),
+            (to_core(across), spots[0, 1], True, 1, line_rows),
         ],
         [near_own, near_partner],
+        done,
         (),
-        (),
-    )
-    done = apply([(red_y, red_y_spots, False), (blue_x, blue_x_spots, False)], [far_own], done, ())
+    )
+    done = apply([(corner, spots[1, 1], False, 0, line_rows)], [far_own], done, ())
     key, input_grad, grad_buffer = apply(
-        [(to_core(red_y), red_y_spots, True), (to_core(blue_x), blue_x_spots, True)],
-        [far_partner],
-        done,
-        (kept, there),
+        [(to_core(corner), spots[1, 1], True, 0, line_rows)], [far_partner], done, (kept, there)
     )
     return (
         key.reshape(micro_count, tok_dev, key_width),

time: 101 us -> 76.2 us (0.75)
  waiting for transfers between devices: 60.5 us -> 38.5 us
  Pallas kernels: 16.2 us -> 13.9 us
  local copies, waits for them, and re-layouts: 2.84 us -> 1.67 us
    ppermute x20 -> x19, waiting for transfers between devices: 60.5 us -> 38.5 us  [send(): return lax.ppermute(value, ('fsdp', 'dp'), pairs)]
    pallas_call x2, Pallas kernels: 3.73 us -> 1.46 us  [wgrad(): pl.pallas_call(functools.partial(wgrad_kernel, cot_at, places), in_specs=...]
    unnamed x13 -> x12, local copies, waits for them, and re-layouts: 2.77 us -> 1.62 us
    pallas_call x3 -> x4, Pallas kernels: 7.25 us -> 8.12 us  [apply(): pl.pallas_call(functools.partial(apply_kernel, grid, [p[1:] for p in piec...]
    ppermute x20 -> x19, starting transfers between devices: 20 us -> 20.6 us  [send(): return lax.ppermute(value, ('fsdp', 'dp'), pairs)]
  transfers between devices with their start and end apart: 20 -> 19, of which waited for: 9 -> 7; matrix products, arithmetic and copies ran while one was open for 1% -> 1% of each run, Pallas kernels for 11% -> 12%
where the time goes in v3:
time: 76.2 us; the launch traced here: 76 us
  waiting for transfers between devices  38.5 us (51%)
  starting transfers between devices  20.6 us (27%)
  Pallas kernels  13.9 us (18%)
  local copies, waits for them, and re-layouts  1.67 us (2%)
  between operations  0.86 us (1%)
    ppermute x19, waiting for transfers between devices, send(): return lax.ppermute(value, ('fsdp', 'dp'), pairs)  38.5 us
    ppermute x19, starting transfers between devices, send(): return lax.ppermute(value, ('fsdp', 'dp'), pairs)  20.6 us
    pallas_call x4, Pallas kernels, apply(): pl.pallas_call(functools.partial(apply_kernel, grid, [p[1:] for p in piec...  8.12 us
    pallas_call x2, Pallas kernels, stage(): pl.pallas_call(functools.partial(stage_kernel, grid, lists), in_specs=[hb...  4.3 us
    unnamed x12, local copies, waits for them, and re-layouts  1.62 us
  transfers between devices with their start and end apart: 19, of which 7 were waited for; matrix products, arithmetic and copies ran while one was open for 1% of the time, Pallas kernels for 12%

profile of v3, /device:TPU:0, one launch (start us, length us, event | category | flops | bytes accessed | tf_op | source)
XLA Modules:
  0.0 76.0 jit_solution(12970974612567498067)
XLA Ops:
  0.6 0.0 copy-start
  0.6 0.0 copy-start.1
  0.7 0.0 copy-start.3
  0.7 2.9 %shard_map.81 = (bf16[256,1536]{1,0:T(8,128)(2,1)}, bf16[256,1536]{1,0:T(8,128)(2,1)}) custom-call(s32[16]{0:T(128)} %order_ref.7, bf16[256,4096]{1,0:T(8,128)(2,1)} %bitcast.10, bf16[256,512]{1,0:T(8,128)(2,1)} %bitcast.4), custom_call_target="tpu_custom_call" | custom-call | tf_op jit(solution)/shard_map/pallas_call | solution.py:245
  3.6 0.6 collective-permute-start.10
  4.2 0.0 copy-done
  4.2 3.7 %collective-permute-start = (bf16[128,512]{1,0:T(8,128)(2,1)S(1)}, bf16[128,512]{1,0:T(8,128)(2,1)S(1)}, u32[]{:S(2)}, u32[]{:S(2)}) collective-permute-start(bf16[128,512]{1,0:T(8,128)(2,1)S(1)} %constant_dynamic-slice_fusion), channel_id=1, source_target_pairs={{0,16},{1,17},{2,18},{3,19},{4,20},{5,21},{6,22},{7,23},{8,24},{9,... | collective-permute-start | bytes 393224 | tf_op jit(solution)/shard_map/ppermute | solution.py:213
  7.9 0.0 copy-done.1
  7.9 0.0 copy-done.3
  7.9 0.0 copy-start.2
  7.9 1.6 %copy-done.2 = bf16[2,128,4096]{2,1,0:T(8,128)(2,1)S(1)} copy-done((bf16[2,128,4096]{2,1,0:T(8,128)(2,1)S(1)}, bf16[2,128,4096]{2,1,0:T(8,128)(2,1)}, u32[]{:S(2)}) %copy-start.2) | copy-done | bytes 2097176
  9.5 0.0 copy-start.4
  9.5 1.4 %shard_map.76 = (bf16[256,1536]{1,0:T(8,128)(2,1)S(1)}, bf16[256,1536]{1,0:T(8,128)(2,1)S(1)}, bf16[256,1024]{1,0:T(8,128)(2,1)S(1)}, bf16[256,1024]{1,0:T(8,128)(2,1)S(1)}) custom-call(s32[16]{0:T(128)S(1)} %copy-done.3, bf16[256,4096]{1,0:T(8,128)(2,1)S(1)} %bitcast.11, bf16[256,512]{1,0:T(8,128)(2,1)S(1)} %bitcast.5), custom_call_target="tpu_custom_call" | custom-call | tf_op jit(solution)/shard_map/pallas_call | solution.py:245
  10.8 0.2 collective-permute-start.9
  11.1 3.7 %collective-permute-done = bf16[128,512]{1,0:T(8,128)(2,1)S(1)} collective-permute-done((bf16[128,512]{1,0:T(8,128)(2,1)S(1)}, bf16[128,512]{1,0:T(8,128)(2,1)S(1)}, u32[]{:S(2)}, u32[]{:S(2)}) %collective-permute-start) | collective-permute-done | bytes 131104 | tf_op jit(solution)/shard_map/ppermute | solution.py:213
  14.8 0.8 %collective-permute-start.1 = (bf16[256,512]{1,0:T(8,128)(2,1)S(1)}, bf16[256,512]{1,0:T(8,128)(2,1)S(1)}, u32[]{:S(2)}, u32[]{:S(2)}) collective-permute-start(bf16[256,512]{1,0:T(8,128)(2,1)S(1)} %pad_maximum_fusion.1), channel_id=1, source_target_pairs={{0,8},{1,9},{2,10},{3,11},{4,12},{5,13},{6,14},{7,15},{8,0},{9,1},... | collective-permute-start | bytes 786440 | tf_op jit(solution)/shard_map/ppermute | solution.py:213
  15.6 0.0 collective-permute-done.10.refs_1_
  15.6 0.0 copy-done.4
  15.6 0.7 shard_map.82
  16.4 1.6 %collective-permute-start.13 = (bf16[512,512]{1,0:T(8,128)(2,1)S(1)}, bf16[512,512]{1,0:T(8,128)(2,1)S(1)}, u32[]{:S(2)}, u32[]{:S(2)}) collective-permute-start(bf16[512,512]{1,0:T(8,128)(2,1)S(1)} %get-tuple-element.40), channel_id=1, source_target_pairs={{0,4},{1,3},{2,6},{3,1},{4,0},{5,7},{6,2},{7,5},{8,12},{9,11},{10,... | collective-permute-start | bytes 1572872 | tf_op jit(solution)/shard_map/ppermute | solution.py:213
  18.0 5.0 %collective-permute-done.1 = bf16[256,512]{1,0:T(8,128)(2,1)S(1)} collective-permute-done((bf16[256,512]{1,0:T(8,128)(2,1)S(1)}, bf16[256,512]{1,0:T(8,128)(2,1)S(1)}, u32[]{:S(2)}, u32[]{:S(2)}) %collective-permute-start.1) | collective-permute-done | bytes 262176 | tf_op jit(solution)/shard_map/ppermute | solution.py:213
  23.0 1.4 %collective-permute-start.2 = (bf16[512,512]{1,0:T(8,128)(2,1)S(1)}, bf16[512,512]{1,0:T(8,128)(2,1)S(1)}, u32[]{:S(2)}, u32[]{:S(2)}) collective-permute-start(bf16[512,512]{1,0:T(8,128)(2,1)S(1)} %pad_maximum_fusion.refs_0_), channel_id=1, source_target_pairs={{0,4},{1,3},{2,6},{3,1},{4,0},{5,7},{6,2},{7,5},{8,12},{9,11},{10,... | collective-permute-start | bytes 1572872 | tf_op jit(solution)/shard_map/ppermute | solution.py:213
  24.4 0.7 collective-permute-start.11
  25.1 0.0 collective-permute-done.9.refs_1_
  25.1 0.7 shard_map.80
  25.9 0.0 collective-permute-done.13
  25.9 0.1 add_convert_fusion.1
  26.0 1.3 %collective-permute-start.14 = (bf16[256,512]{1,0:T(8,128)(2,1)S(1)}, bf16[256,512]{1,0:T(8,128)(2,1)S(1)}, u32[]{:S(2)}, u32[]{:S(2)}) collective-permute-start(bf16[256,512]{1,0:T(8,128)(2,1)S(1)} %add_convert_fusion.1), channel_id=1, source_target_pairs={{0,2},{1,5},{2,0},{3,7},{4,6},{5,1},{6,4},{7,3},{8,10},{9,13},{10,... | collective-permute-start | bytes 786440 | tf_op jit(solution)/shard_map/ppermute | solution.py:213
  27.3 0.0 collective-permute-start.7
  27.3 0.8 %collective-permute-start.5 = (bf16[512,512]{1,0:T(8,128)(2,1)S(1)}, bf16[512,512]{1,0:T(8,128)(2,1)S(1)}, u32[]{:S(2)}, u32[]{:S(2)}) collective-permute-start(bf16[512,512]{1,0:T(8,128)(2,1)S(1)} %pad_maximum_fusion.refs_0_), channel_id=1, source_target_pairs={{0,2},{1,5},{2,0},{3,7},{4,6},{5,1},{6,4},{7,3},{8,10},{9,13},{10,... | collective-permute-start | bytes 1572872 | tf_op jit(solution)/shard_map/ppermute | solution.py:213
  28.1 9.2 %collective-permute-done.2.refs_1_ = bf16[512,512]{1,0:T(8,128)(2,1)S(1)} collective-permute-done((bf16[512,512]{1,0:T(8,128)(2,1)S(1)}, bf16[512,512]{1,0:T(8,128)(2,1)S(1)}, u32[]{:S(2)}, u32[]{:S(2)}) %collective-permute-start.2) | collective-permute-done | bytes 524320 | tf_op jit(solution)/shard_map/ppermute | solution.py:213
  37.3 0.0 collective-permute-start.8
  37.3 10.3 %collective-permute-done.11 = bf16[512,512]{1,0:T(8,128)(2,1)S(1)} collective-permute-done((bf16[512,512]{1,0:T(8,128)(2,1)S(1)}, bf16[512,512]{1,0:T(8,128)(2,1)S(1)}, u32[]{:S(2)}, u32[]{:S(2)}) %collective-permute-start.11) | collective-permute-done | bytes 524320 | tf_op jit(solution)/shard_map/ppermute | solution.py:213
  47.6 1.4 %collective-permute-start.3 = (bf16[512,512]{1,0:T(8,128)(2,1)S(1)}, bf16[512,512]{1,0:T(8,128)(2,1)S(1)}, u32[]{:S(2)}, u32[]{:S(2)}) collective-permute-start(bf16[512,512]{1,0:T(8,128)(2,1)S(1)} %collective-permute-done.2.refs_1_), channel_id=1, source_target_pairs={{0,2},{1,5},{2,0},{3,7},{4,6},{5,1},{6,4},{7,3},{8,10},{9,13},{10,... | collective-permute-start | bytes 1572872 | tf_op jit(solution)/shard_map/ppermute | solution.py:213
  49.0 0.1 add_convert_fusion.2
  49.1 0.0 copy-start.5
  49.1 0.0 collective-permute-done.14
  49.1 0.7 collective-permute-start.12
  49.8 0.1 add_convert_fusion
  49.9 0.0 collective-permute-done.5.refs_0_
  50.0 3.4 %collective-permute-start.15 = (bf16[128,512]{1,0:T(8,128)(2,1)S(1)}, bf16[128,512]{1,0:T(8,128)(2,1)S(1)}, u32[]{:S(2)}, u32[]{:S(2)}) collective-permute-start(bf16[128,512]{1,0:T(8,128)(2,1)S(1)} %get-tuple-element.45), channel_id=1, source_target_pairs={{0,24},{1,25},{2,26},{3,27},{4,28},{5,29},{6,30},{7,31},{8,16},{9,... | collective-permute-start | bytes 393224 | tf_op jit(solution)/shard_map/ppermute | solution.py:213
  53.4 6.2 %collective-permute-done.12 = bf16[256,512]{1,0:T(8,128)(2,1)S(1)} collective-permute-done((bf16[256,512]{1,0:T(8,128)(2,1)S(1)}, bf16[256,512]{1,0:T(8,128)(2,1)S(1)}, u32[]{:S(2)}, u32[]{:S(2)}) %collective-permute-start.12) | collective-permute-done | bytes 262176 | tf_op jit(solution)/shard_map/ppermute | solution.py:213
  59.6 2.0 %collective-permute-start.16 = (bf16[128,512]{1,0:T(8,128)(2,1)S(1)}, bf16[128,512]{1,0:T(8,128)(2,1)S(1)}, u32[]{:S(2)}, u32[]{:S(2)}) collective-permute-start(bf16[128,512]{1,0:T(8,128)(2,1)S(1)} %get-tuple-element.46), channel_id=1, source_target_pairs={{0,16},{1,17},{2,18},{3,19},{4,20},{5,21},{6,22},{7,23},{8,24},{9,... | collective-permute-start | bytes 393224 | tf_op jit(solution)/shard_map/ppermute | solution.py:213
  61.6 0.1 convert_add_fusion
  61.8 0.0 collective-permute-done.3.refs_0_
  61.8 2.0 %collective-permute-start.17 = (bf16[128,512]{1,0:T(8,128)(2,1)S(1)}, bf16[128,512]{1,0:T(8,128)(2,1)S(1)}, u32[]{:S(2)}, u32[]{:S(2)}) collective-permute-start(bf16[128,512]{1,0:T(8,128)(2,1)S(1)} %slice.57), channel_id=1, source_target_pairs={{0,8},{1,9},{2,10},{3,11},{4,12},{5,13},{6,14},{7,15},{8,0},{9,1},... | collective-permute-start | bytes 393224 | tf_op jit(solution)/shard_map/ppermute | solution.py:213
  63.7 0.0 collective-permute-done.15
  63.7 0.0 collective-permute-start.6
  63.7 3.2 %collective-permute-done.16 = bf16[128,512]{1,0:T(8,128)(2,1)S(1)} collective-permute-done((bf16[128,512]{1,0:T(8,128)(2,1)S(1)}, bf16[128,512]{1,0:T(8,128)(2,1)S(1)}, u32[]{:S(2)}, u32[]{:S(2)}) %collective-permute-start.16) | collective-permute-done | bytes 131104 | tf_op jit(solution)/shard_map/ppermute | solution.py:213
  67.0 0.0 collective-permute-start.4
  67.0 0.7 collective-permute-done.17
  67.7 0.0 copy-done.5
  67.7 0.1 fusion.3.refs_4_
  67.8 0.1 collective-permute-start.18
  67.8 0.0 collective-permute-done.7.refs_2_
  67.9 0.0 collective-permute-done.8.refs_3_
  67.9 2.5 %shard_map.77 = (f32[256,512]{1,0:T(8,128)S(1)}, bf16[256,4096]{1,0:T(8,128)(2,1)}) custom-call(s32[16]{0:T(128)S(1)} %copy-done.3, bf16[256,512]{1,0:T(8,128)(2,1)S(1)} %bitcast.6, bf16[512,512]{1,0:T(8,128)(2,1)S(1)} %pad_maximum_fusion.refs_0_, bf16[512,512]{1,0:T(8,128)(2,1)S(1)} %collective-permute-done.2.refs_1_, ...), custom_call_target="tpu_custom_call" | custom-call | flops 1073741824 | bytes 2097152 | tf_op jit(solution)/shard_map/pallas_call | solution.py:337
  70.4 0.0 collective-permute-done.6.refs_1_
  70.4 1.9 %shard_map.78 = (f32[256,512]{1,0:T(8,128)S(1)}, bf16[256,4096]{1,0:T(8,128)(2,1)}) custom-call(s32[16]{0:T(128)S(1)} %copy-done.3, bf16[256,512]{1,0:T(8,128)(2,1)S(1)} %bitcast.7, bf16[512,512]{1,0:T(8,128)(2,1)S(1)} %collective-permute-done.5.refs_0_, bf16[512,512]{1,0:T(8,128)(2,1)S(1)} %collective-permute-done.6.refs_1_, ...), custom_call_target="tpu_custom_call", output_to_operand_aliasing={{1}: (7, {})} | custom-call | flops 536870912 | bytes 2097152 | tf_op jit(solution)/shard_map/pallas_call | solution.py:337
  72.3 1.7 %shard_map.79 = (f32[256,512]{1,0:T(8,128)S(1)}, bf16[256,4096]{1,0:T(8,128)(2,1)}) custom-call(s32[16]{0:T(128)S(1)} %copy-done.3, bf16[256,512]{1,0:T(8,128)(2,1)S(1)} %bitcast.8, bf16[512,512]{1,0:T(8,128)(2,1)S(1)} %collective-permute-done.3.refs_0_, bf16[256,1024]{1,0:T(8,128)(2,1)S(1)} %get-tuple-element.25.refs_5_.refs_1_, ...), custom_call_target="tpu_custom_call", output_to_operand_aliasing={{1}: (5, {})} | custom-call | flops 268435456 | bytes 2097152 | tf_op jit(solution)/shard_map/pallas_call | solution.py:337
  74.0 0.0 collective-permute-done.18.refs_5_
  74.0 0.0 collective-permute-done.4.refs_0_
  74.0 2.0 %shard_map.83 = (bf16[256,512]{1,0:T(8,128)(2,1)}, bf16[256,4096]{1,0:T(8,128)(2,1)}, f32[256,512]{1,0:T(8,128)}) custom-call(s32[16]{0:T(128)S(1)} %copy-done.3, bf16[256,512]{1,0:T(8,128)(2,1)S(1)} %bitcast.9, bf16[512,512]{1,0:T(8,128)(2,1)S(1)} %collective-permute-done.4.refs_0_, ...), custom_call_target="tpu_custom_call", output_to_operand_aliasing={{1}: (5, {})} | custom-call | flops 268435456 | bytes 2097152 | tf_op jit(solution)/shard_map/pallas_call | solution.py:337
  (5 shorter events, 0.1 us)
Async XLA Ops:
  0.6 3.6 %copy-start = (bf16[256,512]{1,0:T(8,128)(2,1)S(1)}, bf16[256,512]{1,0:T(8,128)(2,1)}, u32[]{:S(2)}) copy-start(bf16[256,512]{1,0:T(8,128)(2,1)} %param.7) | copy-start | bytes 786436
  0.6 7.2 %copy-start.1 = (bf16[2,128,512]{2,1,0:T(8,128)(2,1)S(1)}, bf16[2,128,512]{2,1,0:T(8,128)(2,1)}, u32[]{:S(2)}) copy-start(bf16[2,128,512]{2,1,0:T(8,128)(2,1)} %param.6) | copy-start | bytes 786436
  0.7 7.2 %copy-start.3 = (s32[16]{0:T(128)S(1)}, s32[16]{0:T(128)}, u32[]{:S(2)}) copy-start(s32[16]{0:T(128)} %order_ref.7) | copy-start | bytes 196
  3.6 12.0 %collective-permute-start.10 = (bf16[256,1536]{1,0:T(8,128)(2,1)}, bf16[256,1536]{1,0:T(8,128)(2,1)S(1)}, u32[]{:S(2)}, u32[]{:S(2)}) collective-permute-start(bf16[256,1536]{1,0:T(8,128)(2,1)} %get-tuple-element.36), channel_id=1, source_target_pairs={{0,1},{1,0},{2,3},{3,2},{4,5},{5,4},{6,7},{7,6},{8,9},{9,8},{10,11... | collective-permute-start | bytes 2359304 | tf_op jit(solution)/shard_map/ppermute | solution.py:213
  4.2 10.6 %collective-permute-start = (bf16[128,512]{1,0:T(8,128)(2,1)S(1)}, bf16[128,512]{1,0:T(8,128)(2,1)S(1)}, u32[]{:S(2)}, u32[]{:S(2)}) collective-permute-start(bf16[128,512]{1,0:T(8,128)(2,1)S(1)} %constant_dynamic-slice_fusion), channel_id=1, source_target_pairs={{0,16},{1,17},{2,18},{3,19},{4,20},{5,21},{6,22},{7,23},{8,24},{9,... | collective-permute-start | bytes 393224 | tf_op jit(solution)/shard_map/ppermute | solution.py:213
  7.9 1.6 %copy-start.2 = (bf16[2,128,4096]{2,1,0:T(8,128)(2,1)S(1)}, bf16[2,128,4096]{2,1,0:T(8,128)(2,1)}, u32[]{:S(2)}) copy-start(bf16[2,128,4096]{2,1,0:T(8,128)(2,1)} %param.5) | copy-start | bytes 6291460
  9.5 6.2 %copy-start.4 = (bf16[256,1536]{1,0:T(8,128)(2,1)S(1)}, bf16[256,1536]{1,0:T(8,128)(2,1)}, u32[]{:S(2)}) copy-start(bf16[256,1536]{1,0:T(8,128)(2,1)} %get-tuple-element.35.refs_0_) | copy-start | bytes 2359300
  10.8 14.3 %collective-permute-start.9 = (bf16[256,1536]{1,0:T(8,128)(2,1)S(1)}, bf16[256,1536]{1,0:T(8,128)(2,1)S(1)}, u32[]{:S(2)}, u32[]{:S(2)}) collective-permute-start(bf16[256,1536]{1,0:T(8,128)(2,1)S(1)} %get-tuple-element.27.refs_6_.refs_3_), channel_id=1, source_target_pairs={{0,1},{1,0},{2,3},{3,2},{4,5},{5,4},{6,7},{7,6},{8,9},{9,8},{10,11... | collective-permute-start | bytes 2359304 | tf_op jit(solution)/shard_map/ppermute | solution.py:213
  14.8 8.2 %collective-permute-start.1 = (bf16[256,512]{1,0:T(8,128)(2,1)S(1)}, bf16[256,512]{1,0:T(8,128)(2,1)S(1)}, u32[]{:S(2)}, u32[]{:S(2)}) collective-permute-start(bf16[256,512]{1,0:T(8,128)(2,1)S(1)} %pad_maximum_fusion.1), channel_id=1, source_target_pairs={{0,8},{1,9},{2,10},{3,11},{4,12},{5,13},{6,14},{7,15},{8,0},{9,1},... | collective-permute-start | bytes 786440 | tf_op jit(solution)/shard_map/ppermute | solution.py:213
  16.4 9.5 %collective-permute-start.13 = (bf16[512,512]{1,0:T(8,128)(2,1)S(1)}, bf16[512,512]{1,0:T(8,128)(2,1)S(1)}, u32[]{:S(2)}, u32[]{:S(2)}) collective-permute-start(bf16[512,512]{1,0:T(8,128)(2,1)S(1)} %get-tuple-element.40), channel_id=1, source_target_pairs={{0,4},{1,3},{2,6},{3,1},{4,0},{5,7},{6,2},{7,5},{8,12},{9,11},{10,... | collective-permute-start | bytes 1572872 | tf_op jit(solution)/shard_map/ppermute | solution.py:213
  23.0 14.2 %collective-permute-start.2 = (bf16[512,512]{1,0:T(8,128)(2,1)S(1)}, bf16[512,512]{1,0:T(8,128)(2,1)S(1)}, u32[]{:S(2)}, u32[]{:S(2)}) collective-permute-start(bf16[512,512]{1,0:T(8,128)(2,1)S(1)} %pad_maximum_fusion.refs_0_), channel_id=1, source_target_pairs={{0,4},{1,3},{2,6},{3,1},{4,0},{5,7},{6,2},{7,5},{8,12},{9,11},{10,... | collective-permute-start | bytes 1572872 | tf_op jit(solution)/shard_map/ppermute | solution.py:213
  24.4 23.2 %collective-permute-start.11 = (bf16[512,512]{1,0:T(8,128)(2,1)S(1)}, bf16[512,512]{1,0:T(8,128)(2,1)S(1)}, u32[]{:S(2)}, u32[]{:S(2)}) collective-permute-start(bf16[512,512]{1,0:T(8,128)(2,1)S(1)} %get-tuple-element.37), channel_id=1, source_target_pairs={{0,4},{1,3},{2,6},{3,1},{4,0},{5,7},{6,2},{7,5},{8,12},{9,11},{10,... | collective-permute-start | bytes 1572872 | tf_op jit(solution)/shard_map/ppermute | solution.py:213
  26.0 23.1 %collective-permute-start.14 = (bf16[256,512]{1,0:T(8,128)(2,1)S(1)}, bf16[256,512]{1,0:T(8,128)(2,1)S(1)}, u32[]{:S(2)}, u32[]{:S(2)}) collective-permute-start(bf16[256,512]{1,0:T(8,128)(2,1)S(1)} %add_convert_fusion.1), channel_id=1, source_target_pairs={{0,2},{1,5},{2,0},{3,7},{4,6},{5,1},{6,4},{7,3},{8,10},{9,13},{10,... | collective-permute-start | bytes 786440 | tf_op jit(solution)/shard_map/ppermute | solution.py:213
  27.3 40.6 %collective-permute-start.7 = (bf16[512,512]{1,0:T(8,128)(2,1)S(1)}, bf16[512,512]{1,0:T(8,128)(2,1)S(1)}, u32[]{:S(2)}, u32[]{:S(2)}) collective-permute-start(bf16[512,512]{1,0:T(8,128)(2,1)S(1)} %pad_maximum_fusion.refs_0_), channel_id=1, source_target_pairs={{0,1},{1,0},{2,3},{3,2},{4,5},{5,4},{6,7},{7,6},{8,9},{9,8},{10,11... | collective-permute-start | bytes 1572872 | tf_op jit(solution)/shard_map/ppermute | solution.py:213
  27.3 22.7 %collective-permute-start.5 = (bf16[512,512]{1,0:T(8,128)(2,1)S(1)}, bf16[512,512]{1,0:T(8,128)(2,1)S(1)}, u32[]{:S(2)}, u32[]{:S(2)}) collective-permute-start(bf16[512,512]{1,0:T(8,128)(2,1)S(1)} %pad_maximum_fusion.refs_0_), channel_id=1, source_target_pairs={{0,2},{1,5},{2,0},{3,7},{4,6},{5,1},{6,4},{7,3},{8,10},{9,13},{10,... | collective-permute-start | bytes 1572872 | tf_op jit(solution)/shard_map/ppermute | solution.py:213
  37.3 30.6 %collective-permute-start.8 = (bf16[512,512]{1,0:T(8,128)(2,1)S(1)}, bf16[512,512]{1,0:T(8,128)(2,1)S(1)}, u32[]{:S(2)}, u32[]{:S(2)}) collective-permute-start(bf16[512,512]{1,0:T(8,128)(2,1)S(1)} %collective-permute-done.2.refs_1_), channel_id=1, source_target_pairs={{0,1},{1,0},{2,3},{3,2},{4,5},{5,4},{6,7},{7,6},{8,9},{9,8},{10,11... | collective-permute-start | bytes 1572872 | tf_op jit(solution)/shard_map/ppermute | solution.py:213
  47.6 14.1 %collective-permute-start.3 = (bf16[512,512]{1,0:T(8,128)(2,1)S(1)}, bf16[512,512]{1,0:T(8,128)(2,1)S(1)}, u32[]{:S(2)}, u32[]{:S(2)}) collective-permute-start(bf16[512,512]{1,0:T(8,128)(2,1)S(1)} %collective-permute-done.2.refs_1_), channel_id=1, source_target_pairs={{0,2},{1,5},{2,0},{3,7},{4,6},{5,1},{6,4},{7,3},{8,10},{9,13},{10,... | collective-permute-start | bytes 1572872 | tf_op jit(solution)/shard_map/ppermute | solution.py:213
  49.1 18.6 %copy-start.5 = (f32[256,512]{1,0:T(8,128)S(1)}, f32[256,512]{1,0:T(8,128)}, u32[]{:S(2)}) copy-start(f32[256,512]{1,0:T(8,128)} %param.8) | copy-start | bytes 1572868
  49.1 10.5 %collective-permute-start.12 = (bf16[256,512]{1,0:T(8,128)(2,1)S(1)}, bf16[256,512]{1,0:T(8,128)(2,1)S(1)}, u32[]{:S(2)}, u32[]{:S(2)}) collective-permute-start(bf16[256,512]{1,0:T(8,128)(2,1)S(1)} %add_convert_fusion.2), channel_id=1, source_target_pairs={{0,2},{1,5},{2,0},{3,7},{4,6},{5,1},{6,4},{7,3},{8,10},{9,13},{10,... | collective-permute-start | bytes 786440 | tf_op jit(solution)/shard_map/ppermute | solution.py:213
  50.0 13.8 %collective-permute-start.15 = (bf16[128,512]{1,0:T(8,128)(2,1)S(1)}, bf16[128,512]{1,0:T(8,128)(2,1)S(1)}, u32[]{:S(2)}, u32[]{:S(2)}) collective-permute-start(bf16[128,512]{1,0:T(8,128)(2,1)S(1)} %get-tuple-element.45), channel_id=1, source_target_pairs={{0,24},{1,25},{2,26},{3,27},{4,28},{5,29},{6,30},{7,31},{8,16},{9,... | collective-permute-start | bytes 393224 | tf_op jit(solution)/shard_map/ppermute | solution.py:213
  59.6 7.4 %collective-permute-start.16 = (bf16[128,512]{1,0:T(8,128)(2,1)S(1)}, bf16[128,512]{1,0:T(8,128)(2,1)S(1)}, u32[]{:S(2)}, u32[]{:S(2)}) collective-permute-start(bf16[128,512]{1,0:T(8,128)(2,1)S(1)} %get-tuple-element.46), channel_id=1, source_target_pairs={{0,16},{1,17},{2,18},{3,19},{4,20},{5,21},{6,22},{7,23},{8,24},{9,... | collective-permute-start | bytes 393224 | tf_op jit(solution)/shard_map/ppermute | solution.py:213
  61.8 5.9 %collective-permute-start.17 = (bf16[128,512]{1,0:T(8,128)(2,1)S(1)}, bf16[128,512]{1,0:T(8,128)(2,1)S(1)}, u32[]{:S(2)}, u32[]{:S(2)}) collective-permute-start(bf16[128,512]{1,0:T(8,128)(2,1)S(1)} %slice.57), channel_id=1, source_target_pairs={{0,8},{1,9},{2,10},{3,11},{4,12},{5,13},{6,14},{7,15},{8,0},{9,1},... | collective-permute-start | bytes 393224 | tf_op jit(solution)/shard_map/ppermute | solution.py:213
  63.7 6.6 %collective-permute-start.6 = (bf16[512,512]{1,0:T(8,128)(2,1)S(1)}, bf16[512,512]{1,0:T(8,128)(2,1)S(1)}, u32[]{:S(2)}, u32[]{:S(2)}) collective-permute-start(bf16[512,512]{1,0:T(8,128)(2,1)S(1)} %collective-permute-done.5.refs_0_), channel_id=1, source_target_pairs={{0,1},{1,0},{2,3},{3,2},{4,5},{5,4},{6,7},{7,6},{8,9},{9,8},{10,11... | collective-permute-start | bytes 1572872 | tf_op jit(solution)/shard_map/ppermute | solution.py:213
  67.0 7.0 %collective-permute-start.4 = (bf16[512,512]{1,0:T(8,128)(2,1)S(1)}, bf16[512,512]{1,0:T(8,128)(2,1)S(1)}, u32[]{:S(2)}, u32[]{:S(2)}) collective-permute-start(bf16[512,512]{1,0:T(8,128)(2,1)S(1)} %collective-permute-done.3.refs_0_), channel_id=1, source_target_pairs={{0,1},{1,0},{2,3},{3,2},{4,5},{5,4},{6,7},{7,6},{8,9},{9,8},{10,11... | collective-permute-start | bytes 1572872 | tf_op jit(solution)/shard_map/ppermute | solution.py:213
  67.8 6.2 %collective-permute-start.18 = (f32[128,512]{1,0:T(8,128)S(1)}, f32[128,512]{1,0:T(8,128)S(1)}, u32[]{:S(2)}, u32[]{:S(2)}) collective-permute-start(f32[128,512]{1,0:T(8,128)S(1)} %fusion.3.refs_4_), channel_id=1, source_target_pairs={{0,1},{1,0},{2,3},{3,2},{4,5},{5,4},{6,7},{7,6},{8,9},{9,8},{10,11... | collective-permute-start | bytes 786440 | tf_op jit(solution)/shard_map/ppermute | solution.py:213

commit v4 on v3

--- a/solution.py
+++ b/solution.py
@@ -76,10 +76,11 @@
     return (partner_of(z, dz, nz) * ny + (y ^ dy)) * nx + (x ^ dx)
 
 
-def stage_kernel(grid, lists, order_hbm, x_ref, *refs):
-    refs = list(refs)
-    cot_ref = refs.pop(0) if len(refs) == 5 + 2 * len(lists) else None
-    outs, (buf, order_ref, x_sems, sems) = refs[:-4], refs[-4:]
+def stage_kernel(grid, lists, direct, order_hbm, x_ref, *refs):
+    count = 2 * len(lists)
+    cot_ref, outs, refs = refs[0], refs[1 : 1 + count], refs[1 + count :]
+    laid = outs if direct else refs[:count]
+    buf, order_ref, x_sems, out_sems, sems = refs[-5:]
     chunks, step, _ = buf.shape
     half = lax.axis_index("dp") % 2
     loads = []
@@ -90,12 +91,13 @@
         loads[-1].start()
     fetch = pltpu.make_async_copy(order_hbm, order_ref, sems.at[0])
     fetch.start()
-    stores = []
-    if cot_ref is not None:
-        for k, to_ref in enumerate(outs[:2]):
-            to = to_ref.at[:, len(lists[0]) * LANES :]
-            stores.append(pltpu.make_async_copy(cot_ref, to, sems.at[1 + k]))
-            stores[-1].start()
+    cots = []
+    for i, to_ref in enumerate(laid):
+        wide = LANES * len(lists[i // 2])
+        if to_ref.shape[1] > wide:
+            to = to_ref.at[:, wide:]
+            cots.append(pltpu.make_async_copy(cot_ref, to, sems.at[1 + len(cots)]))
+            cots[-1].start()
     fetch.wait()
     sides = (half, 1 - half)
     cols = [
@@ -103,13 +105,20 @@
         for spots in lists
         for side in sides
     ]
+    for copy in cots:
+        copy.wait()
+    stores = []
     for c in range(chunks):
         loads[c].wait()
         rows = slice(c * step, (c + 1) * step)
-        for i, to_ref in enumerate(outs):
+        for i, to_ref in enumerate(laid):
             for k, col in enumerate(cols[i]):
                 at = pl.ds(pl.multiple_of((2 * col + sides[i % 2]) * LANES, LANES), LANES)
                 to_ref[rows, k * LANES : (k + 1) * LANES] = buf[c, :, at]
+            if not direct:
+                sem = out_sems.at[c * count + i]
+                stores.append(pltpu.make_async_copy(to_ref.at[rows], outs[i].at[rows], sem))
+                stores[-1].start()
     for store in stores:
         store.wait()
 
@@ -237,29 +246,34 @@
     near_spots, far_spots = ([(k, da, db) for db in (0, 1) for k in line] for da in (0, 1))
     chunks = 4
 
-    def stage(lists, extra, limit):
+    def stage(lists, given, direct, limit):
         shapes = []
-        for spots in lists:
-            wide = part * len(spots) + (extra[0].shape[1] if extra and spots is lists[0] else 0)
-            shapes += [jax.ShapeDtypeStruct((rows, wide), bf16)] * 2
+        for i in range(2 * len(lists)):
+            wide = part * len(lists[i // 2]) + (key_width if i in given else 0)
+            shapes.append(jax.ShapeDtypeStruct((rows, wide), bf16))
         return pl.pallas_call(
-            functools.partial(stage_kernel, grid, lists),
-            in_specs=[hbm] * (2 + len(extra)),
-            out_specs=[vmem] * len(shapes),
+            functools.partial(stage_kernel, grid, lists, direct),
+            in_specs=[hbm] * 3,
+            out_specs=[vmem if direct else hbm] * len(shapes),
             out_shape=shapes,
-            scratch_shapes=[
+            scratch_shapes=[pltpu.VMEM(s.shape, bf16) for s in shapes if not direct]
+            + [
                 pltpu.VMEM((chunks, rows // chunks, width), bf16),
                 pltpu.SMEM(owner_order.shape, jnp.int32),
                 pltpu.SemaphoreType.DMA((chunks,)),
+                pltpu.SemaphoreType.DMA((chunks * len(shapes),)),
                 pltpu.SemaphoreType.DMA((3,)),
             ],
             compiler_params=pltpu.CompilerParams(vmem_limit_bytes=limit),
-        )(owner_order, flat, *extra)
+        )(owner_order, flat, cot)
 
     first_spots = [(k, 1, db) for ks in groups for db in (0, 1) for k in ks]
-    first_own, first_partner = stage([first_spots], [cot], TIGHT_BYTES)
+    first_own, first_partner = stage([first_spots], (1,), False, TIGHT_BYTES)
+    first_own = jnp.concatenate([first_own, cot], axis=1)
     first_got = to_core(first_partner)
-    near_own, near_partner, far_own, far_partner = stage([near_spots, far_spots], [cot], 8 << 20)
+    near_own, near_partner, far_own, far_partner = stage(
+        [near_spots, far_spots], (0, 1), True, 8 << 20
+    )
     near_got = to_core(near_partner)
 
     def wgrad(sources, order, lists, dtype):
@@ -293,10 +307,14 @@
         f32,
     )
 
-    held = lax.dynamic_slice_in_dim(kv_weight, half * part, part, axis=0)
-    for d in doubling:
-        held = jnp.concatenate([held, over_z(held, d)], axis=0)
-    beside = over_first(held)
+    def gather_z(value):
+        for d in doubling:
+            value = jnp.concatenate([value, over_z(value, d)], axis=0)
+        return value
+
+    own = lax.dynamic_slice_in_dim(kv_weight, half * part, part, axis=0)
+    held = gather_z(own)
+    beside = gather_z(over_first(own))
     across = over_second(held)
     corner = over_second(beside)
 
@@ -361,12 +379,19 @@
     done = apply(
         [
             (held, spots[0, 0], False, 0, 0),
-            (beside, spots[1, 0], False, 1, 0),
-            (to_core(held), spots[0, 0], True, 2, 0),
-            (to_core(beside), spots[1, 0], True, 3, 0),
+            (to_core(held), spots[0, 0], True, 1, 0),
         ],
-        [near_own, far_own, near_partner, far_partner],
+        [near_own, near_partner],
         (),
+        (),
+    )
+    done = apply(
+        [
+            (beside, spots[1, 0], False, 0, 0),
+            (to_core(beside), spots[1, 0], True, 1, 0),
+        ],
+        [far_own, far_partner],
+        done,
         (),
     )
     done = apply(

time: 76.2 us -> 73.4 us (0.963)
  waiting for transfers between devices: 38.5 us -> 29.8 us
  starting transfers between devices: 20.6 us -> 25.1 us
  Pallas kernels: 13.9 us -> 15.1 us
    ppermute x19 -> x21, waiting for transfers between devices: 38.5 us -> 29.8 us  [send(): return lax.ppermute(value, ('fsdp', 'dp'), pairs)]
    ppermute x19 -> x21, starting transfers between devices: 20.6 us -> 25.1 us  [send(): return lax.ppermute(value, ('fsdp', 'dp'), pairs)]
    pallas_call x4 -> x5, Pallas kernels: 8.12 us -> 9.34 us  [apply(): pl.pallas_call(functools.partial(apply_kernel, grid, [p[1:] for p in piec...]
    unnamed x12 -> x14, local copies, waits for them, and re-layouts: 1.62 us -> 1.64 us
  transfers between devices with their start and end apart: 19 -> 21, of which waited for: 7 -> 7; matrix products, arithmetic and copies ran while one was open for 1% -> 1% of each run, Pallas kernels for 12% -> 14%
where the time goes in v4:
time: 73.4 us; the launch traced here: 73.2 us
  waiting for transfers between devices  29.8 us (41%)
  starting transfers between devices  25.1 us (34%)
  Pallas kernels  15.1 us (21%)
  local copies, waits for them, and re-layouts  1.7 us (2%)
  between operations  0.91 us (1%)
    ppermute x21, waiting for transfers between devices, send(): return lax.ppermute(value, ('fsdp', 'dp'), pairs)  29.8 us
    ppermute x21, starting transfers between devices, send(): return lax.ppermute(value, ('fsdp', 'dp'), pairs)  25.1 us
    pallas_call x5, Pallas kernels, apply(): pl.pallas_call(functools.partial(apply_kernel, grid, [p[1:] for p in piec...  9.34 us
    pallas_call x2, Pallas kernels, stage(): pl.pallas_call(functools.partial(stage_kernel, grid, lists, direct), in_s...  4.34 us
    unnamed x14, local copies, waits for them, and re-layouts  1.64 us
  transfers between devices with their start and end apart: 21, of which 7 were waited for; matrix products, arithmetic and copies ran while one was open for 1% of the time, Pallas kernels for 14%

profile of v4, /device:TPU:0, one launch (start us, length us, event | category | flops | bytes accessed | tf_op | source)
XLA Modules:
  0.0 73.2 jit_solution(2125588182674603058)
XLA Ops:
  0.6 0.0 copy-start
  0.6 0.0 copy-start.1
  0.7 0.0 copy-start.3
  0.7 2.8 %shard_map.82 = (bf16[256,1024]{1,0:T(8,128)(2,1)}, bf16[256,1536]{1,0:T(8,128)(2,1)}) custom-call(s32[16]{0:T(128)} %order_ref.9, bf16[256,4096]{1,0:T(8,128)(2,1)} %bitcast.12, bf16[256,512]{1,0:T(8,128)(2,1)} %bitcast.4), custom_call_target="tpu_custom_call" | custom-call | tf_op jit(solution)/shard_map/pallas_call | solution.py:254
  3.5 0.6 collective-permute-start.12
  4.1 0.0 copy-done
  4.1 3.7 %collective-permute-start.5 = (bf16[128,512]{1,0:T(8,128)(2,1)S(1)}, bf16[128,512]{1,0:T(8,128)(2,1)S(1)}, u32[]{:S(2)}, u32[]{:S(2)}) collective-permute-start(bf16[128,512]{1,0:T(8,128)(2,1)S(1)} %constant_dynamic-slice_fusion), channel_id=1, source_target_pairs={{0,16},{1,17},{2,18},{3,19},{4,20},{5,21},{6,22},{7,23},{8,24},{9,... | collective-permute-start | bytes 393224 | tf_op jit(solution)/shard_map/ppermute | solution.py:222
  7.8 1.5 %collective-permute-start = (bf16[128,512]{1,0:T(8,128)(2,1)S(1)}, bf16[128,512]{1,0:T(8,128)(2,1)S(1)}, u32[]{:S(2)}, u32[]{:S(2)}) collective-permute-start(bf16[128,512]{1,0:T(8,128)(2,1)S(1)} %constant_dynamic-slice_fusion), channel_id=1, source_target_pairs={{0,4},{1,3},{2,6},{3,1},{4,0},{5,7},{6,2},{7,5},{8,12},{9,11},{10,... | collective-permute-start | bytes 393224 | tf_op jit(solution)/shard_map/ppermute | solution.py:222
  9.3 0.0 copy-done.1
  9.3 1.6 %copy-done.2 = bf16[2,128,4096]{2,1,0:T(8,128)(2,1)S(1)} copy-done((bf16[2,128,4096]{2,1,0:T(8,128)(2,1)S(1)}, bf16[2,128,4096]{2,1,0:T(8,128)(2,1)}, u32[]{:S(2)}) %copy-start.2) | copy-done | bytes 2097176
  10.9 1.5 %shard_map.76 = (bf16[256,1536]{1,0:T(8,128)(2,1)S(1)}, bf16[256,1536]{1,0:T(8,128)(2,1)S(1)}, bf16[256,1024]{1,0:T(8,128)(2,1)S(1)}, bf16[256,1024]{1,0:T(8,128)(2,1)S(1)}) custom-call(s32[16]{0:T(128)S(1)} %copy-done.3, bf16[256,4096]{1,0:T(8,128)(2,1)S(1)} %bitcast.13, bf16[256,512]{1,0:T(8,128)(2,1)S(1)} %bitcast.5), custom_call_target="tpu_custom_call" | custom-call | tf_op jit(solution)/shard_map/pallas_call | solution.py:254
  12.4 0.1 collective-permute-start.11
  12.5 0.1 pad_maximum_fusion.refs_0_
  12.5 2.2 %collective-permute-done.5 = bf16[128,512]{1,0:T(8,128)(2,1)S(1)} collective-permute-done((bf16[128,512]{1,0:T(8,128)(2,1)S(1)}, bf16[128,512]{1,0:T(8,128)(2,1)S(1)}, u32[]{:S(2)}, u32[]{:S(2)}) %collective-permute-start.5) | collective-permute-done | bytes 131104 | tf_op jit(solution)/shard_map/ppermute | solution.py:222
  14.7 0.8 %collective-permute-start.6 = (bf16[256,512]{1,0:T(8,128)(2,1)S(1)}, bf16[256,512]{1,0:T(8,128)(2,1)S(1)}, u32[]{:S(2)}, u32[]{:S(2)}) collective-permute-start(bf16[256,512]{1,0:T(8,128)(2,1)S(1)} %pad_maximum_fusion.3), channel_id=1, source_target_pairs={{0,8},{1,9},{2,10},{3,11},{4,12},{5,13},{6,14},{7,15},{8,0},{9,1},... | collective-permute-start | bytes 786440 | tf_op jit(solution)/shard_map/ppermute | solution.py:222
  15.5 0.0 collective-permute-done
  15.5 3.4 %collective-permute-start.1 = (bf16[128,512]{1,0:T(8,128)(2,1)S(1)}, bf16[128,512]{1,0:T(8,128)(2,1)S(1)}, u32[]{:S(2)}, u32[]{:S(2)}) collective-permute-start(bf16[128,512]{1,0:T(8,128)(2,1)S(1)} %collective-permute-done), channel_id=1, source_target_pairs={{0,16},{1,17},{2,18},{3,19},{4,20},{5,21},{6,22},{7,23},{8,24},{9,... | collective-permute-start | bytes 393224 | tf_op jit(solution)/shard_map/ppermute | solution.py:222
  18.9 0.0 collective-permute-done.12.refs_1_
  18.9 0.7 %shard_map.83 = (bf16[512,512]{1,0:T(8,128)(2,1)S(1)}, bf16[512,512]{1,0:T(8,128)(2,1)S(1)}) custom-call(bf16[256,1536]{1,0:T(8,128)(2,1)S(1)} %pad_maximum_fusion.refs_0_, bf16[256,1536]{1,0:T(8,128)(2,1)S(1)} %collective-permute-done.12.refs_1_), custom_call_target="tpu_custom_call" | custom-call | flops 536870912 | bytes 4194304 | tf_op jit(solution)/shard_map/pallas_call | solution.py:282
  19.6 1.6 %collective-permute-start.15 = (bf16[512,512]{1,0:T(8,128)(2,1)S(1)}, bf16[512,512]{1,0:T(8,128)(2,1)S(1)}, u32[]{:S(2)}, u32[]{:S(2)}) collective-permute-start(bf16[512,512]{1,0:T(8,128)(2,1)S(1)} %get-tuple-element.44), channel_id=1, source_target_pairs={{0,4},{1,3},{2,6},{3,1},{4,0},{5,7},{6,2},{7,5},{8,12},{9,11},{10,... | collective-permute-start | bytes 1572872 | tf_op jit(solution)/shard_map/ppermute | solution.py:222
  21.2 2.9 %collective-permute-done.1 = bf16[128,512]{1,0:T(8,128)(2,1)S(1)} collective-permute-done((bf16[128,512]{1,0:T(8,128)(2,1)S(1)}, bf16[128,512]{1,0:T(8,128)(2,1)S(1)}, u32[]{:S(2)}, u32[]{:S(2)}) %collective-permute-start.1) | collective-permute-done | bytes 131104 | tf_op jit(solution)/shard_map/ppermute | solution.py:222
  24.1 4.2 %collective-permute-start.2 = (bf16[256,512]{1,0:T(8,128)(2,1)S(1)}, bf16[256,512]{1,0:T(8,128)(2,1)S(1)}, u32[]{:S(2)}, u32[]{:S(2)}) collective-permute-start(bf16[256,512]{1,0:T(8,128)(2,1)S(1)} %pad_maximum_fusion.2), channel_id=1, source_target_pairs={{0,8},{1,9},{2,10},{3,11},{4,12},{5,13},{6,14},{7,15},{8,0},{9,1},... | collective-permute-start | bytes 786440 | tf_op jit(solution)/shard_map/ppermute | solution.py:222
  28.3 1.6 %collective-permute-start.13 = (bf16[512,512]{1,0:T(8,128)(2,1)S(1)}, bf16[512,512]{1,0:T(8,128)(2,1)S(1)}, u32[]{:S(2)}, u32[]{:S(2)}) collective-permute-start(bf16[512,512]{1,0:T(8,128)(2,1)S(1)} %get-tuple-element.41), channel_id=1, source_target_pairs={{0,4},{1,3},{2,6},{3,1},{4,0},{5,7},{6,2},{7,5},{8,12},{9,11},{10,... | collective-permute-start | bytes 1572872 | tf_op jit(solution)/shard_map/ppermute | solution.py:222
  29.9 0.0 collective-permute-done.6
  30.0 0.1 collective-permute-start.10
  30.1 0.0 collective-permute-done.11.refs_1_
  30.1 1.6 %collective-permute-start.7 = (bf16[512,512]{1,0:T(8,128)(2,1)S(1)}, bf16[512,512]{1,0:T(8,128)(2,1)S(1)}, u32[]{:S(2)}, u32[]{:S(2)}) collective-permute-start(bf16[512,512]{1,0:T(8,128)(2,1)S(1)} %pad_maximum_fusion.1.refs_0_), channel_id=1, source_target_pairs={{0,2},{1,5},{2,0},{3,7},{4,6},{5,1},{6,4},{7,3},{8,10},{9,13},{10,... | collective-permute-start | bytes 1572872 | tf_op jit(solution)/shard_map/ppermute | solution.py:222
  31.6 0.7 shard_map.81
  32.4 0.0 collective-permute-done.15
  32.4 0.1 add_convert_fusion.1
  32.4 0.6 collective-permute-start.16
  33.1 1.2 %collective-permute-done.2 = bf16[256,512]{1,0:T(8,128)(2,1)S(1)} collective-permute-done((bf16[256,512]{1,0:T(8,128)(2,1)S(1)}, bf16[256,512]{1,0:T(8,128)(2,1)S(1)}, u32[]{:S(2)}, u32[]{:S(2)}) %collective-permute-start.2) | collective-permute-done | bytes 262176 | tf_op jit(solution)/shard_map/ppermute | solution.py:222
  34.3 0.1 collective-permute-start.9
  34.4 7.7 %collective-permute-done.13 = bf16[512,512]{1,0:T(8,128)(2,1)S(1)} collective-permute-done((bf16[512,512]{1,0:T(8,128)(2,1)S(1)}, bf16[512,512]{1,0:T(8,128)(2,1)S(1)}, u32[]{:S(2)}, u32[]{:S(2)}) %collective-permute-start.13) | collective-permute-done | bytes 524320 | tf_op jit(solution)/shard_map/ppermute | solution.py:222
  42.1 1.5 %collective-permute-start.3 = (bf16[512,512]{1,0:T(8,128)(2,1)S(1)}, bf16[512,512]{1,0:T(8,128)(2,1)S(1)}, u32[]{:S(2)}, u32[]{:S(2)}) collective-permute-start(bf16[512,512]{1,0:T(8,128)(2,1)S(1)} %constant_dynamic-update-slice_fusion.refs_0_), channel_id=1, source_target_pairs={{0,2},{1,5},{2,0},{3,7},{4,6},{5,1},{6,4},{7,3},{8,10},{9,13},{10,... | collective-permute-start | bytes 1572872 | tf_op jit(solution)/shard_map/ppermute | solution.py:222
  43.6 0.1 add_convert_fusion.2
  43.7 0.0 copy-start.5
  43.7 0.6 collective-permute-done.16
  44.3 1.5 %collective-permute-start.14 = (bf16[256,512]{1,0:T(8,128)(2,1)S(1)}, bf16[256,512]{1,0:T(8,128)(2,1)S(1)}, u32[]{:S(2)}, u32[]{:S(2)}) collective-permute-start(bf16[256,512]{1,0:T(8,128)(2,1)S(1)} %add_convert_fusion.2), channel_id=1, source_target_pairs={{0,2},{1,5},{2,0},{3,7},{4,6},{5,1},{6,4},{7,3},{8,10},{9,13},{10,... | collective-permute-start | bytes 786440 | tf_op jit(solution)/shard_map/ppermute | solution.py:222
  45.8 0.1 add_convert_fusion
  45.9 0.0 collective-permute-done.7.refs_0_
  45.9 0.5 collective-permute-start.17
  46.4 7.7 %collective-permute-done.14 = bf16[256,512]{1,0:T(8,128)(2,1)S(1)} collective-permute-done((bf16[256,512]{1,0:T(8,128)(2,1)S(1)}, bf16[256,512]{1,0:T(8,128)(2,1)S(1)}, u32[]{:S(2)}, u32[]{:S(2)}) %collective-permute-start.14) | collective-permute-done | bytes 262176 | tf_op jit(solution)/shard_map/ppermute | solution.py:222
  54.1 0.0 collective-permute-start.18
  54.1 0.1 convert_add_fusion
  54.2 0.0 collective-permute-done.3.refs_0_
  54.2 1.3 %collective-permute-start.19 = (bf16[128,512]{1,0:T(8,128)(2,1)S(1)}, bf16[128,512]{1,0:T(8,128)(2,1)S(1)}, u32[]{:S(2)}, u32[]{:S(2)}) collective-permute-start(bf16[128,512]{1,0:T(8,128)(2,1)S(1)} %slice.57), channel_id=1, source_target_pairs={{0,8},{1,9},{2,10},{3,11},{4,12},{5,13},{6,14},{7,15},{8,0},{9,1},... | collective-permute-start | bytes 393224 | tf_op jit(solution)/shard_map/ppermute | solution.py:222
  55.6 0.0 collective-permute-done.17
  55.6 0.0 collective-permute-start.8
  55.6 7.5 %collective-permute-done.18 = bf16[128,512]{1,0:T(8,128)(2,1)S(1)} collective-permute-done((bf16[128,512]{1,0:T(8,128)(2,1)S(1)}, bf16[128,512]{1,0:T(8,128)(2,1)S(1)}, u32[]{:S(2)}, u32[]{:S(2)}) %collective-permute-start.18) | collective-permute-done | bytes 131104 | tf_op jit(solution)/shard_map/ppermute | solution.py:222
  63.1 0.0 collective-permute-start.4
  63.2 0.0 collective-permute-done.19
  63.2 0.1 fusion.3.refs_4_
  63.3 0.5 collective-permute-start.20
  63.8 0.0 collective-permute-done.10.refs_1_
  63.8 1.8 %shard_map.77 = (f32[256,512]{1,0:T(8,128)S(1)}, bf16[256,4096]{1,0:T(8,128)(2,1)}) custom-call(s32[16]{0:T(128)S(1)} %copy-done.3, bf16[256,512]{1,0:T(8,128)(2,1)S(1)} %bitcast.7, bf16[512,512]{1,0:T(8,128)(2,1)S(1)} %pad_maximum_fusion.1.refs_0_, bf16[512,512]{1,0:T(8,128)(2,1)S(1)} %collective-permute-done.10.refs_1_, ...), custom_call_target="tpu_custom_call" | custom-call | flops 536870912 | bytes 2097152 | tf_op jit(solution)/shard_map/pallas_call | solution.py:355
  65.6 0.0 collective-permute-done.9.refs_1_
  65.6 1.9 %shard_map.78 = (f32[256,512]{1,0:T(8,128)S(1)}, bf16[256,4096]{1,0:T(8,128)(2,1)}) custom-call(s32[16]{0:T(128)S(1)} %copy-done.3, bf16[256,512]{1,0:T(8,128)(2,1)S(1)} %bitcast.8, bf16[512,512]{1,0:T(8,128)(2,1)S(1)} %constant_dynamic-update-slice_fusion.refs_0_, ...), custom_call_target="tpu_custom_call", output_to_operand_aliasing={{1}: (7, {})} | custom-call | flops 536870912 | bytes 2097152 | tf_op jit(solution)/shard_map/pallas_call | solution.py:355
  67.6 0.0 collective-permute-done.8.refs_1_
  67.6 1.9 %shard_map.79 = (f32[256,512]{1,0:T(8,128)S(1)}, bf16[256,4096]{1,0:T(8,128)(2,1)}) custom-call(s32[16]{0:T(128)S(1)} %copy-done.3, bf16[256,512]{1,0:T(8,128)(2,1)S(1)} %bitcast.9, bf16[512,512]{1,0:T(8,128)(2,1)S(1)} %collective-permute-done.7.refs_0_, bf16[512,512]{1,0:T(8,128)(2,1)S(1)} %collective-permute-done.8.refs_1_, ...), custom_call_target="tpu_custom_call", output_to_operand_aliasing={{1}: (7, {})} | custom-call | flops 536870912 | bytes 2097152 | tf_op jit(solution)/shard_map/pallas_call | solution.py:355
  69.5 1.7 %shard_map.80 = (f32[256,512]{1,0:T(8,128)S(1)}, bf16[256,4096]{1,0:T(8,128)(2,1)}) custom-call(s32[16]{0:T(128)S(1)} %copy-done.3, bf16[256,512]{1,0:T(8,128)(2,1)S(1)} %bitcast.10, bf16[512,512]{1,0:T(8,128)(2,1)S(1)} %collective-permute-done.3.refs_0_, bf16[256,1024]{1,0:T(8,128)(2,1)S(1)} %get-tuple-element.27.refs_2_.refs_1_, ...), custom_call_target="tpu_custom_call", output_to_operand_aliasing={{1}: (5, {})} | custom-call | flops 268435456 | bytes 2097152 | tf_op jit(solution)/shard_map/pallas_call | solution.py:355
  71.2 0.0 collective-permute-done.4.refs_0_
  71.2 0.0 collective-permute-done.20.refs_5_
  71.2 2.0 %shard_map.84 = (bf16[256,512]{1,0:T(8,128)(2,1)}, bf16[256,4096]{1,0:T(8,128)(2,1)}, f32[256,512]{1,0:T(8,128)}) custom-call(s32[16]{0:T(128)S(1)} %copy-done.3, bf16[256,512]{1,0:T(8,128)(2,1)S(1)} %bitcast.11, bf16[512,512]{1,0:T(8,128)(2,1)S(1)} %collective-permute-done.4.refs_0_, ...), custom_call_target="tpu_custom_call", output_to_operand_aliasing={{1}: (5, {})} | custom-call | flops 268435456 | bytes 2097152 | tf_op jit(solution)/shard_map/pallas_call | solution.py:355
  (14 shorter events, 0.2 us)
Async XLA Ops:
  0.6 3.4 %copy-start = (bf16[256,512]{1,0:T(8,128)(2,1)S(1)}, bf16[256,512]{1,0:T(8,128)(2,1)}, u32[]{:S(2)}) copy-start(bf16[256,512]{1,0:T(8,128)(2,1)} %param.7) | copy-start | bytes 786436
  0.6 8.7 %copy-start.1 = (bf16[2,128,512]{2,1,0:T(8,128)(2,1)S(1)}, bf16[2,128,512]{2,1,0:T(8,128)(2,1)}, u32[]{:S(2)}) copy-start(bf16[2,128,512]{2,1,0:T(8,128)(2,1)} %param.6) | copy-start | bytes 786436
  0.7 8.6 %copy-start.3 = (s32[16]{0:T(128)S(1)}, s32[16]{0:T(128)}, u32[]{:S(2)}) copy-start(s32[16]{0:T(128)} %order_ref.9) | copy-start | bytes 196
  3.5 15.4 %collective-permute-start.12 = (bf16[256,1536]{1,0:T(8,128)(2,1)}, bf16[256,1536]{1,0:T(8,128)(2,1)S(1)}, u32[]{:S(2)}, u32[]{:S(2)}) collective-permute-start(bf16[256,1536]{1,0:T(8,128)(2,1)} %get-tuple-element.40), channel_id=1, source_target_pairs={{0,1},{1,0},{2,3},{3,2},{4,5},{5,4},{6,7},{7,6},{8,9},{9,8},{10,11... | collective-permute-start | bytes 2359304 | tf_op jit(solution)/shard_map/ppermute | solution.py:222
  4.1 10.6 %collective-permute-start.5 = (bf16[128,512]{1,0:T(8,128)(2,1)S(1)}, bf16[128,512]{1,0:T(8,128)(2,1)S(1)}, u32[]{:S(2)}, u32[]{:S(2)}) collective-permute-start(bf16[128,512]{1,0:T(8,128)(2,1)S(1)} %constant_dynamic-slice_fusion), channel_id=1, source_target_pairs={{0,16},{1,17},{2,18},{3,19},{4,20},{5,21},{6,22},{7,23},{8,24},{9,... | collective-permute-start | bytes 393224 | tf_op jit(solution)/shard_map/ppermute | solution.py:222
  7.8 7.8 %collective-permute-start = (bf16[128,512]{1,0:T(8,128)(2,1)S(1)}, bf16[128,512]{1,0:T(8,128)(2,1)S(1)}, u32[]{:S(2)}, u32[]{:S(2)}) collective-permute-start(bf16[128,512]{1,0:T(8,128)(2,1)S(1)} %constant_dynamic-slice_fusion), channel_id=1, source_target_pairs={{0,4},{1,3},{2,6},{3,1},{4,0},{5,7},{6,2},{7,5},{8,12},{9,11},{10,... | collective-permute-start | bytes 393224 | tf_op jit(solution)/shard_map/ppermute | solution.py:222
  9.3 1.6 %copy-start.2 = (bf16[2,128,4096]{2,1,0:T(8,128)(2,1)S(1)}, bf16[2,128,4096]{2,1,0:T(8,128)(2,1)}, u32[]{:S(2)}) copy-start(bf16[2,128,4096]{2,1,0:T(8,128)(2,1)} %param.5) | copy-start | bytes 6291460
  10.9 1.6 %copy-start.4 = (bf16[256,1024]{1,0:T(8,128)(2,1)S(1)}, bf16[256,1024]{1,0:T(8,128)(2,1)}, u32[]{:S(2)}) copy-start(bf16[256,1024]{1,0:T(8,128)(2,1)} %get-tuple-element.39) | copy-start | bytes 1572868
  12.4 17.7 %collective-permute-start.11 = (bf16[256,1536]{1,0:T(8,128)(2,1)S(1)}, bf16[256,1536]{1,0:T(8,128)(2,1)S(1)}, u32[]{:S(2)}, u32[]{:S(2)}) collective-permute-start(bf16[256,1536]{1,0:T(8,128)(2,1)S(1)} %get-tuple-element.29.refs_3_), channel_id=1, source_target_pairs={{0,1},{1,0},{2,3},{3,2},{4,5},{5,4},{6,7},{7,6},{8,9},{9,8},{10,11... | collective-permute-start | bytes 2359304 | tf_op jit(solution)/shard_map/ppermute | solution.py:222
  14.7 15.2 %collective-permute-start.6 = (bf16[256,512]{1,0:T(8,128)(2,1)S(1)}, bf16[256,512]{1,0:T(8,128)(2,1)S(1)}, u32[]{:S(2)}, u32[]{:S(2)}) collective-permute-start(bf16[256,512]{1,0:T(8,128)(2,1)S(1)} %pad_maximum_fusion.3), channel_id=1, source_target_pairs={{0,8},{1,9},{2,10},{3,11},{4,12},{5,13},{6,14},{7,15},{8,0},{9,1},... | collective-permute-start | bytes 786440 | tf_op jit(solution)/shard_map/ppermute | solution.py:222
  15.5 8.6 %collective-permute-start.1 = (bf16[128,512]{1,0:T(8,128)(2,1)S(1)}, bf16[128,512]{1,0:T(8,128)(2,1)S(1)}, u32[]{:S(2)}, u32[]{:S(2)}) collective-permute-start(bf16[128,512]{1,0:T(8,128)(2,1)S(1)} %collective-permute-done), channel_id=1, source_target_pairs={{0,16},{1,17},{2,18},{3,19},{4,20},{5,21},{6,22},{7,23},{8,24},{9,... | collective-permute-start | bytes 393224 | tf_op jit(solution)/shard_map/ppermute | solution.py:222
  19.6 12.7 %collective-permute-start.15 = (bf16[512,512]{1,0:T(8,128)(2,1)S(1)}, bf16[512,512]{1,0:T(8,128)(2,1)S(1)}, u32[]{:S(2)}, u32[]{:S(2)}) collective-permute-start(bf16[512,512]{1,0:T(8,128)(2,1)S(1)} %get-tuple-element.44), channel_id=1, source_target_pairs={{0,4},{1,3},{2,6},{3,1},{4,0},{5,7},{6,2},{7,5},{8,12},{9,11},{10,... | collective-permute-start | bytes 1572872 | tf_op jit(solution)/shard_map/ppermute | solution.py:222
  24.1 10.1 %collective-permute-start.2 = (bf16[256,512]{1,0:T(8,128)(2,1)S(1)}, bf16[256,512]{1,0:T(8,128)(2,1)S(1)}, u32[]{:S(2)}, u32[]{:S(2)}) collective-permute-start(bf16[256,512]{1,0:T(8,128)(2,1)S(1)} %pad_maximum_fusion.2), channel_id=1, source_target_pairs={{0,8},{1,9},{2,10},{3,11},{4,12},{5,13},{6,14},{7,15},{8,0},{9,1},... | collective-permute-start | bytes 786440 | tf_op jit(solution)/shard_map/ppermute | solution.py:222
  28.3 13.7 %collective-permute-start.13 = (bf16[512,512]{1,0:T(8,128)(2,1)S(1)}, bf16[512,512]{1,0:T(8,128)(2,1)S(1)}, u32[]{:S(2)}, u32[]{:S(2)}) collective-permute-start(bf16[512,512]{1,0:T(8,128)(2,1)S(1)} %get-tuple-element.41), channel_id=1, source_target_pairs={{0,4},{1,3},{2,6},{3,1},{4,0},{5,7},{6,2},{7,5},{8,12},{9,11},{10,... | collective-permute-start | bytes 1572872 | tf_op jit(solution)/shard_map/ppermute | solution.py:222
  30.0 33.8 %collective-permute-start.10 = (bf16[512,512]{1,0:T(8,128)(2,1)S(1)}, bf16[512,512]{1,0:T(8,128)(2,1)S(1)}, u32[]{:S(2)}, u32[]{:S(2)}) collective-permute-start(bf16[512,512]{1,0:T(8,128)(2,1)S(1)} %pad_maximum_fusion.1.refs_0_), channel_id=1, source_target_pairs={{0,1},{1,0},{2,3},{3,2},{4,5},{5,4},{6,7},{7,6},{8,9},{9,8},{10,11... | collective-permute-start | bytes 1572872 | tf_op jit(solution)/shard_map/ppermute | solution.py:222
  30.1 15.8 %collective-permute-start.7 = (bf16[512,512]{1,0:T(8,128)(2,1)S(1)}, bf16[512,512]{1,0:T(8,128)(2,1)S(1)}, u32[]{:S(2)}, u32[]{:S(2)}) collective-permute-start(bf16[512,512]{1,0:T(8,128)(2,1)S(1)} %pad_maximum_fusion.1.refs_0_), channel_id=1, source_target_pairs={{0,2},{1,5},{2,0},{3,7},{4,6},{5,1},{6,4},{7,3},{8,10},{9,13},{10,... | collective-permute-start | bytes 1572872 | tf_op jit(solution)/shard_map/ppermute | solution.py:222
  32.4 11.8 %collective-permute-start.16 = (bf16[256,512]{1,0:T(8,128)(2,1)S(1)}, bf16[256,512]{1,0:T(8,128)(2,1)S(1)}, u32[]{:S(2)}, u32[]{:S(2)}) collective-permute-start(bf16[256,512]{1,0:T(8,128)(2,1)S(1)} %add_convert_fusion.1), channel_id=1, source_target_pairs={{0,2},{1,5},{2,0},{3,7},{4,6},{5,1},{6,4},{7,3},{8,10},{9,13},{10,... | collective-permute-start | bytes 786440 | tf_op jit(solution)/shard_map/ppermute | solution.py:222
  34.3 31.3 %collective-permute-start.9 = (bf16[512,512]{1,0:T(8,128)(2,1)S(1)}, bf16[512,512]{1,0:T(8,128)(2,1)S(1)}, u32[]{:S(2)}, u32[]{:S(2)}) collective-permute-start(bf16[512,512]{1,0:T(8,128)(2,1)S(1)} %constant_dynamic-update-slice_fusion.refs_0_), channel_id=1, source_target_pairs={{0,1},{1,0},{2,3},{3,2},{4,5},{5,4},{6,7},{7,6},{8,9},{9,8},{10,11... | collective-permute-start | bytes 1572872 | tf_op jit(solution)/shard_map/ppermute | solution.py:222
  42.1 12.1 %collective-permute-start.3 = (bf16[512,512]{1,0:T(8,128)(2,1)S(1)}, bf16[512,512]{1,0:T(8,128)(2,1)S(1)}, u32[]{:S(2)}, u32[]{:S(2)}) collective-permute-start(bf16[512,512]{1,0:T(8,128)(2,1)S(1)} %constant_dynamic-update-slice_fusion.refs_0_), channel_id=1, source_target_pairs={{0,2},{1,5},{2,0},{3,7},{4,6},{5,1},{6,4},{7,3},{8,10},{9,13},{10,... | collective-permute-start | bytes 1572872 | tf_op jit(solution)/shard_map/ppermute | solution.py:222
  43.7 19.5 %copy-start.5 = (f32[256,512]{1,0:T(8,128)S(1)}, f32[256,512]{1,0:T(8,128)}, u32[]{:S(2)}) copy-start(f32[256,512]{1,0:T(8,128)} %param.8) | copy-start | bytes 1572868
  44.3 9.8 %collective-permute-start.14 = (bf16[256,512]{1,0:T(8,128)(2,1)S(1)}, bf16[256,512]{1,0:T(8,128)(2,1)S(1)}, u32[]{:S(2)}, u32[]{:S(2)}) collective-permute-start(bf16[256,512]{1,0:T(8,128)(2,1)S(1)} %add_convert_fusion.2), channel_id=1, source_target_pairs={{0,2},{1,5},{2,0},{3,7},{4,6},{5,1},{6,4},{7,3},{8,10},{9,13},{10,... | collective-permute-start | bytes 786440 | tf_op jit(solution)/shard_map/ppermute | solution.py:222
  45.9 9.7 %collective-permute-start.17 = (bf16[128,512]{1,0:T(8,128)(2,1)S(1)}, bf16[128,512]{1,0:T(8,128)(2,1)S(1)}, u32[]{:S(2)}, u32[]{:S(2)}) collective-permute-start(bf16[128,512]{1,0:T(8,128)(2,1)S(1)} %get-tuple-element.49), channel_id=1, source_target_pairs={{0,24},{1,25},{2,26},{3,27},{4,28},{5,29},{6,30},{7,31},{8,16},{9,... | collective-permute-start | bytes 393224 | tf_op jit(solution)/shard_map/ppermute | solution.py:222
  54.1 9.0 %collective-permute-start.18 = (bf16[128,512]{1,0:T(8,128)(2,1)S(1)}, bf16[128,512]{1,0:T(8,128)(2,1)S(1)}, u32[]{:S(2)}, u32[]{:S(2)}) collective-permute-start(bf16[128,512]{1,0:T(8,128)(2,1)S(1)} %get-tuple-element.50), channel_id=1, source_target_pairs={{0,16},{1,17},{2,18},{3,19},{4,20},{5,21},{6,22},{7,23},{8,24},{9,... | collective-permute-start | bytes 393224 | tf_op jit(solution)/shard_map/ppermute | solution.py:222
  54.2 8.9 %collective-permute-start.19 = (bf16[128,512]{1,0:T(8,128)(2,1)S(1)}, bf16[128,512]{1,0:T(8,128)(2,1)S(1)}, u32[]{:S(2)}, u32[]{:S(2)}) collective-permute-start(bf16[128,512]{1,0:T(8,128)(2,1)S(1)} %slice.57), channel_id=1, source_target_pairs={{0,8},{1,9},{2,10},{3,11},{4,12},{5,13},{6,14},{7,15},{8,0},{9,1},... | collective-permute-start | bytes 393224 | tf_op jit(solution)/shard_map/ppermute | solution.py:222
  55.6 12.0 %collective-permute-start.8 = (bf16[512,512]{1,0:T(8,128)(2,1)S(1)}, bf16[512,512]{1,0:T(8,128)(2,1)S(1)}, u32[]{:S(2)}, u32[]{:S(2)}) collective-permute-start(bf16[512,512]{1,0:T(8,128)(2,1)S(1)} %collective-permute-done.7.refs_0_), channel_id=1, source_target_pairs={{0,1},{1,0},{2,3},{3,2},{4,5},{5,4},{6,7},{7,6},{8,9},{9,8},{10,11... | collective-permute-start | bytes 1572872 | tf_op jit(solution)/shard_map/ppermute | solution.py:222
  63.1 8.1 %collective-permute-start.4 = (bf16[512,512]{1,0:T(8,128)(2,1)S(1)}, bf16[512,512]{1,0:T(8,128)(2,1)S(1)}, u32[]{:S(2)}, u32[]{:S(2)}) collective-permute-start(bf16[512,512]{1,0:T(8,128)(2,1)S(1)} %collective-permute-done.3.refs_0_), channel_id=1, source_target_pairs={{0,1},{1,0},{2,3},{3,2},{4,5},{5,4},{6,7},{7,6},{8,9},{9,8},{10,11... | collective-permute-start | bytes 1572872 | tf_op jit(solution)/shard_map/ppermute | solution.py:222
  63.3 7.9 %collective-permute-start.20 = (f32[128,512]{1,0:T(8,128)S(1)}, f32[128,512]{1,0:T(8,128)S(1)}, u32[]{:S(2)}, u32[]{:S(2)}) collective-permute-start(f32[128,512]{1,0:T(8,128)S(1)} %fusion.3.refs_4_), channel_id=1, source_target_pairs={{0,1},{1,0},{2,3},{3,2},{4,5},{5,4},{6,7},{7,6},{8,9},{9,8},{10,11... | collective-permute-start | bytes 786440 | tf_op jit(solution)/shard_map/ppermute | solution.py:222
